TPU v7x, 16 devices: a 4x2x1 block of a 4x4x8 slice. The times are simulated.
16 devices in a mesh: dp: 2 (over y, z), tp: 8 (over x, core).
Axes of the slice: x: 4, y: 2, z: 1, core: 2. Of those that a mesh axis runs over, the one named last changes fastest.
The devices are a block of a 4x4x8 slice.
Arguments:
- hidden: bfloat16 [128, 1, 2048], P('dp'), parts along dimension 0
- ln_gain: bfloat16 [2, 2, 2048], replicated
- ln_shift: bfloat16 [2, 2, 2048], replicated
- w_qkv: bfloat16 [2, 2048, 6144], P(None, None, 'tp')
- b_qkv: bfloat16 [2, 6144], P(None, 'tp')
- w_out: bfloat16 [2, 2048, 2048], P(None, 'tp')
- b_out: bfloat16 [2, 2048], replicated
- w_up: bfloat16 [2, 2048, 8192], P(None, None, 'tp')
- b_up: bfloat16 [2, 8192], P(None, 'tp')
- w_down: bfloat16 [2, 8192, 2048], P(None, 'tp')
- b_down: bfloat16 [2, 2048], replicated
- k_cache: bfloat16 [2, 128, 256, 16, 128], P(None, 'dp', None, 'tp'), parts along dimension 1
- v_cache: bfloat16 [2, 128, 256, 16, 128], P(None, 'dp', None, 'tp'), parts along dimension 1
- write_slot: int32 [128], P('dp'), parts along dimension 0
- key_pos: int32 [128, 256], P('dp'), parts along dimension 0
- key_valid: int32 [128, 256], P('dp'), parts along dimension 0
Outputs:
- output 1: bfloat16 [128, 1, 2048], P('dp'), parts along dimension 0
- output 2: bfloat16 [2, 128, 256, 16, 128], P(None, 'dp', None, 'tp'), parts along dimension 1
- output 3: bfloat16 [2, 128, 256, 16, 128], P(None, 'dp', None, 'tp'), parts along dimension 1
There are 2 independent parts. A program takes and returns all parts, laid end to end along the dimension named above; an argument that names none is the same for every part.
All inputs are finite; a program needn't handle non-finite values.
Results may differ from a plain program's by a relative error of at most 0.0132686.
Values are sent between devices in bfloat16 or wider.
A program may use at most 768 MiB of HBM per device.

v0:
```python
import math
import jax
import jax.numpy as jnp
from jax import lax
from jax.sharding import PartitionSpec as P

LN_EPS = 1e-5


def alibi_slopes(n_heads):
    return jnp.exp2(-8.0 * jnp.arange(1, n_heads + 1).astype(jnp.float32) / n_heads)


def layer_norm(x_rows, gain, shift):
    x_f32 = x_rows.astype(jnp.float32)
    mean_val = jnp.mean(x_f32, axis=-1, keepdims=True)
    centered = x_f32 - mean_val
    var_val = jnp.mean(centered * centered, axis=-1, keepdims=True)
    normed = centered * lax.rsqrt(var_val + LN_EPS)
    return (normed * gain.astype(jnp.float32) + shift.astype(jnp.float32)).astype(jnp.bfloat16)


def solution(mesh):
    tp_size = mesh.shape['tp']

    def device_step(hidden, ln_gain, ln_shift, w_qkv, b_qkv, w_out, b_out, w_up, b_up, w_down, b_down, k_cache, v_cache, write_slot, key_pos, key_valid):
        n_layers, n_batch, cache_len, n_local, head_dim = k_cache.shape
        all_slopes = alibi_slopes(n_local * tp_size)
        my_slopes = lax.dynamic_slice_in_dim(all_slopes, lax.axis_index('tp') * n_local, n_local)
        t_index = lax.broadcasted_iota(jnp.int32, (n_batch, cache_len), 1)
        is_new = t_index == write_slot[:, None]
        allowed = jnp.logical_or(key_valid > 0, is_new)
        pos_bias = jnp.where(allowed[:, None, :], my_slopes[None, :, None] * key_pos.astype(jnp.float32)[:, None, :], -jnp.inf)
        new_mask = is_new[:, :, None, None]
        score_scale = 1.0 / math.sqrt(head_dim)
        x_cur = hidden[:, 0, :]
        k_list = []
        v_list = []
        for layer_idx in range(n_layers):
            normed = layer_norm(x_cur, ln_gain[layer_idx, 0], ln_shift[layer_idx, 0])
            qkv_out = (jnp.dot(normed, w_qkv[layer_idx], preferred_element_type=jnp.float32) + b_qkv[layer_idx].astype(jnp.float32)).astype(jnp.bfloat16)
            qkv_out = qkv_out.reshape(n_batch, n_local, 3, head_dim)
            k_all = jnp.where(new_mask, qkv_out[:, None, :, 1, :], k_cache[layer_idx])
            v_all = jnp.where(new_mask, qkv_out[:, None, :, 2, :], v_cache[layer_idx])
            scores = jnp.einsum('bhd,bthd->bht', qkv_out[:, :, 0, :], k_all, preferred_element_type=jnp.float32) * score_scale + pos_bias
            attn_probs = jax.nn.softmax(scores, axis=-1).astype(jnp.bfloat16)
            attn_out = jnp.einsum('bht,bthd->bhd', attn_probs, v_all, preferred_element_type=jnp.float32).astype(jnp.bfloat16)
            proj_part = jnp.dot(attn_out.reshape(n_batch, n_local * head_dim), w_out[layer_idx], preferred_element_type=jnp.float32)
            proj_sum = lax.psum(proj_part, 'tp')
            x_mid = (x_cur.astype(jnp.float32) + proj_sum + b_out[layer_idx].astype(jnp.float32)).astype(jnp.bfloat16)
            normed_mlp = layer_norm(x_mid, ln_gain[layer_idx, 1], ln_shift[layer_idx, 1])
            up_act = jnp.dot(normed_mlp, w_up[layer_idx], preferred_element_type=jnp.float32) + b_up[layer_idx].astype(jnp.float32)
            gelu_out = jax.nn.gelu(up_act, approximate=True).astype(jnp.bfloat16)
            down_part = jnp.dot(gelu_out, w_down[layer_idx], preferred_element_type=jnp.float32)
            down_sum = lax.psum(down_part, 'tp')
            x_cur = (x_mid.astype(jnp.float32) + down_sum + b_down[layer_idx].astype(jnp.float32)).astype(jnp.bfloat16)
            k_list.append(k_all)
            v_list.append(v_all)
        return x_cur[:, None, :], jnp.stack(k_list), jnp.stack(v_list)

    cache_spec = P(None, 'dp', None, 'tp', None)
    in_specs = (P('dp', None, None), P(), P(), P(None, None, 'tp'), P(None, 'tp'), P(None, 'tp', None), P(), P(None, None, 'tp'), P(None, 'tp'), P(None, 'tp', None), P(), cache_spec, cache_spec, P('dp'), P('dp', None), P('dp', None))
    out_specs = (P('dp', None, None), cache_spec, cache_spec)
    return jax.shard_map(device_step, mesh=mesh, in_specs=in_specs, out_specs=out_specs, check_vma=False)
```

profile of v0, /device:TPU:113, one launch (start us, length us, event | category | flops | bytes accessed | tf_op | source)
XLA Modules:
  0.0 363.8 jit_solution(4188841024567318945)
XLA Ops:
  7.2 0.1 all-reduce.5.cloned.1.call-start
  7.3 1.1 convert_reduce_fusion.3
  8.4 1.2 fusion.85
  9.6 0.8 convert_reduce_fusion.4
  10.4 0.8 slice_convert_fusion.2
  11.2 0.8 slice_convert_fusion.1
  12.0 0.8 convert_element_type.183
  12.8 2.7 fusion.49
  15.6 0.1 fusion.212
  15.9 0.1 dynamic_slice.3
  15.9 0.9 compare_or_fusion
  16.9 25.6 %broadcast_select_fusion.7 = (bf16[64,256,2,128]{3,2,1,0:T(2,128)(2,1)S(1)}, bf16[64,256,2,128]{3,2,1,0:T(2,128)(2,1)}) fusion(pred[64,256]{1,0:T(8,128)(4,1)S(1)} %get-tuple-element.42, bf16[2,64,256,2,128]{4,3,2,1,0:T(2,128)(2,1)} %param.27, bf16[64,2,128]{2,1,0:T(2,128)(2,1)S(1)} %copy.35, bf16[2,64,256,2,128]{4,3,2,1,0:T(2,128)(2,1)} %param.28, ...), kind=kLoop, calls=%fused_computation.13 | loop fusion | flops 8388608 | bytes 33636352 | tf_op jit(solution)/shard_map/jit(_where)/select_n | solution.py:43
  42.5 0.0 copy-start.2
  42.5 0.0 copy-start.4
  42.5 2.3 fusion.10
  44.8 0.3 fusion.56
  45.1 4.6 %fusion.8 = f32[64,2,1,128]{3,2,1,0:T(1,128)S(1)} fusion(bf16[64,256,2,128]{3,2,1,0:T(2,128)(2,1)} %get-tuple-element.34, bf16[64,2,256,1]{2,0,1,3:T(8,128)(2,1)S(1)} %fusion.56), kind=kOutput, calls=%fused_computation.18 | convolution fusion | flops 8388608 | bytes 8519680 | tf_op jit(solution)/shard_map/bht,bthd->bhd/dot_general | solution.py:47
  49.7 1.1 fusion.60
  50.8 0.1 all-reduce.5.cloned.1.call-update
  50.9 0.1 all-reduce.7.cloned.1.call-start
  51.0 53.5 %all-reduce.5.cloned.1.call-done = f32[64,2048]{1,0:T(8,128)} async-done(((f32[64,2048]{1,0:T(8,128)}), f32[64,2048]{1,0:T(8,128)}) %all-reduce.5.cloned.1.call-update) | async-done | bytes 524304 | tf_op jit(solution)/shard_map/psum | solution.py:49
  104.5 1.2 convert_reduce_fusion.2
  105.7 0.2 fusion.80
  106.0 5.9 %fusion.16 = f32[64,2048]{1,0:T(8,128)} fusion(bf16[2,1024,2048]{2,1,0:T(8,128)(2,1)} %param.25, bf16[2,2048,1024]{2,1,0:T(8,128)(2,1)} %param.23, bf16[64,2048]{1,0:T(8,128)(2,1)S(1)} %get-tuple-element.10, f32[2048]{0:T(1024)S(1)} %bitcast.159, f32[2048]{0:T(1024)S(1)} %bitcast.158, f32[64]{0:T(128)S(1)} %add_rsqrt_fusion.2, ...), kind=kOutput, calls=%fused_computation.26 | convolution fusion | flops 538312704 | bytes 9196032 | tf_op jit(solution)/shard_map/dot_general | solution.py:54
  111.9 0.1 all-reduce.7.cloned.1.call-update
  112.0 0.2 all-reduce.9.cloned.1.call-start
  112.3 51.8 %all-reduce.7.cloned.1.call-done = f32[64,2048]{1,0:T(8,128)} async-done(((f32[64,2048]{1,0:T(8,128)}), f32[64,2048]{1,0:T(8,128)}) %all-reduce.7.cloned.1.call-update) | async-done | bytes 524304 | tf_op jit(solution)/shard_map/psum | solution.py:55
  164.0 1.2 convert_reduce_fusion.1
  165.3 0.2 fusion.76
  165.5 2.6 fusion.46
  168.2 0.1 fusion.211
  168.4 25.7 %broadcast_select_fusion.5 = (bf16[64,256,2,128]{3,2,1,0:T(2,128)(2,1)S(1)}, bf16[64,256,2,128]{3,2,1,0:T(2,128)(2,1)}) fusion(pred[64,256]{1,0:T(8,128)(4,1)S(1)} %get-tuple-element.42, bf16[2,64,256,2,128]{4,3,2,1,0:T(2,128)(2,1)} %param.27, bf16[64,2,128]{2,1,0:T(2,128)(2,1)S(1)} %copy.40, bf16[2,64,256,2,128]{4,3,2,1,0:T(2,128)(2,1)} %param.28, ...), kind=kLoop, calls=%fused_computation.11 | loop fusion | flops 8388608 | bytes 33636352 | tf_op jit(solution)/shard_map/jit(_where)/select_n | solution.py:43
  194.1 41.4 %broadcast_select_fusion.1 = (bf16[1,64,256,2,128]{4,3,2,1,0:T(2,128)(2,1)}, bf16[1,64,256,2,128]{4,3,2,1,0:T(2,128)(2,1)}, bf16[1,64,256,2,128]{4,3,2,1,0:T(2,128)(2,1)}, bf16[1,64,256,2,128]{4,3,2,1,0:T(2,128)(2,1)}) fusion(pred[64,256]{1,0:T(8,128)(4,1)S(1)} %get-tuple-element.42, bf16[2,64,256,2,128]{4,3,2,1,0:T(2,128)(2,1)} %param.28, ...), kind=kLoop, calls=%fused_computation.7 | loop fusion | flops 16777216 | bytes 67256320 | tf_op jit(solution)/shard_map/jit(_where)/select_n | solution.py:44
  235.5 2.3 fusion.6
  237.7 0.3 fusion.57
  238.0 4.6 %fusion.4 = f32[64,2,1,128]{3,2,1,0:T(1,128)S(1)} fusion(bf16[64,256,2,128]{3,2,1,0:T(2,128)(2,1)} %get-tuple-element.32, bf16[64,2,256,1]{2,0,1,3:T(8,128)(2,1)S(1)} %fusion.57), kind=kOutput, calls=%fused_computation.14 | convolution fusion | flops 8388608 | bytes 8519680 | tf_op jit(solution)/shard_map/bht,bthd->bhd/dot_general | solution.py:47
  242.6 1.2 fusion.58
  243.8 0.1 all-reduce.9.cloned.1.call-update
  243.9 0.1 all-reduce.11.cloned.1.call-start
  243.9 27.8 %pad_maximum_fusion.1 = bf16[2,64,256,2,128]{4,3,2,1,0:T(2,128)(2,1)} fusion(bf16[1,64,256,2,128]{4,3,2,1,0:T(2,128)(2,1)} %get-tuple-element.12, bf16[1,64,256,2,128]{4,3,2,1,0:T(2,128)(2,1)} %get-tuple-element.11), kind=kLoop, calls=%fused_computation.5 | loop fusion | flops 8388608 | bytes 33554432 | tf_op jit(solution)/shard_map/stack | solution.py:59
  271.7 24.2 %all-reduce.9.cloned.1.call-done = f32[64,2048]{1,0:T(8,128)} async-done(((f32[64,2048]{1,0:T(8,128)}), f32[64,2048]{1,0:T(8,128)}) %all-reduce.9.cloned.1.call-update) | async-done | bytes 524304 | tf_op jit(solution)/shard_map/psum | solution.py:49
  295.9 1.2 convert_reduce_fusion
  297.1 0.2 fusion.72
  297.4 6.0 %fusion.12 = f32[64,2048]{1,0:T(8,128)} fusion(bf16[2,1024,2048]{2,1,0:T(8,128)(2,1)} %param.25, bf16[2,2048,1024]{2,1,0:T(8,128)(2,1)} %param.23, bf16[64,2048]{1,0:T(8,128)(2,1)S(1)} %get-tuple-element.6, f32[2048]{0:T(1024)S(1)} %bitcast.155, f32[2048]{0:T(1024)S(1)} %bitcast.154, f32[64]{0:T(128)S(1)} %add_rsqrt_fusion, ...), kind=kOutput, calls=%fused_computation.22 | convolution fusion | flops 538312704 | bytes 9196032 | tf_op jit(solution)/shard_map/dot_general | solution.py:54
  303.3 0.1 all-reduce.11.cloned.1.call-update
  303.4 27.8 %pad_maximum_fusion = bf16[2,64,256,2,128]{4,3,2,1,0:T(2,128)(2,1)} fusion(bf16[1,64,256,2,128]{4,3,2,1,0:T(2,128)(2,1)} %get-tuple-element.21, bf16[1,64,256,2,128]{4,3,2,1,0:T(2,128)(2,1)} %get-tuple-element.22), kind=kLoop, calls=%fused_computation.4 | loop fusion | flops 8388608 | bytes 33554432 | tf_op jit(solution)/shard_map/stack | solution.py:59
  331.1 24.3 %all-reduce.11.cloned.1.call-done = f32[64,2048]{1,0:T(8,128)} async-done(((f32[64,2048]{1,0:T(8,128)}), f32[64,2048]{1,0:T(8,128)}) %all-reduce.11.cloned.1.call-update) | async-done | bytes 524304 | tf_op jit(solution)/shard_map/psum | solution.py:55
  355.4 1.8 fusion.126
  (33 shorter events, 0.5 us)
Async XLA Ops:
  7.2 97.3 %all-reduce.5.cloned.1.call-start = ((), (), s32[]{:S(2)}) async-start(), calls=%async_computation | async-start | bytes 1048576 | tf_op jit(solution)/shard_map/psum | solution.py:49
  42.5 7.2 %copy-start.1 = (bf16[2,256,2048]{2,1,0:T(8,128)(2,1)S(1)}, bf16[2,256,2048]{2,1,0:T(8,128)(2,1)}, u32[]{:S(2)}) copy-start(bf16[2,256,2048]{2,1,0:T(8,128)(2,1)} %param.21) | copy-start | bytes 6291460
  42.5 8.4 %copy-start.2 = (bf16[2,2048]{1,0:T(2,128)(2,1)S(1)}, bf16[2,2048]{1,0:T(2,128)(2,1)}, u32[]{:S(2)}) copy-start(bf16[2,2048]{1,0:T(2,128)(2,1)} %param.22) | copy-start | bytes 24580
  42.5 8.5 %copy-start.4 = (bf16[2,1024]{1,0:T(2,128)(2,1)S(1)}, bf16[2,1024]{1,0:T(2,128)(2,1)}, u32[]{:S(2)}) copy-start(bf16[2,1024]{1,0:T(2,128)(2,1)} %param.24) | copy-start | bytes 12292
  42.5 62.0 %copy-start = (bf16[64,1,2048]{2,0,1:T(8,128)(2,1)S(1)}, bf16[64,1,2048]{2,0,1:T(8,128)(2,1)}, u32[]{:S(2)}) copy-start(bf16[64,1,2048]{2,0,1:T(8,128)(2,1)} %param.16) | copy-start | bytes 786436
  49.6 62.6 %copy-start.3 = (bf16[2,2048]{1,0:T(2,128)(2,1)S(1)}, bf16[2,2048]{1,0:T(2,128)(2,1)}, u32[]{:S(2)}) copy-start(bf16[2,2048]{1,0:T(2,128)(2,1)} %param.26) | copy-start | bytes 24580
  50.9 113.2 %all-reduce.7.cloned.1.call-start = ((), (), s32[]{:S(2)}) async-start(), calls=%async_computation.1 | async-start | bytes 1048576 | tf_op jit(solution)/shard_map/psum | solution.py:55
  112.0 183.9 %all-reduce.9.cloned.1.call-start = ((), (), s32[]{:S(2)}) async-start(), calls=%async_computation.2 | async-start | bytes 1048576 | tf_op jit(solution)/shard_map/psum | solution.py:49
  243.9 111.6 %all-reduce.11.cloned.1.call-start = ((), (), s32[]{:S(2)}) async-start(), calls=%async_computation.3 | async-start | bytes 1048576 | tf_op jit(solution)/shard_map/psum | solution.py:55
Sparse Core Ops, SparseCore 0:
  51.0 53.4 all-reduce.4
  112.1 51.8 all-reduce.6
  244.0 51.8 all-reduce.8
  303.5 51.8 all-reduce.10
where the time goes:
time: 367 us; the launch traced here: 364 us
  other arithmetic  162 us (44%)
  waiting for transfers between devices  154 us (42%)
  matrix products  33.1 us (9%)
  between operations  14.1 us (4%)
    psum x2, waiting for transfers between devices, device_step(): proj_sum = lax.psum(proj_part, 'tp')  77.7 us
    psum x2, waiting for transfers between devices, device_step(): down_sum = lax.psum(down_part, 'tp')  76.1 us
    another operation x2, other arithmetic, device_step(): return (x_cur[:, None, :], jnp.stack(k_list), jnp.stack(v_list))  55.5 us
    select_n x2, other arithmetic, device_step(): k_all = jnp.where(new_mask, qkv_out[:, None, :, 1, :], k_cache[layer_idx])  51.3 us
    select_n x1, other arithmetic, device_step(): v_all = jnp.where(new_mask, qkv_out[:, None, :, 2, :], v_cache[layer_idx])  41.4 us
    dot_general x2, matrix products, device_step(): jnp.dot(gelu_out, w_down[layer_idx], preferred_element_type=jnp.float32)  11.9 us
    dot_general x2, matrix products, device_step(): jnp.einsum('bht,bthd->bhd', attn_probs, v_all, preferred_element_type=jnp...  9.14 us
  transfers between devices with their start and end apart: 4, of which 4 were waited for; matrix products, arithmetic and copies ran while one was open for 15% of the time, Pallas kernels for 0%

commit v1 on v0

v1 whole, which is shorter than its diff:
```python
import functools
import math

import jax
import jax.numpy as jnp
from jax import lax
from jax.experimental import pallas as pl
from jax.experimental.pallas import tpu as pltpu
from jax.sharding import PartitionSpec as P

LN_EPS = 1e-5
MESH = pl.DeviceIdType.MESH
F32 = jnp.float32
BF16 = jnp.bfloat16
GROUP = 8
MIB = 2 ** 20


def layer_norm_f32(x_f32, gain, shift):
    mean_val = jnp.mean(x_f32, axis=-1, keepdims=True)
    centered = x_f32 - mean_val
    var_val = jnp.mean(centered * centered, axis=-1, keepdims=True)
    normed = centered * lax.rsqrt(var_val + LN_EPS)
    return (normed * gain.astype(F32) + shift.astype(F32)).astype(BF16)


def attn_kernel(layer, n_heads, first, *refs):
    if first:
        (x_ref, gain_ref, shift_ref, wq_hbm, bq_ref, wo_hbm, slot_smem, slot_ref, pos_ref, valid_ref, k_hbm, v_hbm,
         part_ref, k_out, v_out,
         wq, wo, kbuf, vbuf, qkv, bias, attn, sem_w, sem_in, sem_out) = refs
    else:
        (x_ref, gain_ref, shift_ref, wq_hbm, bq_ref, wo_hbm, slot_smem, slot_ref, pos_ref, valid_ref, k_hbm, v_hbm,
         k_alias, v_alias,
         part_ref, k_out, v_out,
         wq, wo, kbuf, vbuf, qkv, bias, attn, sem_w, sem_in, sem_out) = refs
    n_batch, n_cols, head_dim = kbuf.shape
    n_groups = n_batch // GROUP
    n_local = attn.shape[1] // head_dim
    width = x_ref.shape[1]
    cache_len = n_cols // n_local
    n_chunk = 4
    step = width // n_chunk
    w_copies = [
        pltpu.make_async_copy(wq_hbm.at[layer, pl.ds(i * step, step)], wq.at[pl.ds(i * step, step)], sem_w.at[i])
        for i in range(n_chunk)
    ]
    for c in w_copies:
        c.start()

    def in_copy(which, g):
        src, dst = ((k_hbm, kbuf), (v_hbm, vbuf))[which]
        return pltpu.make_async_copy(src.at[layer, pl.ds(g * GROUP, GROUP)], dst.at[pl.ds(g * GROUP, GROUP)], sem_in.at[which, g])

    def out_copy(which, g):
        src, dst = ((kbuf, k_out), (vbuf, v_out))[which]
        return pltpu.make_async_copy(src.at[pl.ds(g * GROUP, GROUP)], dst.at[layer, pl.ds(g * GROUP, GROUP)], sem_out.at[which])

    for g in range(n_groups):
        in_copy(0, g).start()
        in_copy(1, g).start()
    wo_copy = pltpu.make_async_copy(wo_hbm.at[layer], wo, sem_w.at[n_chunk])
    wo_copy.start()

    t_row = lax.broadcasted_iota(jnp.int32, (cache_len, n_cols), 0)
    t_col = lax.broadcasted_iota(jnp.int32, (cache_len, n_cols), 1) // n_local
    spread = (t_row == t_col).astype(BF16)
    pos = jnp.dot(pos_ref[...].astype(F32).astype(BF16), spread, preferred_element_type=F32)
    valid = jnp.dot(valid_ref[...].astype(F32).astype(BF16), spread, preferred_element_type=F32)
    col = lax.broadcasted_iota(jnp.int32, (n_batch, n_cols), 1)
    allowed = jnp.logical_or(valid > 0.5, col // n_local == slot_ref[...])
    head0 = lax.axis_index('tp') * n_local
    for h in range(n_local):
        num = (jnp.full((n_batch, n_cols), 1 + h, jnp.int32) + head0).astype(F32)
        slope = jnp.exp2(-8.0 * num / n_heads)
        keep = jnp.logical_and(allowed, col % n_local == h)
        bias[h] = jnp.where(keep, slope * pos, -jnp.inf)

    if first:
        x_in = layer_norm_f32(x_ref[...].astype(F32), gain_ref[layer, 0:1], shift_ref[layer, 0:1])
    else:
        x_in = x_ref[...]
    acc = None
    for i in range(n_chunk):
        w_copies[i].wait()
        d = jnp.dot(x_in[:, i * step:(i + 1) * step], wq[i * step:(i + 1) * step], preferred_element_type=F32)
        acc = d if acc is None else acc + d
    qkv[...] = (acc + bq_ref[layer:layer + 1].astype(F32)).astype(BF16).astype(F32)

    scale = 1.0 / math.sqrt(head_dim)
    rows = n_local * GROUP

    def group(g, carry):
        in_copy(0, g).wait()
        in_copy(1, g).wait()
        base = pl.multiple_of(g * GROUP, GROUP)
        row16 = lax.broadcasted_iota(jnp.int32, (16, head_dim), 0)
        fresh = qkv[pl.ds(base, GROUP), :]
        for b in range(GROUP):
            first_row = slot_smem[g * GROUP + b] * n_local
            start = pl.multiple_of((first_row // 16) * 16, 16)
            off = first_row - start
            for which, buf in ((1, kbuf), (2, vbuf)):
                block = buf[base + b, pl.ds(start, 16), :].astype(F32)
                for h in range(n_local):
                    new = fresh[b:b + 1, (3 * h + which) * head_dim:(3 * h + which + 1) * head_dim]
                    block = jnp.where(row16 == off + h, new, block)
                buf[base + b, pl.ds(start, 16), :] = block.astype(BF16)
        q16 = jnp.concatenate(
            [fresh[:, 3 * h * head_dim:(3 * h + 1) * head_dim] for h in range(n_local)], axis=0
        ).astype(BF16)
        row_s = lax.broadcasted_iota(jnp.int32, (rows, n_cols), 0) % GROUP
        s = None
        for b in range(GROUP):
            sb = lax.dot_general(q16, kbuf[base + b], (((1,), (1,)), ((), ())), preferred_element_type=F32)
            s = sb if s is None else jnp.where(row_s == b, sb, s)
        s = s * scale + jnp.concatenate([bias[h, pl.ds(base, GROUP)] for h in range(n_local)], axis=0)
        top = jnp.max(s, axis=-1, keepdims=True)
        e = jnp.exp(s - top)
        p = (e * (1.0 / jnp.sum(e, axis=-1, keepdims=True))).astype(BF16)
        row_o = lax.broadcasted_iota(jnp.int32, (rows, head_dim), 0) % GROUP
        o = None
        for b in range(GROUP):
            ob = jnp.dot(p, vbuf[base + b], preferred_element_type=F32)
            o = ob if o is None else jnp.where(row_o == b, ob, o)
        for h in range(n_local):
            attn[pl.ds(base, GROUP), h * head_dim:(h + 1) * head_dim] = o[h * GROUP:(h + 1) * GROUP]
        out_copy(0, g).start()
        out_copy(1, g).start()
        return carry

    lax.fori_loop(0, n_groups, group, 0)
    wo_copy.wait()
    part_ref[...] = jnp.dot(attn[...].astype(BF16), wo[...], preferred_element_type=F32)
    for g in range(n_groups):
        out_copy(0, g).wait()
        out_copy(1, g).wait()


def reduce_kernel(layer, n_tp, last, *refs):
    n_out = 1 if last else 2
    (part_ref, res_ref, gain_ref, shift_ref, bo_ref, wu_hbm, bu_ref, wd_hbm, bd_ref) = refs[:9]
    out_ref = refs[9]
    own_ref = None if last else refs[10]
    (wu, wd, part2, d2d, mid, got, gath, gath2, sem_w, pair_s, pair_r, chip_s, chip_r, ag_s, ag_r, agp_s, agp_r) = refs[9 + n_out:]
    n_batch, width = part_ref.shape
    n_chip = n_tp // 2
    blk = n_batch // n_tp
    me = lax.axis_index('tp')
    x = me // 2
    c = me % 2
    partner = x * 2 + (1 - c)

    def chip(d):
        return lax.rem(x + d, n_chip)

    w_copies = [pltpu.make_async_copy(wu_hbm.at[layer], wu, sem_w.at[0]), pltpu.make_async_copy(wd_hbm.at[layer], wd, sem_w.at[1])]
    for w in w_copies:
        w.start()
    barrier = pltpu.get_barrier_semaphore()
    peers = [partner] + [chip(d) * 2 + c for d in range(1, n_chip)]
    for peer in peers:
        pl.semaphore_signal(barrier, inc=1, device_id={'tp': peer}, device_id_type=MESH)
    pl.semaphore_wait(barrier, len(peers))

    order = [2, 1, 3, 0] if n_chip == 4 else list(range(1, n_chip)) + [0]

    def rows_of(core, d):
        return pl.ds(pl.multiple_of((core * n_chip + chip(d)) * blk, blk), blk)

    def reduce_scatter(phase, src):
        pair = {
            d: pltpu.make_async_remote_copy(
                src_ref=src.at[rows_of(1 - c, d)], dst_ref=d2d.at[phase, d], send_sem=pair_s.at[phase, d],
                recv_sem=pair_r.at[phase, d], device_id={'tp': partner}, device_id_type=MESH)
            for d in order
        }
        for d in order:
            pair[d].start()
        hops = {}
        acc = None
        for d in order:
            pair[d].wait_recv()
            both = src[rows_of(c, d), :] + d2d[phase, d]
            if d == 0:
                acc = both
            else:
                mid[phase, d] = both
                hops[d] = pltpu.make_async_remote_copy(
                    src_ref=mid.at[phase, d], dst_ref=got.at[phase, d], send_sem=chip_s.at[phase, d],
                    recv_sem=chip_r.at[phase, d], device_id={'tp': chip(d) * 2 + c}, device_id_type=MESH)
                hops[d].start()
        for d in sorted(hops, key=lambda d: min(d, n_chip - d)):
            hops[d].wait_recv()
            acc = acc + got[phase, d]
        for d in order:
            pair[d].wait_send()
            if d:
                hops[d].wait_send()
        return acc

    def all_gather(phase, buf, value):
        buf[c, x] = value
        hops = {}
        for d in order[:-1]:
            hops[d] = pltpu.make_async_remote_copy(
                src_ref=buf.at[c, x], dst_ref=buf.at[c, x], send_sem=ag_s.at[phase, d], recv_sem=ag_r.at[phase, d],
                device_id={'tp': chip(d) * 2 + c}, device_id_type=MESH)
            hops[d].start()

        def pass_on(d):
            slot = lax.rem(x + n_chip - d, n_chip)
            cp = pltpu.make_async_remote_copy(
                src_ref=buf.at[c, slot], dst_ref=buf.at[c, slot], send_sem=agp_s.at[phase, d], recv_sem=agp_r.at[phase, d],
                device_id={'tp': partner}, device_id_type=MESH)
            cp.start()
            return cp

        passed = [pass_on(0)]
        for d in sorted(hops, key=lambda d: min(d, n_chip - d)):
            hops[d].wait_recv()
            passed.append(pass_on(d))
        for cp in passed:
            cp.wait()
        for d in hops:
            hops[d].wait_send()
        return buf[...].astype(F32).reshape(n_batch, width)

    if last:
        res = res_ref[...].astype(F32)
    else:
        res = res_ref[rows_of(c, 0), :].astype(F32)
    total = reduce_scatter(0, part_ref)
    x_mid = (res + total + bo_ref[layer:layer + 1].astype(F32)).astype(BF16).astype(F32)
    normed = all_gather(0, gath, layer_norm_f32(x_mid, gain_ref[layer, 1:2], shift_ref[layer, 1:2])).astype(BF16)
    w_copies[0].wait()
    up = jnp.dot(normed, wu[...], preferred_element_type=F32) + bu_ref[layer:layer + 1].astype(F32)
    act = jax.nn.gelu(up, approximate=True).astype(BF16)
    w_copies[1].wait()
    part2[...] = jnp.dot(act, wd[...], preferred_element_type=F32)
    total = reduce_scatter(1, part2)
    x_next = (x_mid + total + bd_ref[layer:layer + 1].astype(F32)).astype(BF16)
    if last:
        out_ref[...] = all_gather(1, gath2, x_next).astype(BF16)
    else:
        own_ref[...] = x_next
        nxt = layer_norm_f32(x_next.astype(F32), gain_ref[layer + 1, 0:1], shift_ref[layer + 1, 0:1])
        out_ref[...] = all_gather(1, gath2, nxt).astype(BF16)


def solution(mesh):
    tp_size = mesh.shape['tp']
    vm = pl.BlockSpec(memory_space=pltpu.VMEM)
    sm = pl.BlockSpec(memory_space=pltpu.SMEM)
    hbm = pl.BlockSpec(memory_space=pltpu.HBM)

    def device_step(hidden, ln_gain, ln_shift, w_qkv, b_qkv, w_out, b_out, w_up, b_up, w_down, b_down, k_cache, v_cache, write_slot, key_pos, key_valid):
        n_layers, n_batch, cache_len, n_local, head_dim = k_cache.shape
        width = hidden.shape[-1]
        n_cols = cache_len * n_local
        flat = (n_layers, n_batch, n_cols, head_dim)
        in_hbm = functools.partial(pltpu.with_memory_space_constraint, memory_space=pltpu.HBM)
        k_in, v_in = in_hbm(k_cache.reshape(flat)), in_hbm(v_cache.reshape(flat))
        w_qkv, w_out, w_up, w_down = map(in_hbm, (w_qkv, w_out, w_up, w_down))
        x0 = hidden.reshape(n_batch, width)
        slot_col = write_slot.reshape(n_batch, 1)
        n_groups = n_batch // GROUP
        blk = n_batch // tp_size
        n_chip = tp_size // 2

        def attn(layer, x_in, caches):
            first = caches is None
            ins = [x_in, ln_gain, ln_shift, w_qkv, b_qkv, w_out, write_slot, slot_col, key_pos, key_valid, k_in, v_in]
            specs = [vm, vm, vm, hbm, vm, hbm, sm, vm, vm, vm, hbm, hbm]
            alias = {}
            if not first:
                alias = {len(ins): 1, len(ins) + 1: 2}
                ins += list(caches)
                specs += [hbm, hbm]
            shape = jax.ShapeDtypeStruct(flat, BF16)
            return pl.pallas_call(
                functools.partial(attn_kernel, layer, n_local * tp_size, first),
                out_shape=(jax.ShapeDtypeStruct((n_batch, width), F32), shape, shape),
                in_specs=specs,
                out_specs=(vm, hbm, hbm),
                scratch_shapes=[
                    pltpu.VMEM(w_qkv.shape[1:], BF16),
                    pltpu.VMEM(w_out.shape[1:], BF16),
                    pltpu.VMEM(flat[1:], BF16),
                    pltpu.VMEM(flat[1:], BF16),
                    pltpu.VMEM((n_batch, b_qkv.shape[1]), F32),
                    pltpu.VMEM((n_local, n_batch, n_cols), F32),
                    pltpu.VMEM((n_batch, n_local * head_dim), F32),
                    pltpu.SemaphoreType.DMA((5,)),
                    pltpu.SemaphoreType.DMA((2, n_groups)),
                    pltpu.SemaphoreType.DMA((2,)),
                ],
                input_output_aliases=alias,
                compiler_params=pltpu.CompilerParams(vmem_limit_bytes=48 * MIB),
                name=f'attn_{layer}',
            )(*ins)

        def reduce(layer, part, res):
            last = layer == n_layers - 1
            ins = [part, res, ln_gain, ln_shift, b_out, w_up, b_up, w_down, b_down]
            specs = [vm, vm, vm, vm, vm, hbm, vm, hbm, vm]
            outs = [jax.ShapeDtypeStruct((n_batch, width), BF16)]
            if not last:
                outs.append(jax.ShapeDtypeStruct((blk, width), BF16))
            dma = pltpu.SemaphoreType.DMA((2, n_chip))
            return pl.pallas_call(
                functools.partial(reduce_kernel, layer, tp_size, last),
                out_shape=tuple(outs),
                in_specs=specs,
                out_specs=tuple([vm] * len(outs)),
                scratch_shapes=[
                    pltpu.VMEM(w_up.shape[1:], BF16),
                    pltpu.VMEM(w_down.shape[1:], BF16),
                    pltpu.VMEM((n_batch, width), F32),
                    pltpu.VMEM((2, n_chip, blk, width), F32),
                    pltpu.VMEM((2, n_chip, blk, width), F32),
                    pltpu.VMEM((2, n_chip, blk, width), F32),
                    pltpu.VMEM((2, n_chip, blk, width), BF16),
                    pltpu.VMEM((2, n_chip, blk, width), BF16),
                    pltpu.SemaphoreType.DMA((2,)),
                ] + [dma] * 8,
                compiler_params=pltpu.CompilerParams(vmem_limit_bytes=32 * MIB, collective_id=layer, has_side_effects=True),
                name=f'reduce_{layer}',
            )(*ins)

        caches, x_in, res = None, x0, x0
        for layer in range(n_layers):
            part, k_new, v_new = attn(layer, x_in, caches)
            caches = (k_new, v_new)
            outs = reduce(layer, part, res)
            x_in = outs[0]
            res = outs[-1]
        return x_in[:, None, :], caches[0].reshape(k_cache.shape), caches[1].reshape(v_cache.shape)

    cache_spec = P(None, 'dp', None, 'tp', None)
    in_specs = (P('dp', None, None), P(), P(), P(None, None, 'tp'), P(None, 'tp'), P(None, 'tp', None), P(), P(None, None, 'tp'), P(None, 'tp'), P(None, 'tp', None), P(), cache_spec, cache_spec, P('dp'), P('dp', None), P('dp', None))
    out_specs = (P('dp', None, None), cache_spec, cache_spec)
    return jax.shard_map(device_step, mesh=mesh, in_specs=in_specs, out_specs=out_specs, check_vma=False)
```

time: 367 us -> 93.7 us (0.26)
  other arithmetic: 162 us -> 0 us
  waiting for transfers between devices: 154 us -> 0 us
  Pallas kernels: 0 us -> 85.7 us
  matrix products: 33.1 us -> 0 us
  between operations: 14.1 us -> 0.69 us
  local copies, waits for them, and re-layouts: 0.67 us -> 6.86 us
    psum x4 -> x0, waiting for transfers between devices: 154 us -> none  [the longest x2 77.7 us: device_step(): proj_sum = lax.psum(proj_part, 'tp')]
    select_n x3 -> x0, other arithmetic: 92.6 us -> none  [the longest x2 51.3 us: device_step(): k_all = jnp.where(new_mask, qkv_out[:, None, :, 1, :], k_cache[layer_idx])]
    pallas_call x0 -> x4, Pallas kernels: none -> 85.7 us  [the longest x2 56.3 us: reduce(): pl.pallas_call(functools.partial(reduce_kernel, layer, tp_size, last), ou...]
    another operation x2 -> x0, other arithmetic: 55.5 us -> none  [device_step(): return (x_cur[:, None, :], jnp.stack(k_list), jnp.stack(v_list))]
    dot_general x10 -> x0, matrix products: 33.1 us -> none  [the longest x2 11.9 us: device_step(): jnp.dot(gelu_out, w_down[layer_idx], preferred_element_type=jnp.float32)]
    reduce_sum x8 -> x0, other arithmetic: 6.67 us -> none  [the longest x4 4.75 us: layer_norm(): mean_val = jnp.mean(x_f32, axis=-1, keepdims=True)]
    unnamed x10 -> x21, local copies, waits for them, and re-layouts: 0.03 us -> 6.12 us
  transfers between devices with their start and end apart: 4 -> 0, of which waited for: 4 -> 0; matrix products, arithmetic and copies ran while one was open for 15% -> 0% of each run, Pallas kernels for 0% -> 0%
where the time goes in v1:
time: 93.7 us; the launch traced here: 93.3 us
  Pallas kernels  85.7 us (91%)
  local copies, waits for them, and re-layouts  6.86 us (7%)
    pallas_call x2, Pallas kernels, reduce(): pl.pallas_call(functools.partial(reduce_kernel, layer, tp_size, last), ou...  56.3 us
    pallas_call x2, Pallas kernels, attn(): pl.pallas_call(functools.partial(attn_kernel, layer, n_local * tp_size, f...  29.5 us
    unnamed x21, local copies, waits for them, and re-layouts  6.12 us

profile of v1, /device:TPU:113, one launch (start us, length us, event | category | flops | bytes accessed | tf_op | source)
XLA Modules:
  0.0 93.3 jit_solution(18359638640585859074)
XLA Ops:
  0.6 0.7 copy.21.refs_7_
  1.4 0.0 copy-start
  1.4 0.9 %copy-done = bf16[64,1,2048]{2,0,1:T(8,128)(2,1)S(1)} copy-done((bf16[64,1,2048]{2,0,1:T(8,128)(2,1)S(1)}, bf16[64,1,2048]{2,0,1:T(8,128)(2,1)}, u32[]{:S(2)}) %copy-start) | copy-done | bytes 262168
  2.3 0.0 copy-start.1
  2.3 0.8 copy-done.1
  3.2 0.0 copy-start.2
  3.2 0.8 copy-done.2
  4.0 0.0 copy-start.3
  4.0 0.7 copy-done.3
  4.7 0.0 copy-start.4
  4.7 0.7 copy-done.4
  5.4 0.0 copy-start.8
  5.4 0.7 copy-done.8
  6.1 0.0 copy-start.9
  6.1 0.7 copy-done.9
  6.8 0.0 copy-start.5
  6.8 0.0 copy-start.6
  6.8 0.0 copy-start.7
  6.8 15.1 %attn_0.1 = (f32[64,2048]{1,0:T(8,128)S(1)}, bf16[2,64,512,128]{3,2,1,0:T(8,128)(2,1)}, bf16[2,64,512,128]{3,2,1,0:T(8,128)(2,1)}) custom-call(bf16[64,2048]{1,0:T(8,128)(2,1)S(1)} %bitcast.7, bf16[2,2,2048]{2,1,0:T(2,128)(2,1)S(1)} %copy-done.3, bf16[2,2,2048]{2,1,0:T(2,128)(2,1)S(1)} %copy-done.4, bf16[2,2048,768]{2,1,0:T(8,128)(2,1)} %refs_3_.6, ...), custom_call_target="tpu_custom_call" | custom-call | tf_op jit(solution)/shard_map/attn_0/pallas_call | solution.py:281
  21.9 0.0 copy-done.5
  21.9 0.0 copy-done.6
  21.9 0.0 copy-done.7
  22.0 29.5 %reduce_0.1 = (bf16[64,2048]{1,0:T(8,128)(2,1)S(1)}, bf16[8,2048]{1,0:T(8,128)(2,1)S(1)}) custom-call(f32[64,2048]{1,0:T(8,128)S(1)} %get-tuple-element.11.refs_0_, bf16[64,2048]{1,0:T(8,128)(2,1)S(1)} %bitcast.8, bf16[2,2,2048]{2,1,0:T(2,128)(2,1)S(1)} %copy-done.3, bf16[2,2,2048]{2,1,0:T(2,128)(2,1)S(1)} %copy-done.4, bf16[2,2048]{1,0:T(2,128)(2,1)S(1)} %copy-done.5, ...), custom_call_target="tpu_custom_call" | custom-call | tf_op jit(solution)/shard_map/reduce_0/pallas_call | solution.py:311
  51.4 14.3 %attn_1.1 = (f32[64,2048]{1,0:T(8,128)S(1)}, bf16[2,64,512,128]{3,2,1,0:T(8,128)(2,1)}, bf16[2,64,512,128]{3,2,1,0:T(8,128)(2,1)}) custom-call(bf16[64,2048]{1,0:T(8,128)(2,1)S(1)} %get-tuple-element.12.refs_0_, bf16[2,2,2048]{2,1,0:T(2,128)(2,1)S(1)} %copy-done.3, ...), custom_call_target="tpu_custom_call", output_to_operand_aliasing={{1}: (12, {}), {2}: (13, {})} | custom-call | tf_op jit(solution)/shard_map/attn_1/pallas_call | solution.py:281
  65.8 26.8 %reduce_1.1 = bf16[64,2048]{1,0:T(8,128)(2,1)S(1)} custom-call(f32[64,2048]{1,0:T(8,128)S(1)} %get-tuple-element.15.refs_0_, bf16[8,2048]{1,0:T(8,128)(2,1)S(1)} %get-tuple-element.16.refs_1_, bf16[2,2,2048]{2,1,0:T(2,128)(2,1)S(1)} %copy-done.3, bf16[2,2,2048]{2,1,0:T(2,128)(2,1)S(1)} %copy-done.4, bf16[2,2048]{1,0:T(2,128)(2,1)S(1)} %copy-done.5, ...), custom_call_target="tpu_custom_call" | custom-call | tf_op jit(solution)/shard_map/reduce_1/pallas_call | solution.py:311
  92.6 0.7 copy.26
Async XLA Ops:
  1.4 0.9 %copy-start = (bf16[64,1,2048]{2,0,1:T(8,128)(2,1)S(1)}, bf16[64,1,2048]{2,0,1:T(8,128)(2,1)}, u32[]{:S(2)}) copy-start(bf16[64,1,2048]{2,0,1:T(8,128)(2,1)} %param.16) | copy-start | bytes 786436
  2.3 0.8 copy-start.1
  3.2 0.8 copy-start.2
  4.0 0.7 copy-start.3
  4.7 0.7 copy-start.4
  5.4 0.7 copy-start.8
  6.1 0.7 copy-start.9
  6.8 15.1 %copy-start.5 = (bf16[2,2048]{1,0:T(2,128)(2,1)S(1)}, bf16[2,2048]{1,0:T(2,128)(2,1)}, u32[]{:S(2)}) copy-start(bf16[2,2048]{1,0:T(2,128)(2,1)} %refs_4_.7) | copy-start | bytes 24580
  6.8 15.2 %copy-start.6 = (bf16[2,2048]{1,0:T(2,128)(2,1)S(1)}, bf16[2,2048]{1,0:T(2,128)(2,1)}, u32[]{:S(2)}) copy-start(bf16[2,2048]{1,0:T(2,128)(2,1)} %refs_8_.7) | copy-start | bytes 24580
  6.8 15.2 %copy-start.7 = (bf16[2,1024]{1,0:T(2,128)(2,1)S(1)}, bf16[2,1024]{1,0:T(2,128)(2,1)}, u32[]{:S(2)}) copy-start(bf16[2,1024]{1,0:T(2,128)(2,1)} %refs_6_.7) | copy-start | bytes 12292

commit v2 on v1

--- a/solution.py
+++ b/solution.py
@@ -26,14 +26,16 @@
 
 def attn_kernel(layer, n_heads, first, *refs):
     if first:
-        (x_ref, gain_ref, shift_ref, wq_hbm, bq_ref, wo_hbm, slot_smem, slot_ref, pos_ref, valid_ref, k_hbm, v_hbm,
-         part_ref, k_out, v_out,
-         wq, wo, kbuf, vbuf, qkv, bias, attn, sem_w, sem_in, sem_out) = refs
-    else:
-        (x_ref, gain_ref, shift_ref, wq_hbm, bq_ref, wo_hbm, slot_smem, slot_ref, pos_ref, valid_ref, k_hbm, v_hbm,
-         k_alias, v_alias,
-         part_ref, k_out, v_out,
-         wq, wo, kbuf, vbuf, qkv, bias, attn, sem_w, sem_in, sem_out) = refs
+        (x_in_ref, gain_in, shift_in, bq_in, wq_hbm, wo_hbm, slot_hbm, pos_in, valid_in, k_hbm, v_hbm,
+         part_ref, kall, vall,
+         x_ref, gain_ref, shift_ref, bq_ref, pos_ref, valid_ref, slot_smem,
+         wq, wo, qkv, bias, attn, sem_w, sem_s, sem_in) = refs
+    else:
+        (x_ref, bq_in, wq_hbm, wo_hbm, slot_hbm, pos_in, valid_in, k_raw, v_raw,
+         part_ref, k_out, v_out, kall, vall,
+         bq_ref, pos_ref, valid_ref, slot_smem,
+         wq, wo, qkv, bias, attn, sem_w, sem_s, sem_out) = refs
+    kbuf, vbuf = kall.at[layer], vall.at[layer]
     n_batch, n_cols, head_dim = kbuf.shape
     n_groups = n_batch // GROUP
     n_local = attn.shape[1] // head_dim
@@ -41,12 +43,19 @@
     cache_len = n_cols // n_local
     n_chunk = 4
     step = width // n_chunk
+    pairs = [(slot_hbm, slot_smem), (pos_in, pos_ref), (valid_in, valid_ref), (bq_in, bq_ref)]
+    if first:
+        pairs = [(x_in_ref, x_ref), (gain_in, gain_ref), (shift_in, shift_ref)] + pairs
+    small = [pltpu.make_async_copy(src, dst, sem_s.at[i]) for i, (src, dst) in enumerate(pairs)]
+    for c in small:
+        c.start()
     w_copies = [
         pltpu.make_async_copy(wq_hbm.at[layer, pl.ds(i * step, step)], wq.at[pl.ds(i * step, step)], sem_w.at[i])
         for i in range(n_chunk)
     ]
     for c in w_copies:
         c.start()
+    wo_copy = pltpu.make_async_copy(wo_hbm.at[layer], wo, sem_w.at[n_chunk])
 
     def in_copy(which, g):
         src, dst = ((k_hbm, kbuf), (v_hbm, vbuf))[which]
@@ -56,25 +65,30 @@
         src, dst = ((kbuf, k_out), (vbuf, v_out))[which]
         return pltpu.make_async_copy(src.at[pl.ds(g * GROUP, GROUP)], dst.at[layer, pl.ds(g * GROUP, GROUP)], sem_out.at[which])
 
-    for g in range(n_groups):
-        in_copy(0, g).start()
-        in_copy(1, g).start()
-    wo_copy = pltpu.make_async_copy(wo_hbm.at[layer], wo, sem_w.at[n_chunk])
-    wo_copy.start()
+    if first:
+        for g in range(n_groups):
+            in_copy(0, g).start()
+            in_copy(1, g).start()
+        wo_copy.start()
+        old = []
+    else:
+        wo_copy.start()
+        old = [
+            pltpu.make_async_copy(src.at[layer - 1, pl.ds(g * GROUP, GROUP)], dst.at[layer - 1, pl.ds(g * GROUP, GROUP)], sem_out.at[2 + i])
+            for g in range(n_groups) for i, (src, dst) in enumerate(((kall, k_out), (vall, v_out)))
+        ]
+        for c in old:
+            c.start()
 
     t_row = lax.broadcasted_iota(jnp.int32, (cache_len, n_cols), 0)
     t_col = lax.broadcasted_iota(jnp.int32, (cache_len, n_cols), 1) // n_local
     spread = (t_row == t_col).astype(BF16)
+    for c in small:
+        c.wait()
     pos = jnp.dot(pos_ref[...].astype(F32).astype(BF16), spread, preferred_element_type=F32)
     valid = jnp.dot(valid_ref[...].astype(F32).astype(BF16), spread, preferred_element_type=F32)
-    col = lax.broadcasted_iota(jnp.int32, (n_batch, n_cols), 1)
-    allowed = jnp.logical_or(valid > 0.5, col // n_local == slot_ref[...])
-    head0 = lax.axis_index('tp') * n_local
-    for h in range(n_local):
-        num = (jnp.full((n_batch, n_cols), 1 + h, jnp.int32) + head0).astype(F32)
-        slope = jnp.exp2(-8.0 * num / n_heads)
-        keep = jnp.logical_and(allowed, col % n_local == h)
-        bias[h] = jnp.where(keep, slope * pos, -jnp.inf)
+    bias[0] = pos
+    bias[1] = valid
 
     if first:
         x_in = layer_norm_f32(x_ref[...].astype(F32), gain_ref[layer, 0:1], shift_ref[layer, 0:1])
@@ -89,15 +103,21 @@
 
     scale = 1.0 / math.sqrt(head_dim)
     rows = n_local * GROUP
+    head0 = lax.axis_index('tp') * n_local
 
     def group(g, carry):
-        in_copy(0, g).wait()
-        in_copy(1, g).wait()
+        if first:
+            in_copy(0, g).wait()
+            in_copy(1, g).wait()
         base = pl.multiple_of(g * GROUP, GROUP)
         row16 = lax.broadcasted_iota(jnp.int32, (16, head_dim), 0)
         fresh = qkv[pl.ds(base, GROUP), :]
+        row8 = lax.broadcasted_iota(jnp.int32, (GROUP, n_cols), 0)
+        slots = jnp.zeros((GROUP, n_cols), jnp.int32)
         for b in range(GROUP):
-            first_row = slot_smem[g * GROUP + b] * n_local
+            slot = slot_smem[g * GROUP + b]
+            slots = jnp.where(row8 == b, slot, slots)
+            first_row = slot * n_local
             start = pl.multiple_of((first_row // 16) * 16, 16)
             off = first_row - start
             for which, buf in ((1, kbuf), (2, vbuf)):
@@ -106,6 +126,14 @@
                     new = fresh[b:b + 1, (3 * h + which) * head_dim:(3 * h + which + 1) * head_dim]
                     block = jnp.where(row16 == off + h, new, block)
                 buf[base + b, pl.ds(start, 16), :] = block.astype(BF16)
+        col = lax.broadcasted_iota(jnp.int32, (GROUP, n_cols), 1)
+        allowed = jnp.logical_or(bias[1, pl.ds(base, GROUP)] > 0.5, col // n_local == slots)
+        pos_g = bias[0, pl.ds(base, GROUP)]
+        parts = []
+        for h in range(n_local):
+            num = (jnp.full((GROUP, n_cols), 1 + h, jnp.int32) + head0).astype(F32)
+            slope = jnp.exp2(-8.0 * num / n_heads)
+            parts.append(jnp.where(jnp.logical_and(allowed, col % n_local == h), slope * pos_g, -jnp.inf))
         q16 = jnp.concatenate(
             [fresh[:, 3 * h * head_dim:(3 * h + 1) * head_dim] for h in range(n_local)], axis=0
         ).astype(BF16)
@@ -114,7 +142,7 @@
         for b in range(GROUP):
             sb = lax.dot_general(q16, kbuf[base + b], (((1,), (1,)), ((), ())), preferred_element_type=F32)
             s = sb if s is None else jnp.where(row_s == b, sb, s)
-        s = s * scale + jnp.concatenate([bias[h, pl.ds(base, GROUP)] for h in range(n_local)], axis=0)
+        s = s * scale + jnp.concatenate(parts, axis=0)
         top = jnp.max(s, axis=-1, keepdims=True)
         e = jnp.exp(s - top)
         p = (e * (1.0 / jnp.sum(e, axis=-1, keepdims=True))).astype(BF16)
@@ -125,24 +153,31 @@
             o = ob if o is None else jnp.where(row_o == b, ob, o)
         for h in range(n_local):
             attn[pl.ds(base, GROUP), h * head_dim:(h + 1) * head_dim] = o[h * GROUP:(h + 1) * GROUP]
-        out_copy(0, g).start()
-        out_copy(1, g).start()
+        if not first:
+            out_copy(0, g).start()
+            out_copy(1, g).start()
         return carry
 
     lax.fori_loop(0, n_groups, group, 0)
     wo_copy.wait()
     part_ref[...] = jnp.dot(attn[...].astype(BF16), wo[...], preferred_element_type=F32)
-    for g in range(n_groups):
-        out_copy(0, g).wait()
-        out_copy(1, g).wait()
+    if not first:
+        for c in old:
+            c.wait()
+        for g in range(n_groups):
+            out_copy(0, g).wait()
+            out_copy(1, g).wait()
 
 
 def reduce_kernel(layer, n_tp, last, *refs):
-    n_out = 1 if last else 2
-    (part_ref, res_ref, gain_ref, shift_ref, bo_ref, wu_hbm, bu_ref, wd_hbm, bd_ref) = refs[:9]
-    out_ref = refs[9]
-    own_ref = None if last else refs[10]
-    (wu, wd, part2, d2d, mid, got, gath, gath2, sem_w, pair_s, pair_r, chip_s, chip_r, ag_s, ag_r, agp_s, agp_r) = refs[9 + n_out:]
+    if last:
+        part_ref, res_ref, gain_ref, shift_ref, bo_ref, wu_hbm, bu_ref, wd_hbm, bd_ref, out_ref = refs[:10]
+        rest = refs[10:]
+    else:
+        (part_ref, res_ref, gain_ref, shift_ref, bo_ref, wu_hbm, bu_ref, wd_hbm, bd_ref, k_hbm, v_hbm, k_raw, v_raw,
+         out_ref, own_ref, kall, vall) = refs[:17]
+        rest = refs[17:]
+    (wu, wd, part2, d2d, mid, got, gath, gath2, sem_w, pair_s, pair_r, chip_s, chip_r, ag_s, ag_r, agp_s, agp_r) = rest
     n_batch, width = part_ref.shape
     n_chip = n_tp // 2
     blk = n_batch // n_tp
@@ -155,6 +190,9 @@
         return lax.rem(x + d, n_chip)
 
     w_copies = [pltpu.make_async_copy(wu_hbm.at[layer], wu, sem_w.at[0]), pltpu.make_async_copy(wd_hbm.at[layer], wd, sem_w.at[1])]
+    if not last:
+        w_copies.append(pltpu.make_async_copy(k_hbm.at[layer + 1], kall.at[layer + 1], sem_w.at[2]))
+        w_copies.append(pltpu.make_async_copy(v_hbm.at[layer + 1], vall.at[layer + 1], sem_w.at[3]))
     for w in w_copies:
         w.start()
     barrier = pltpu.get_barrier_semaphore()
@@ -246,6 +284,8 @@
         own_ref[...] = x_next
         nxt = layer_norm_f32(x_next.astype(F32), gain_ref[layer + 1, 0:1], shift_ref[layer + 1, 0:1])
         out_ref[...] = all_gather(1, gath2, nxt).astype(BF16)
+        w_copies[2].wait()
+        w_copies[3].wait()
 
 
 def solution(mesh):
@@ -263,50 +303,57 @@
         k_in, v_in = in_hbm(k_cache.reshape(flat)), in_hbm(v_cache.reshape(flat))
         w_qkv, w_out, w_up, w_down = map(in_hbm, (w_qkv, w_out, w_up, w_down))
         x0 = hidden.reshape(n_batch, width)
-        slot_col = write_slot.reshape(n_batch, 1)
         n_groups = n_batch // GROUP
         blk = n_batch // tp_size
         n_chip = tp_size // 2
+        shape = jax.ShapeDtypeStruct(flat, BF16)
+        held = pltpu.VMEM(flat, BF16)
+        shared = [in_hbm(a) for a in (b_qkv, w_qkv, w_out, write_slot, key_pos, key_valid)]
 
         def attn(layer, x_in, caches):
-            first = caches is None
-            ins = [x_in, ln_gain, ln_shift, w_qkv, b_qkv, w_out, write_slot, slot_col, key_pos, key_valid, k_in, v_in]
-            specs = [vm, vm, vm, hbm, vm, hbm, sm, vm, vm, vm, hbm, hbm]
+            first = layer == 0
+            small = [pltpu.VMEM(b_qkv.shape, BF16), pltpu.VMEM(key_pos.shape, jnp.int32), pltpu.VMEM(key_valid.shape, jnp.int32), pltpu.SMEM(write_slot.shape, jnp.int32)]
             alias = {}
-            if not first:
-                alias = {len(ins): 1, len(ins) + 1: 2}
-                ins += list(caches)
-                specs += [hbm, hbm]
-            shape = jax.ShapeDtypeStruct(flat, BF16)
+            part = jax.ShapeDtypeStruct((n_batch, width), F32)
+            if first:
+                ins = [in_hbm(x_in), in_hbm(ln_gain), in_hbm(ln_shift)] + shared + [k_in, v_in]
+                specs = [hbm] * len(ins)
+                small = [pltpu.VMEM(x_in.shape, BF16), pltpu.VMEM(ln_gain.shape, BF16), pltpu.VMEM(ln_shift.shape, BF16)] + small
+                outs, out_specs = (part, held, held), (vm, vm, vm)
+            else:
+                ins = [x_in] + shared + list(caches)
+                specs = [vm] + [hbm] * len(shared) + [vm] * 2
+                outs, out_specs = (part, shape, shape, held, held), (vm, hbm, hbm, vm, vm)
+                alias = {len(ins) - 2: 3, len(ins) - 1: 4}
             return pl.pallas_call(
                 functools.partial(attn_kernel, layer, n_local * tp_size, first),
-                out_shape=(jax.ShapeDtypeStruct((n_batch, width), F32), shape, shape),
+                out_shape=outs,
                 in_specs=specs,
-                out_specs=(vm, hbm, hbm),
-                scratch_shapes=[
+                out_specs=out_specs,
+                scratch_shapes=small + [
                     pltpu.VMEM(w_qkv.shape[1:], BF16),
                     pltpu.VMEM(w_out.shape[1:], BF16),
-                    pltpu.VMEM(flat[1:], BF16),
-                    pltpu.VMEM(flat[1:], BF16),
                     pltpu.VMEM((n_batch, b_qkv.shape[1]), F32),
-                    pltpu.VMEM((n_local, n_batch, n_cols), F32),
+                    pltpu.VMEM((2, n_batch, n_cols), F32),
                     pltpu.VMEM((n_batch, n_local * head_dim), F32),
                     pltpu.SemaphoreType.DMA((5,)),
-                    pltpu.SemaphoreType.DMA((2, n_groups)),
-                    pltpu.SemaphoreType.DMA((2,)),
+                    pltpu.SemaphoreType.DMA((7,)),
+                    pltpu.SemaphoreType.DMA((2, n_groups) if first else (4,)),
                 ],
                 input_output_aliases=alias,
-                compiler_params=pltpu.CompilerParams(vmem_limit_bytes=48 * MIB),
+                compiler_params=pltpu.CompilerParams(vmem_limit_bytes=14 * MIB),
                 name=f'attn_{layer}',
             )(*ins)
 
-        def reduce(layer, part, res):
+        def reduce(layer, part, res, caches=()):
             last = layer == n_layers - 1
             ins = [part, res, ln_gain, ln_shift, b_out, w_up, b_up, w_down, b_down]
             specs = [vm, vm, vm, vm, vm, hbm, vm, hbm, vm]
             outs = [jax.ShapeDtypeStruct((n_batch, width), BF16)]
             if not last:
-                outs.append(jax.ShapeDtypeStruct((blk, width), BF16))
+                ins += [k_in, v_in, *caches]
+                specs += [hbm, hbm, vm, vm]
+                outs += [jax.ShapeDtypeStruct((blk, width), BF16), held, held]
             dma = pltpu.SemaphoreType.DMA((2, n_chip))
             return pl.pallas_call(
                 functools.partial(reduce_kernel, layer, tp_size, last),
@@ -322,20 +369,18 @@
                     pltpu.VMEM((2, n_chip, blk, width), F32),
                     pltpu.VMEM((2, n_chip, blk, width), BF16),
                     pltpu.VMEM((2, n_chip, blk, width), BF16),
-                    pltpu.SemaphoreType.DMA((2,)),
+                    pltpu.SemaphoreType.DMA((4,)),
                 ] + [dma] * 8,
-                compiler_params=pltpu.CompilerParams(vmem_limit_bytes=32 * MIB, collective_id=layer, has_side_effects=True),
+                input_output_aliases={} if last else {len(ins) - 2: 2, len(ins) - 1: 3},
+                compiler_params=pltpu.CompilerParams(vmem_limit_bytes=14 * MIB, collective_id=layer, has_side_effects=True),
                 name=f'reduce_{layer}',
             )(*ins)
 
-        caches, x_in, res = None, x0, x0
-        for layer in range(n_layers):
-            part, k_new, v_new = attn(layer, x_in, caches)
-            caches = (k_new, v_new)
-            outs = reduce(layer, part, res)
-            x_in = outs[0]
-            res = outs[-1]
-        return x_in[:, None, :], caches[0].reshape(k_cache.shape), caches[1].reshape(v_cache.shape)
+        part, k_held, v_held = attn(0, x0, None)
+        h1, x1, k_held, v_held = reduce(0, part, x0, (k_held, v_held))
+        part, k_new, v_new = attn(1, h1, (k_held, v_held))[:3]
+        (x_last,) = reduce(1, part, x1)
+        return x_last[:, None, :], k_new.reshape(k_cache.shape), v_new.reshape(v_cache.shape)
 
     cache_spec = P(None, 'dp', None, 'tp', None)
     in_specs = (P('dp', None, None), P(), P(), P(None, None, 'tp'), P(None, 'tp'), P(None, 'tp', None), P(), P(None, None, 'tp'), P(None, 'tp'), P(None, 'tp', None), P(), cache_spec, cache_spec, P('dp'), P('dp', None), P('dp', None))

time: 93.7 us -> 86.7 us (0.925)
  local copies, waits for them, and re-layouts: 6.86 us -> 0.73 us
    unnamed x21 -> x13, local copies, waits for them, and re-layouts: 6.12 us -> 0.73 us
where the time goes in v2:
time: 86.7 us
  Pallas kernels  85.2 us (98%)
    pallas_call x2, Pallas kernels, reduce(): pl.pallas_call(functools.partial(reduce_kernel, layer, tp_size, last), ou...  56.3 us
    pallas_call x2, Pallas kernels, attn(): pl.pallas_call(functools.partial(attn_kernel, layer, n_local * tp_size, f...  28.9 us

profile of v2, /device:TPU:113, one launch (start us, length us, event | category | flops | bytes accessed | tf_op | source)
XLA Modules:
  0.0 86.7 jit_solution(4138202015455138742)
XLA Ops:
  0.6 0.0 copy-start
  0.6 0.0 copy-start.1
  0.7 0.0 copy-start.2
  0.7 0.0 copy-start.3
  0.7 0.0 copy-start.4
  0.7 0.0 copy-start.5
  0.7 15.8 %attn_0.1 = (f32[64,2048]{1,0:T(8,128)S(1)}, bf16[2,64,512,128]{3,2,1,0:T(8,128)(2,1)S(1)}, bf16[2,64,512,128]{3,2,1,0:T(8,128)(2,1)S(1)}) custom-call(bf16[64,2048]{1,0:T(8,128)(2,1)} %bitcast.6, bf16[2,2,2048]{2,1,0:T(2,128)(2,1)} %refs_2_.7, bf16[2,2,2048]{2,1,0:T(2,128)(2,1)} %refs_3_.7, bf16[2,768]{1,0:T(2,128)(2,1)} %refs_1_.3, ...), custom_call_target="tpu_custom_call" | custom-call | tf_op jit(solution)/shard_map/attn_0/pallas_call | solution.py:328
  16.5 0.0 copy-done
  16.5 0.0 copy-done.1
  16.5 0.0 copy-done.2
  16.5 0.0 copy-done.3
  16.5 0.0 copy-done.4
  16.5 0.0 copy-done.5
  16.5 29.5 %reduce_0.1 = (bf16[64,2048]{1,0:T(8,128)(2,1)S(1)}, bf16[8,2048]{1,0:T(8,128)(2,1)S(1)}, bf16[2,64,512,128]{3,2,1,0:T(8,128)(2,1)S(1)}, bf16[2,64,512,128]{3,2,1,0:T(8,128)(2,1)S(1)}) custom-call(f32[64,2048]{1,0:T(8,128)S(1)} %get-tuple-element.13.refs_0_, bf16[64,2048]{1,0:T(8,128)(2,1)S(1)} %bitcast.7, ...), custom_call_target="tpu_custom_call", output_to_operand_aliasing={{2}: (11, {}), {3}: (12, {})} | custom-call | tf_op jit(solution)/shard_map/reduce_0/pallas_call | solution.py:358
  46.0 13.1 %attn_1.1 = (f32[64,2048]{1,0:T(8,128)S(1)}, bf16[2,64,512,128]{3,2,1,0:T(8,128)(2,1)}, bf16[2,64,512,128]{3,2,1,0:T(8,128)(2,1)}, bf16[2,64,512,128]{3,2,1,0:T(8,128)(2,1)S(1)}, bf16[2,64,512,128]{3,2,1,0:T(8,128)(2,1)S(1)}) custom-call(bf16[64,2048]{1,0:T(8,128)(2,1)S(1)} %get-tuple-element.16.refs_0_, ...), custom_call_target="tpu_custom_call", output_to_operand_aliasing={{3}: (7, {}), {4}: (8, {})} | custom-call | tf_op jit(solution)/shard_map/attn_1/pallas_call | solution.py:328
  59.1 26.8 %reduce_1.1 = bf16[64,2048]{1,0:T(8,128)(2,1)S(1)} custom-call(f32[64,2048]{1,0:T(8,128)S(1)} %get-tuple-element.19.refs_0_, bf16[8,2048]{1,0:T(8,128)(2,1)S(1)} %get-tuple-element.20.refs_1_, bf16[2,2,2048]{2,1,0:T(2,128)(2,1)S(1)} %copy-done.1, bf16[2,2,2048]{2,1,0:T(2,128)(2,1)S(1)} %copy-done.2, bf16[2,2048]{1,0:T(2,128)(2,1)S(1)} %copy-done.3, ...), custom_call_target="tpu_custom_call" | custom-call | tf_op jit(solution)/shard_map/reduce_1/pallas_call | solution.py:358
  86.0 0.7 copy.28
Async XLA Ops:
  0.6 15.8 %copy-start = (bf16[64,1,2048]{2,0,1:T(8,128)(2,1)S(1)}, bf16[64,1,2048]{2,0,1:T(8,128)(2,1)}, u32[]{:S(2)}) copy-start(bf16[64,1,2048]{2,0,1:T(8,128)(2,1)} %param.16) | copy-start | bytes 786436
  0.6 15.8 %copy-start.1 = (bf16[2,2,2048]{2,1,0:T(2,128)(2,1)S(1)}, bf16[2,2,2048]{2,1,0:T(2,128)(2,1)}, u32[]{:S(2)}) copy-start(bf16[2,2,2048]{2,1,0:T(2,128)(2,1)} %refs_2_.7) | copy-start | bytes 49156
  0.7 15.8 %copy-start.2 = (bf16[2,2,2048]{2,1,0:T(2,128)(2,1)S(1)}, bf16[2,2,2048]{2,1,0:T(2,128)(2,1)}, u32[]{:S(2)}) copy-start(bf16[2,2,2048]{2,1,0:T(2,128)(2,1)} %refs_3_.7) | copy-start | bytes 49156
  0.7 15.8 %copy-start.3 = (bf16[2,2048]{1,0:T(2,128)(2,1)S(1)}, bf16[2,2048]{1,0:T(2,128)(2,1)}, u32[]{:S(2)}) copy-start(bf16[2,2048]{1,0:T(2,128)(2,1)} %refs_4_.7) | copy-start | bytes 24580
  0.7 15.8 %copy-start.4 = (bf16[2,2048]{1,0:T(2,128)(2,1)S(1)}, bf16[2,2048]{1,0:T(2,128)(2,1)}, u32[]{:S(2)}) copy-start(bf16[2,2048]{1,0:T(2,128)(2,1)} %refs_8_.5) | copy-start | bytes 24580
  0.7 15.8 %copy-start.5 = (bf16[2,1024]{1,0:T(2,128)(2,1)S(1)}, bf16[2,1024]{1,0:T(2,128)(2,1)}, u32[]{:S(2)}) copy-start(bf16[2,1024]{1,0:T(2,128)(2,1)} %refs_6_.7) | copy-start | bytes 12292

commit v3 on v2

--- a/solution.py
+++ b/solution.py
@@ -13,6 +13,7 @@
 F32 = jnp.float32
 BF16 = jnp.bfloat16
 GROUP = 8
+AHEAD = 3
 MIB = 2 ** 20
 
 
@@ -26,15 +27,15 @@
 
 def attn_kernel(layer, n_heads, first, *refs):
     if first:
-        (x_in_ref, gain_in, shift_in, bq_in, wq_hbm, wo_hbm, slot_hbm, pos_in, valid_in, k_hbm, v_hbm,
-         part_ref, kall, vall,
+        (x_in_ref, gain_in, shift_in, bq_in, wq_hbm, slot_hbm, pos_in, valid_in, k_hbm, v_hbm,
+         attn_ref, kall, vall,
          x_ref, gain_ref, shift_ref, bq_ref, pos_ref, valid_ref, slot_smem,
-         wq, wo, qkv, bias, attn, sem_w, sem_s, sem_in) = refs
-    else:
-        (x_ref, bq_in, wq_hbm, wo_hbm, slot_hbm, pos_in, valid_in, k_raw, v_raw,
-         part_ref, k_out, v_out, kall, vall,
+         wq, qkv, bias, attn, sem_w, sem_s, sem_in) = refs
+    else:
+        (x_ref, bq_in, wq_hbm, slot_hbm, pos_in, valid_in, k_raw, v_raw,
+         attn_ref, k_out, v_out, kall, vall,
          bq_ref, pos_ref, valid_ref, slot_smem,
-         wq, wo, qkv, bias, attn, sem_w, sem_s, sem_out) = refs
+         wq, qkv, bias, attn, sem_w, sem_s, sem_out) = refs
     kbuf, vbuf = kall.at[layer], vall.at[layer]
     n_batch, n_cols, head_dim = kbuf.shape
     n_groups = n_batch // GROUP
@@ -55,7 +56,6 @@
     ]
     for c in w_copies:
         c.start()
-    wo_copy = pltpu.make_async_copy(wo_hbm.at[layer], wo, sem_w.at[n_chunk])
 
     def in_copy(which, g):
         src, dst = ((k_hbm, kbuf), (v_hbm, vbuf))[which]
@@ -66,13 +66,10 @@
         return pltpu.make_async_copy(src.at[pl.ds(g * GROUP, GROUP)], dst.at[layer, pl.ds(g * GROUP, GROUP)], sem_out.at[which])
 
     if first:
-        for g in range(n_groups):
+        for g in range(AHEAD):
             in_copy(0, g).start()
             in_copy(1, g).start()
-        wo_copy.start()
-        old = []
-    else:
-        wo_copy.start()
+    else:
         old = [
             pltpu.make_async_copy(src.at[layer - 1, pl.ds(g * GROUP, GROUP)], dst.at[layer - 1, pl.ds(g * GROUP, GROUP)], sem_out.at[2 + i])
             for g in range(n_groups) for i, (src, dst) in enumerate(((kall, k_out), (vall, v_out)))
@@ -109,6 +106,11 @@
         if first:
             in_copy(0, g).wait()
             in_copy(1, g).wait()
+
+            @pl.when(g + AHEAD < n_groups)
+            def _():
+                in_copy(0, g + AHEAD).start()
+                in_copy(1, g + AHEAD).start()
         base = pl.multiple_of(g * GROUP, GROUP)
         row16 = lax.broadcasted_iota(jnp.int32, (16, head_dim), 0)
         fresh = qkv[pl.ds(base, GROUP), :]
@@ -134,23 +136,27 @@
             num = (jnp.full((GROUP, n_cols), 1 + h, jnp.int32) + head0).astype(F32)
             slope = jnp.exp2(-8.0 * num / n_heads)
             parts.append(jnp.where(jnp.logical_and(allowed, col % n_local == h), slope * pos_g, -jnp.inf))
-        q16 = jnp.concatenate(
-            [fresh[:, 3 * h * head_dim:(3 * h + 1) * head_dim] for h in range(n_local)], axis=0
-        ).astype(BF16)
-        row_s = lax.broadcasted_iota(jnp.int32, (rows, n_cols), 0) % GROUP
+        queries = jnp.concatenate([fresh[:, 3 * h * head_dim:(3 * h + 1) * head_dim] for h in range(n_local)], axis=0)
+        odd = lax.broadcasted_iota(jnp.int32, (rows, head_dim), 0) % 2 == 1
+        q_pair = jnp.concatenate([jnp.where(odd, 0.0, queries), jnp.where(odd, queries, 0.0)], axis=1).astype(BF16)
+        row_s = lax.broadcasted_iota(jnp.int32, (rows, n_cols), 0) % GROUP // 2
         s = None
-        for b in range(GROUP):
-            sb = lax.dot_general(q16, kbuf[base + b], (((1,), (1,)), ((), ())), preferred_element_type=F32)
-            s = sb if s is None else jnp.where(row_s == b, sb, s)
+        for b in range(0, GROUP, 2):
+            keys = jnp.concatenate([kbuf[base + b], kbuf[base + b + 1]], axis=1)
+            sb = lax.dot_general(q_pair, keys, (((1,), (1,)), ((), ())), preferred_element_type=F32)
+            s = sb if s is None else jnp.where(row_s == b // 2, sb, s)
         s = s * scale + jnp.concatenate(parts, axis=0)
         top = jnp.max(s, axis=-1, keepdims=True)
         e = jnp.exp(s - top)
         p = (e * (1.0 / jnp.sum(e, axis=-1, keepdims=True))).astype(BF16)
         row_o = lax.broadcasted_iota(jnp.int32, (rows, head_dim), 0) % GROUP
         o = None
-        for b in range(GROUP):
-            ob = jnp.dot(p, vbuf[base + b], preferred_element_type=F32)
-            o = ob if o is None else jnp.where(row_o == b, ob, o)
+        for b in range(0, GROUP, 2):
+            values = jnp.concatenate([vbuf[base + b], vbuf[base + b + 1]], axis=1)
+            ob = jnp.dot(p, values, preferred_element_type=F32)
+            for i in range(2):
+                oi = ob[:, i * head_dim:(i + 1) * head_dim]
+                o = oi if o is None else jnp.where(row_o == b + i, oi, o)
         for h in range(n_local):
             attn[pl.ds(base, GROUP), h * head_dim:(h + 1) * head_dim] = o[h * GROUP:(h + 1) * GROUP]
         if not first:
@@ -159,8 +165,7 @@
         return carry
 
     lax.fori_loop(0, n_groups, group, 0)
-    wo_copy.wait()
-    part_ref[...] = jnp.dot(attn[...].astype(BF16), wo[...], preferred_element_type=F32)
+    attn_ref[...] = attn[...].astype(BF16)
     if not first:
         for c in old:
             c.wait()
@@ -170,14 +175,14 @@
 
 
 def reduce_kernel(layer, n_tp, last, *refs):
+    (attn_ref, wo_hbm, res_ref, gain_ref, shift_ref, bo_ref, wu_hbm, bu_ref, wd_hbm, bd_ref) = refs[:10]
     if last:
-        part_ref, res_ref, gain_ref, shift_ref, bo_ref, wu_hbm, bu_ref, wd_hbm, bd_ref, out_ref = refs[:10]
-        rest = refs[10:]
-    else:
-        (part_ref, res_ref, gain_ref, shift_ref, bo_ref, wu_hbm, bu_ref, wd_hbm, bd_ref, k_hbm, v_hbm, k_raw, v_raw,
-         out_ref, own_ref, kall, vall) = refs[:17]
-        rest = refs[17:]
-    (wu, wd, part2, d2d, mid, got, gath, gath2, sem_w, pair_s, pair_r, chip_s, chip_r, ag_s, ag_r, agp_s, agp_r) = rest
+        out_ref, rest = refs[10], refs[11:]
+    else:
+        (k_hbm, v_hbm, k_raw, v_raw, out_ref, own_ref, kall, vall) = refs[10:18]
+        rest = refs[18:]
+    (wo, wu, wd, part_ref, part2, d2d, mid, got, gath, gath2, sem_w,
+     pair_s, pair_r, chip_s, chip_r, ag_s, ag_r, agp_s, agp_r) = rest
     n_batch, width = part_ref.shape
     n_chip = n_tp // 2
     blk = n_batch // n_tp
@@ -189,6 +194,8 @@
     def chip(d):
         return lax.rem(x + d, n_chip)
 
+    wo_copy = pltpu.make_async_copy(wo_hbm.at[layer], wo, sem_w.at[4])
+    wo_copy.start()
     w_copies = [pltpu.make_async_copy(wu_hbm.at[layer], wu, sem_w.at[0]), pltpu.make_async_copy(wd_hbm.at[layer], wd, sem_w.at[1])]
     if not last:
         w_copies.append(pltpu.make_async_copy(k_hbm.at[layer + 1], kall.at[layer + 1], sem_w.at[2]))
@@ -196,9 +203,11 @@
     for w in w_copies:
         w.start()
     barrier = pltpu.get_barrier_semaphore()
-    peers = [partner] + [chip(d) * 2 + c for d in range(1, n_chip)]
+    peers = [partner] + [chip(d) * 2 + 1 - c for d in range(1, n_chip)]
     for peer in peers:
         pl.semaphore_signal(barrier, inc=1, device_id={'tp': peer}, device_id_type=MESH)
+    wo_copy.wait()
+    part_ref[...] = jnp.dot(attn_ref[...], wo[...], preferred_element_type=F32)
     pl.semaphore_wait(barrier, len(peers))
 
     order = [2, 1, 3, 0] if n_chip == 4 else list(range(1, n_chip)) + [0]
@@ -216,40 +225,36 @@
         for d in order:
             pair[d].start()
         hops = {}
-        acc = None
         for d in order:
             pair[d].wait_recv()
-            both = src[rows_of(c, d), :] + d2d[phase, d]
-            if d == 0:
-                acc = both
-            else:
-                mid[phase, d] = both
-                hops[d] = pltpu.make_async_remote_copy(
-                    src_ref=mid.at[phase, d], dst_ref=got.at[phase, d], send_sem=chip_s.at[phase, d],
-                    recv_sem=chip_r.at[phase, d], device_id={'tp': chip(d) * 2 + c}, device_id_type=MESH)
-                hops[d].start()
+            mid[phase, d] = src[rows_of(c, d), :] + d2d[phase, d]
+            hops[d] = pltpu.make_async_remote_copy(
+                src_ref=mid.at[phase, d], dst_ref=got.at[phase, d], send_sem=chip_s.at[phase, d],
+                recv_sem=chip_r.at[phase, d], device_id={'tp': chip(d) * 2 + 1 - c}, device_id_type=MESH)
+            hops[d].start()
+        acc = None
         for d in sorted(hops, key=lambda d: min(d, n_chip - d)):
             hops[d].wait_recv()
-            acc = acc + got[phase, d]
+            acc = got[phase, d] if acc is None else acc + got[phase, d]
         for d in order:
             pair[d].wait_send()
-            if d:
-                hops[d].wait_send()
+            hops[d].wait_send()
         return acc
 
     def all_gather(phase, buf, value):
-        buf[c, x] = value
+        buf[1 - c, x] = value
         hops = {}
         for d in order[:-1]:
             hops[d] = pltpu.make_async_remote_copy(
-                src_ref=buf.at[c, x], dst_ref=buf.at[c, x], send_sem=ag_s.at[phase, d], recv_sem=ag_r.at[phase, d],
-                device_id={'tp': chip(d) * 2 + c}, device_id_type=MESH)
+                src_ref=buf.at[1 - c, x], dst_ref=buf.at[1 - c, x], send_sem=ag_s.at[phase, d], recv_sem=ag_r.at[phase, d],
+                device_id={'tp': chip(d) * 2 + 1 - c}, device_id_type=MESH)
             hops[d].start()
 
         def pass_on(d):
             slot = lax.rem(x + n_chip - d, n_chip)
+            half = 1 - c if d == 0 else c
             cp = pltpu.make_async_remote_copy(
-                src_ref=buf.at[c, slot], dst_ref=buf.at[c, slot], send_sem=agp_s.at[phase, d], recv_sem=agp_r.at[phase, d],
+                src_ref=buf.at[half, slot], dst_ref=buf.at[half, slot], send_sem=agp_s.at[phase, d], recv_sem=agp_r.at[phase, d],
                 device_id={'tp': partner}, device_id_type=MESH)
             cp.start()
             return cp
@@ -267,7 +272,7 @@
     if last:
         res = res_ref[...].astype(F32)
     else:
-        res = res_ref[rows_of(c, 0), :].astype(F32)
+        res = res_ref[rows_of(1 - c, 0), :].astype(F32)
     total = reduce_scatter(0, part_ref)
     x_mid = (res + total + bo_ref[layer:layer + 1].astype(F32)).astype(BF16).astype(F32)
     normed = all_gather(0, gath, layer_norm_f32(x_mid, gain_ref[layer, 1:2], shift_ref[layer, 1:2])).astype(BF16)
@@ -284,8 +289,8 @@
         own_ref[...] = x_next
         nxt = layer_norm_f32(x_next.astype(F32), gain_ref[layer + 1, 0:1], shift_ref[layer + 1, 0:1])
         out_ref[...] = all_gather(1, gath2, nxt).astype(BF16)
-        w_copies[2].wait()
-        w_copies[3].wait()
+        for w in w_copies[2:]:
+            w.wait()
 
 
 def solution(mesh):
@@ -308,47 +313,46 @@
         n_chip = tp_size // 2
         shape = jax.ShapeDtypeStruct(flat, BF16)
         held = pltpu.VMEM(flat, BF16)
-        shared = [in_hbm(a) for a in (b_qkv, w_qkv, w_out, write_slot, key_pos, key_valid)]
+        shared = [in_hbm(a) for a in (write_slot, key_pos, key_valid)]
 
         def attn(layer, x_in, caches):
             first = layer == 0
             small = [pltpu.VMEM(b_qkv.shape, BF16), pltpu.VMEM(key_pos.shape, jnp.int32), pltpu.VMEM(key_valid.shape, jnp.int32), pltpu.SMEM(write_slot.shape, jnp.int32)]
+            work = [
+                pltpu.VMEM(w_qkv.shape[1:], BF16),
+                pltpu.VMEM((n_batch, b_qkv.shape[1]), F32),
+                pltpu.VMEM((2, n_batch, n_cols), F32),
+                pltpu.VMEM((n_batch, n_local * head_dim), F32),
+            ]
             alias = {}
-            part = jax.ShapeDtypeStruct((n_batch, width), F32)
+            mixed = jax.ShapeDtypeStruct((n_batch, n_local * head_dim), BF16)
             if first:
-                ins = [in_hbm(x_in), in_hbm(ln_gain), in_hbm(ln_shift)] + shared + [k_in, v_in]
+                ins = [in_hbm(x_in), in_hbm(ln_gain), in_hbm(ln_shift), in_hbm(b_qkv), w_qkv] + shared + [k_in, v_in]
                 specs = [hbm] * len(ins)
                 small = [pltpu.VMEM(x_in.shape, BF16), pltpu.VMEM(ln_gain.shape, BF16), pltpu.VMEM(ln_shift.shape, BF16)] + small
-                outs, out_specs = (part, held, held), (vm, vm, vm)
+                outs, out_specs = (mixed, held, held), (vm, vm, vm)
+                scratch = small + work + [pltpu.SemaphoreType.DMA((5,)), pltpu.SemaphoreType.DMA((7,)), pltpu.SemaphoreType.DMA((2, n_groups))]
             else:
-                ins = [x_in] + shared + list(caches)
-                specs = [vm] + [hbm] * len(shared) + [vm] * 2
-                outs, out_specs = (part, shape, shape, held, held), (vm, hbm, hbm, vm, vm)
+                ins = [x_in, in_hbm(b_qkv), w_qkv] + shared + list(caches)
+                specs = [vm, hbm, hbm] + [hbm] * len(shared) + [vm] * 2
+                outs, out_specs = (mixed, shape, shape, held, held), (vm, hbm, hbm, vm, vm)
                 alias = {len(ins) - 2: 3, len(ins) - 1: 4}
+                scratch = small + work + [pltpu.SemaphoreType.DMA((5,)), pltpu.SemaphoreType.DMA((7,)), pltpu.SemaphoreType.DMA((4,))]
             return pl.pallas_call(
                 functools.partial(attn_kernel, layer, n_local * tp_size, first),
                 out_shape=outs,
                 in_specs=specs,
                 out_specs=out_specs,
-                scratch_shapes=small + [
-                    pltpu.VMEM(w_qkv.shape[1:], BF16),
-                    pltpu.VMEM(w_out.shape[1:], BF16),
-                    pltpu.VMEM((n_batch, b_qkv.shape[1]), F32),
-                    pltpu.VMEM((2, n_batch, n_cols), F32),
-                    pltpu.VMEM((n_batch, n_local * head_dim), F32),
-                    pltpu.SemaphoreType.DMA((5,)),
-                    pltpu.SemaphoreType.DMA((7,)),
-                    pltpu.SemaphoreType.DMA((2, n_groups) if first else (4,)),
-                ],
+                scratch_shapes=scratch,
                 input_output_aliases=alias,
                 compiler_params=pltpu.CompilerParams(vmem_limit_bytes=14 * MIB),
                 name=f'attn_{layer}',
             )(*ins)
 
-        def reduce(layer, part, res, caches=()):
+        def reduce(layer, mixed, res, caches=()):
             last = layer == n_layers - 1
-            ins = [part, res, ln_gain, ln_shift, b_out, w_up, b_up, w_down, b_down]
-            specs = [vm, vm, vm, vm, vm, hbm, vm, hbm, vm]
+            ins = [mixed, w_out, res, ln_gain, ln_shift, b_out, w_up, b_up, w_down, b_down]
+            specs = [vm, hbm, vm, vm, vm, vm, hbm, vm, hbm, vm]
             outs = [jax.ShapeDtypeStruct((n_batch, width), BF16)]
             if not last:
                 ins += [k_in, v_in, *caches]
@@ -361,25 +365,27 @@
                 in_specs=specs,
                 out_specs=tuple([vm] * len(outs)),
                 scratch_shapes=[
+                    pltpu.VMEM(w_out.shape[1:], BF16),
                     pltpu.VMEM(w_up.shape[1:], BF16),
                     pltpu.VMEM(w_down.shape[1:], BF16),
+                    pltpu.VMEM((n_batch, width), F32),
                     pltpu.VMEM((n_batch, width), F32),
                     pltpu.VMEM((2, n_chip, blk, width), F32),
                     pltpu.VMEM((2, n_chip, blk, width), F32),
                     pltpu.VMEM((2, n_chip, blk, width), F32),
                     pltpu.VMEM((2, n_chip, blk, width), BF16),
                     pltpu.VMEM((2, n_chip, blk, width), BF16),
-                    pltpu.SemaphoreType.DMA((4,)),
+                    pltpu.SemaphoreType.DMA((6,)),
                 ] + [dma] * 8,
                 input_output_aliases={} if last else {len(ins) - 2: 2, len(ins) - 1: 3},
                 compiler_params=pltpu.CompilerParams(vmem_limit_bytes=14 * MIB, collective_id=layer, has_side_effects=True),
                 name=f'reduce_{layer}',
             )(*ins)
 
-        part, k_held, v_held = attn(0, x0, None)
-        h1, x1, k_held, v_held = reduce(0, part, x0, (k_held, v_held))
-        part, k_new, v_new = attn(1, h1, (k_held, v_held))[:3]
-        (x_last,) = reduce(1, part, x1)
+        mixed, k_held, v_held = attn(0, x0, None)
+        h1, x1, k_held, v_held = reduce(0, mixed, x0, (k_held, v_held))
+        mixed, k_new, v_new = attn(1, h1, (k_held, v_held))[:3]
+        (x_last,) = reduce(1, mixed, x1)
         return x_last[:, None, :], k_new.reshape(k_cache.shape), v_new.reshape(v_cache.shape)
 
     cache_spec = P(None, 'dp', None, 'tp', None)

time: 86.7 us -> 80.4 us (0.927)
  Pallas kernels: 85.2 us -> 78.8 us
    pallas_call x2, Pallas kernels: 28.9 us -> 23.7 us  [attn(): pl.pallas_call(functools.partial(attn_kernel, layer, n_local * tp_size, f...]
    pallas_call x2, Pallas kernels: 56.3 us -> 55.1 us  [reduce(): pl.pallas_call(functools.partial(reduce_kernel, layer, tp_size, last), ou...]
where the time goes in v3:
time: 80.4 us; the launch traced here: 80.3 us
  Pallas kernels  78.8 us (98%)
    pallas_call x2, Pallas kernels, reduce(): pl.pallas_call(functools.partial(reduce_kernel, layer, tp_size, last), ou...  55.1 us
    pallas_call x2, Pallas kernels, attn(): pl.pallas_call(functools.partial(attn_kernel, layer, n_local * tp_size, f...  23.7 us

profile of v3, /device:TPU:113, one launch (start us, length us, event | category | flops | bytes accessed | tf_op | source)
XLA Modules:
  0.0 80.3 jit_solution(819764727136579248)
XLA Ops:
  0.6 0.0 copy-start
  0.6 0.0 copy-start.1
  0.7 0.0 copy-start.2
  0.7 0.0 copy-start.3
  0.7 0.0 copy-start.4
  0.7 0.0 copy-start.5
  0.7 11.3 %attn_0.1 = (bf16[64,256]{1,0:T(8,128)(2,1)S(1)}, bf16[2,64,512,128]{3,2,1,0:T(8,128)(2,1)S(1)}, bf16[2,64,512,128]{3,2,1,0:T(8,128)(2,1)S(1)}) custom-call(bf16[64,2048]{1,0:T(8,128)(2,1)} %bitcast.6, bf16[2,2,2048]{2,1,0:T(2,128)(2,1)} %refs_3_.7, bf16[2,2,2048]{2,1,0:T(2,128)(2,1)} %refs_4_.7, bf16[2,768]{1,0:T(2,128)(2,1)} %refs_1_.6, ...), custom_call_target="tpu_custom_call" | custom-call | tf_op jit(solution)/shard_map/attn_0/pallas_call | solution.py:341
  12.0 0.0 copy-done
  12.0 0.0 copy-done.1
  12.0 0.0 copy-done.2
  12.0 0.0 copy-done.3
  12.1 0.0 copy-done.4
  12.1 0.0 copy-done.5
  12.1 28.9 %reduce_0.1 = (bf16[64,2048]{1,0:T(8,128)(2,1)S(1)}, bf16[8,2048]{1,0:T(8,128)(2,1)S(1)}, bf16[2,64,512,128]{3,2,1,0:T(8,128)(2,1)S(1)}, bf16[2,64,512,128]{3,2,1,0:T(8,128)(2,1)S(1)}) custom-call(bf16[64,256]{1,0:T(8,128)(2,1)S(1)} %get-tuple-element.13.refs_0_, bf16[2,256,2048]{2,1,0:T(8,128)(2,1)} %refs_1_.7, ...), custom_call_target="tpu_custom_call", output_to_operand_aliasing={{2}: (12, {}), {3}: (13, {})} | custom-call | tf_op jit(solution)/shard_map/reduce_0/pallas_call | solution.py:362
  40.9 12.4 %attn_1.1 = (bf16[64,256]{1,0:T(8,128)(2,1)S(1)}, bf16[2,64,512,128]{3,2,1,0:T(8,128)(2,1)}, bf16[2,64,512,128]{3,2,1,0:T(8,128)(2,1)}, bf16[2,64,512,128]{3,2,1...) custom-call(bf16[64,2048]{1,0:T(8,128)(2,1)S(1)} %get-tuple-element.16.refs_0_, ...), custom_call_target="tpu_custom_call", output_to_operand_aliasing={{3}: (6, {}), {4}: (7, {})} | custom-call | tf_op jit(solution)/shard_map/attn_1/pallas_call | solution.py:341
  53.3 26.3 %reduce_1.1 = bf16[64,2048]{1,0:T(8,128)(2,1)S(1)} custom-call(bf16[64,256]{1,0:T(8,128)(2,1)S(1)} %get-tuple-element.19.refs_0_, bf16[2,256,2048]{2,1,0:T(8,128)(2,1)} %refs_1_.7, bf16[8,2048]{1,0:T(8,128)(2,1)S(1)} %get-tuple-element.20.refs_2_, bf16[2,2,2048]{2,1,0:T(2,128)(2,1)S(1)} %copy-done.1, bf16[2,2,2048]{2,1,0:T(2,128)(2,1)S(1)} %copy-done.2, ...), custom_call_target="tpu_custom_call" | custom-call | tf_op jit(solution)/shard_map/reduce_1/pallas_call | solution.py:362
  79.6 0.7 copy.28
Async XLA Ops:
  0.6 11.4 %copy-start = (bf16[64,1,2048]{2,0,1:T(8,128)(2,1)S(1)}, bf16[64,1,2048]{2,0,1:T(8,128)(2,1)}, u32[]{:S(2)}) copy-start(bf16[64,1,2048]{2,0,1:T(8,128)(2,1)} %param.16) | copy-start | bytes 786436
  0.6 11.4 %copy-start.1 = (bf16[2,2,2048]{2,1,0:T(2,128)(2,1)S(1)}, bf16[2,2,2048]{2,1,0:T(2,128)(2,1)}, u32[]{:S(2)}) copy-start(bf16[2,2,2048]{2,1,0:T(2,128)(2,1)} %refs_3_.7) | copy-start | bytes 49156
  0.7 11.4 %copy-start.2 = (bf16[2,2,2048]{2,1,0:T(2,128)(2,1)S(1)}, bf16[2,2,2048]{2,1,0:T(2,128)(2,1)}, u32[]{:S(2)}) copy-start(bf16[2,2,2048]{2,1,0:T(2,128)(2,1)} %refs_4_.7) | copy-start | bytes 49156
  0.7 11.4 %copy-start.3 = (bf16[2,2048]{1,0:T(2,128)(2,1)S(1)}, bf16[2,2048]{1,0:T(2,128)(2,1)}, u32[]{:S(2)}) copy-start(bf16[2,2048]{1,0:T(2,128)(2,1)} %refs_5_.7) | copy-start | bytes 24580
  0.7 11.4 %copy-start.4 = (bf16[2,2048]{1,0:T(2,128)(2,1)S(1)}, bf16[2,2048]{1,0:T(2,128)(2,1)}, u32[]{:S(2)}) copy-start(bf16[2,2048]{1,0:T(2,128)(2,1)} %refs_9_.3) | copy-start | bytes 24580
  0.7 11.4 %copy-start.5 = (bf16[2,1024]{1,0:T(2,128)(2,1)S(1)}, bf16[2,1024]{1,0:T(2,128)(2,1)}, u32[]{:S(2)}) copy-start(bf16[2,1024]{1,0:T(2,128)(2,1)} %refs_7_.5) | copy-start | bytes 12292

commit v4 on v3

--- a/solution.py
+++ b/solution.py
@@ -13,7 +13,7 @@
 F32 = jnp.float32
 BF16 = jnp.bfloat16
 GROUP = 8
-AHEAD = 3
+AHEAD = 6
 MIB = 2 ** 20
 
 
@@ -27,35 +27,35 @@
 
 def attn_kernel(layer, n_heads, first, *refs):
     if first:
-        (x_in_ref, gain_in, shift_in, bq_in, wq_hbm, slot_hbm, pos_in, valid_in, k_hbm, v_hbm,
-         attn_ref, kall, vall,
-         x_ref, gain_ref, shift_ref, bq_ref, pos_ref, valid_ref, slot_smem,
-         wq, qkv, bias, attn, sem_w, sem_s, sem_in) = refs
+        (x_in_ref, gain_in, shift_in, bq_in, wq_hbm, wo_hbm, slot_hbm, pos_in, valid_in, k_hbm, v_hbm,
+         part_ref, kall, vall,
+         pos_ref, valid_ref, slot_smem, wo, bias, attn, sem_w, sem_s,
+         x_ref, gain_ref, shift_ref, bq_ref, wq, qkv, sem_in) = refs
     else:
-        (x_ref, bq_in, wq_hbm, slot_hbm, pos_in, valid_in, k_raw, v_raw,
-         attn_ref, k_out, v_out, kall, vall,
-         bq_ref, pos_ref, valid_ref, slot_smem,
-         wq, qkv, bias, attn, sem_w, sem_s, sem_out) = refs
+        (qkv, wo_hbm, slot_hbm, pos_in, valid_in, k_raw, v_raw,
+         part_ref, k_out, v_out, kall, vall,
+         pos_ref, valid_ref, slot_smem, wo, bias, attn, sem_w, sem_s, sem_out) = refs
     kbuf, vbuf = kall.at[layer], vall.at[layer]
     n_batch, n_cols, head_dim = kbuf.shape
     n_groups = n_batch // GROUP
     n_local = attn.shape[1] // head_dim
-    width = x_ref.shape[1]
     cache_len = n_cols // n_local
     n_chunk = 4
-    step = width // n_chunk
-    pairs = [(slot_hbm, slot_smem), (pos_in, pos_ref), (valid_in, valid_ref), (bq_in, bq_ref)]
+    pairs = [(slot_hbm, slot_smem), (pos_in, pos_ref), (valid_in, valid_ref)]
     if first:
-        pairs = [(x_in_ref, x_ref), (gain_in, gain_ref), (shift_in, shift_ref)] + pairs
+        pairs = [(x_in_ref, x_ref), (gain_in, gain_ref), (shift_in, shift_ref), (bq_in, bq_ref)] + pairs
     small = [pltpu.make_async_copy(src, dst, sem_s.at[i]) for i, (src, dst) in enumerate(pairs)]
     for c in small:
         c.start()
-    w_copies = [
-        pltpu.make_async_copy(wq_hbm.at[layer, pl.ds(i * step, step)], wq.at[pl.ds(i * step, step)], sem_w.at[i])
-        for i in range(n_chunk)
-    ]
-    for c in w_copies:
-        c.start()
+    wo_copy = pltpu.make_async_copy(wo_hbm.at[layer], wo, sem_w.at[n_chunk])
+    if first:
+        step = x_ref.shape[1] // n_chunk
+        w_copies = [
+            pltpu.make_async_copy(wq_hbm.at[layer, pl.ds(i * step, step)], wq.at[pl.ds(i * step, step)], sem_w.at[i])
+            for i in range(n_chunk)
+        ]
+        for c in w_copies:
+            c.start()
 
     def in_copy(which, g):
         src, dst = ((k_hbm, kbuf), (v_hbm, vbuf))[which]
@@ -66,10 +66,11 @@
         return pltpu.make_async_copy(src.at[pl.ds(g * GROUP, GROUP)], dst.at[layer, pl.ds(g * GROUP, GROUP)], sem_out.at[which])
 
     if first:
-        for g in range(AHEAD):
+        for g in range(AHEAD - n_chunk):
             in_copy(0, g).start()
             in_copy(1, g).start()
     else:
+        wo_copy.start()
         old = [
             pltpu.make_async_copy(src.at[layer - 1, pl.ds(g * GROUP, GROUP)], dst.at[layer - 1, pl.ds(g * GROUP, GROUP)], sem_out.at[2 + i])
             for g in range(n_groups) for i, (src, dst) in enumerate(((kall, k_out), (vall, v_out)))
@@ -89,14 +90,14 @@
 
     if first:
         x_in = layer_norm_f32(x_ref[...].astype(F32), gain_ref[layer, 0:1], shift_ref[layer, 0:1])
-    else:
-        x_in = x_ref[...]
-    acc = None
-    for i in range(n_chunk):
-        w_copies[i].wait()
-        d = jnp.dot(x_in[:, i * step:(i + 1) * step], wq[i * step:(i + 1) * step], preferred_element_type=F32)
-        acc = d if acc is None else acc + d
-    qkv[...] = (acc + bq_ref[layer:layer + 1].astype(F32)).astype(BF16).astype(F32)
+        acc = None
+        for i in range(n_chunk):
+            w_copies[i].wait()
+            in_copy(0, AHEAD - n_chunk + i).start()
+            in_copy(1, AHEAD - n_chunk + i).start()
+            d = jnp.dot(x_in[:, i * step:(i + 1) * step], wq[i * step:(i + 1) * step], preferred_element_type=F32)
+            acc = d if acc is None else acc + d
+        qkv[...] = (acc + bq_ref[layer:layer + 1].astype(F32)).astype(BF16).astype(F32)
 
     scale = 1.0 / math.sqrt(head_dim)
     rows = n_local * GROUP
@@ -111,6 +112,10 @@
             def _():
                 in_copy(0, g + AHEAD).start()
                 in_copy(1, g + AHEAD).start()
+
+            @pl.when(g + AHEAD == n_groups)
+            def _():
+                wo_copy.start()
         base = pl.multiple_of(g * GROUP, GROUP)
         row16 = lax.broadcasted_iota(jnp.int32, (16, head_dim), 0)
         fresh = qkv[pl.ds(base, GROUP), :]
@@ -165,7 +170,8 @@
         return carry
 
     lax.fori_loop(0, n_groups, group, 0)
-    attn_ref[...] = attn[...].astype(BF16)
+    wo_copy.wait()
+    part_ref[...] = jnp.dot(attn[...].astype(BF16), wo[...], preferred_element_type=F32)
     if not first:
         for c in old:
             c.wait()
@@ -175,13 +181,13 @@
 
 
 def reduce_kernel(layer, n_tp, last, *refs):
-    (attn_ref, wo_hbm, res_ref, gain_ref, shift_ref, bo_ref, wu_hbm, bu_ref, wd_hbm, bd_ref) = refs[:10]
+    (part_ref, res_ref, gain_ref, shift_ref, bo_ref, wu_hbm, bu_ref, wd_hbm, bd_ref) = refs[:9]
     if last:
-        out_ref, rest = refs[10], refs[11:]
+        out_ref, rest = refs[9], refs[10:]
     else:
-        (k_hbm, v_hbm, k_raw, v_raw, out_ref, own_ref, kall, vall) = refs[10:18]
-        rest = refs[18:]
-    (wo, wu, wd, part_ref, part2, d2d, mid, got, gath, gath2, sem_w,
+        (k_hbm, v_hbm, wq_hbm, bq_ref, k_raw, v_raw, out_ref, own_ref, kall, vall) = refs[9:19]
+        rest = refs[19:]
+    (wu, wd, part2, d2d, mid, got, gath, gath2, sem_w,
      pair_s, pair_r, chip_s, chip_r, ag_s, ag_r, agp_s, agp_r) = rest
     n_batch, width = part_ref.shape
     n_chip = n_tp // 2
@@ -194,20 +200,19 @@
     def chip(d):
         return lax.rem(x + d, n_chip)
 
-    wo_copy = pltpu.make_async_copy(wo_hbm.at[layer], wo, sem_w.at[4])
-    wo_copy.start()
     w_copies = [pltpu.make_async_copy(wu_hbm.at[layer], wu, sem_w.at[0]), pltpu.make_async_copy(wd_hbm.at[layer], wd, sem_w.at[1])]
     if not last:
         w_copies.append(pltpu.make_async_copy(k_hbm.at[layer + 1], kall.at[layer + 1], sem_w.at[2]))
         w_copies.append(pltpu.make_async_copy(v_hbm.at[layer + 1], vall.at[layer + 1], sem_w.at[3]))
-    for w in w_copies:
-        w.start()
+        n_qkv = bq_ref.shape[1]
+        wq = wu.at[:, pl.ds(0, n_qkv)]
+        wq_copy = pltpu.make_async_copy(wq_hbm.at[layer + 1], wq, sem_w.at[4])
     barrier = pltpu.get_barrier_semaphore()
     peers = [partner] + [chip(d) * 2 + 1 - c for d in range(1, n_chip)]
     for peer in peers:
         pl.semaphore_signal(barrier, inc=1, device_id={'tp': peer}, device_id_type=MESH)
-    wo_copy.wait()
-    part_ref[...] = jnp.dot(attn_ref[...], wo[...], preferred_element_type=F32)
+    for w in w_copies:
+        w.start()
     pl.semaphore_wait(barrier, len(peers))
 
     order = [2, 1, 3, 0] if n_chip == 4 else list(range(1, n_chip)) + [0]
@@ -279,6 +284,8 @@
     w_copies[0].wait()
     up = jnp.dot(normed, wu[...], preferred_element_type=F32) + bu_ref[layer:layer + 1].astype(F32)
     act = jax.nn.gelu(up, approximate=True).astype(BF16)
+    if not last:
+        wq_copy.start()
     w_copies[1].wait()
     part2[...] = jnp.dot(act, wd[...], preferred_element_type=F32)
     total = reduce_scatter(1, part2)
@@ -288,7 +295,10 @@
     else:
         own_ref[...] = x_next
         nxt = layer_norm_f32(x_next.astype(F32), gain_ref[layer + 1, 0:1], shift_ref[layer + 1, 0:1])
-        out_ref[...] = all_gather(1, gath2, nxt).astype(BF16)
+        normed = all_gather(1, gath2, nxt).astype(BF16)
+        wq_copy.wait()
+        qkv = jnp.dot(normed, wu[:, :n_qkv], preferred_element_type=F32) + bq_ref[layer + 1:layer + 2].astype(F32)
+        out_ref[...] = qkv.astype(BF16).astype(F32)
         for w in w_copies[2:]:
             w.wait()
 
@@ -317,27 +327,38 @@
 
         def attn(layer, x_in, caches):
             first = layer == 0
-            small = [pltpu.VMEM(b_qkv.shape, BF16), pltpu.VMEM(key_pos.shape, jnp.int32), pltpu.VMEM(key_valid.shape, jnp.int32), pltpu.SMEM(write_slot.shape, jnp.int32)]
-            work = [
-                pltpu.VMEM(w_qkv.shape[1:], BF16),
-                pltpu.VMEM((n_batch, b_qkv.shape[1]), F32),
+            n_qkv = b_qkv.shape[1]
+            scratch = [
+                pltpu.VMEM(key_pos.shape, jnp.int32),
+                pltpu.VMEM(key_valid.shape, jnp.int32),
+                pltpu.SMEM(write_slot.shape, jnp.int32),
+                pltpu.VMEM(w_out.shape[1:], BF16),
                 pltpu.VMEM((2, n_batch, n_cols), F32),
                 pltpu.VMEM((n_batch, n_local * head_dim), F32),
+                pltpu.SemaphoreType.DMA((5,)),
+                pltpu.SemaphoreType.DMA((7,)),
             ]
             alias = {}
-            mixed = jax.ShapeDtypeStruct((n_batch, n_local * head_dim), BF16)
+            part = jax.ShapeDtypeStruct((n_batch, width), F32)
             if first:
-                ins = [in_hbm(x_in), in_hbm(ln_gain), in_hbm(ln_shift), in_hbm(b_qkv), w_qkv] + shared + [k_in, v_in]
+                ins = [in_hbm(a) for a in (x_in, ln_gain, ln_shift, b_qkv)] + [w_qkv, w_out] + shared + [k_in, v_in]
                 specs = [hbm] * len(ins)
-                small = [pltpu.VMEM(x_in.shape, BF16), pltpu.VMEM(ln_gain.shape, BF16), pltpu.VMEM(ln_shift.shape, BF16)] + small
-                outs, out_specs = (mixed, held, held), (vm, vm, vm)
-                scratch = small + work + [pltpu.SemaphoreType.DMA((5,)), pltpu.SemaphoreType.DMA((7,)), pltpu.SemaphoreType.DMA((2, n_groups))]
+                outs, out_specs = (part, held, held), (vm, vm, vm)
+                scratch += [
+                    pltpu.VMEM(x_in.shape, BF16),
+                    pltpu.VMEM(ln_gain.shape, BF16),
+                    pltpu.VMEM(ln_shift.shape, BF16),
+                    pltpu.VMEM(b_qkv.shape, BF16),
+                    pltpu.VMEM(w_qkv.shape[1:], BF16),
+                    pltpu.VMEM((n_batch, n_qkv), F32),
+                    pltpu.SemaphoreType.DMA((2, n_groups)),
+                ]
             else:
-                ins = [x_in, in_hbm(b_qkv), w_qkv] + shared + list(caches)
-                specs = [vm, hbm, hbm] + [hbm] * len(shared) + [vm] * 2
-                outs, out_specs = (mixed, shape, shape, held, held), (vm, hbm, hbm, vm, vm)
+                ins = [x_in, w_out] + shared + list(caches)
+                specs = [vm, hbm] + [hbm] * len(shared) + [vm] * 2
+                outs, out_specs = (part, shape, shape, held, held), (vm, hbm, hbm, vm, vm)
                 alias = {len(ins) - 2: 3, len(ins) - 1: 4}
-                scratch = small + work + [pltpu.SemaphoreType.DMA((5,)), pltpu.SemaphoreType.DMA((7,)), pltpu.SemaphoreType.DMA((4,))]
+                scratch += [pltpu.SemaphoreType.DMA((4,))]
             return pl.pallas_call(
                 functools.partial(attn_kernel, layer, n_local * tp_size, first),
                 out_shape=outs,
@@ -345,18 +366,19 @@
                 out_specs=out_specs,
                 scratch_shapes=scratch,
                 input_output_aliases=alias,
-                compiler_params=pltpu.CompilerParams(vmem_limit_bytes=14 * MIB),
+                compiler_params=pltpu.CompilerParams(vmem_limit_bytes=13 * MIB),
                 name=f'attn_{layer}',
             )(*ins)
 
-        def reduce(layer, mixed, res, caches=()):
+        def reduce(layer, part, res, caches=()):
             last = layer == n_layers - 1
-            ins = [mixed, w_out, res, ln_gain, ln_shift, b_out, w_up, b_up, w_down, b_down]
-            specs = [vm, hbm, vm, vm, vm, vm, hbm, vm, hbm, vm]
+            ins = [part, res, ln_gain, ln_shift, b_out, w_up, b_up, w_down, b_down]
+            specs = [vm, vm, vm, vm, vm, hbm, vm, hbm, vm]
             outs = [jax.ShapeDtypeStruct((n_batch, width), BF16)]
             if not last:
-                ins += [k_in, v_in, *caches]
-                specs += [hbm, hbm, vm, vm]
+                ins += [k_in, v_in, w_qkv, b_qkv, *caches]
+                specs += [hbm, hbm, hbm, vm, vm, vm]
+                outs = [jax.ShapeDtypeStruct((n_batch, b_qkv.shape[1]), F32)]
                 outs += [jax.ShapeDtypeStruct((blk, width), BF16), held, held]
             dma = pltpu.SemaphoreType.DMA((2, n_chip))
             return pl.pallas_call(
@@ -365,10 +387,8 @@
                 in_specs=specs,
                 out_specs=tuple([vm] * len(outs)),
                 scratch_shapes=[
-                    pltpu.VMEM(w_out.shape[1:], BF16),
                     pltpu.VMEM(w_up.shape[1:], BF16),
                     pltpu.VMEM(w_down.shape[1:], BF16),
-                    pltpu.VMEM((n_batch, width), F32),
                     pltpu.VMEM((n_batch, width), F32),
                     pltpu.VMEM((2, n_chip, blk, width), F32),
                     pltpu.VMEM((2, n_chip, blk, width), F32),
@@ -378,14 +398,14 @@
                     pltpu.SemaphoreType.DMA((6,)),
                 ] + [dma] * 8,
                 input_output_aliases={} if last else {len(ins) - 2: 2, len(ins) - 1: 3},
-                compiler_params=pltpu.CompilerParams(vmem_limit_bytes=14 * MIB, collective_id=layer, has_side_effects=True),
+                compiler_params=pltpu.CompilerParams(vmem_limit_bytes=13 * MIB, collective_id=layer, has_side_effects=True),
                 name=f'reduce_{layer}',
             )(*ins)
 
-        mixed, k_held, v_held = attn(0, x0, None)
-        h1, x1, k_held, v_held = reduce(0, mixed, x0, (k_held, v_held))
-        mixed, k_new, v_new = attn(1, h1, (k_held, v_held))[:3]
-        (x_last,) = reduce(1, mixed, x1)
+        part, k_held, v_held = attn(0, x0, None)
+        qkv, x1, k_held, v_held = reduce(0, part, x0, (k_held, v_held))
+        part, k_new, v_new = attn(1, qkv, (k_held, v_held))[:3]
+        (x_last,) = reduce(1, part, x1)
         return x_last[:, None, :], k_new.reshape(k_cache.shape), v_new.reshape(v_cache.shape)
 
     cache_spec = P(None, 'dp', None, 'tp', None)

time: 80.4 us -> 79 us (0.983)
  Pallas kernels: 78.8 us -> 77.3 us
    pallas_call x2, Pallas kernels: 23.7 us -> 22.1 us  [attn(): pl.pallas_call(functools.partial(attn_kernel, layer, n_local * tp_size, f...]
where the time goes in v4:
time: 79 us; the launch traced here: 78.9 us
  Pallas kernels  77.3 us (98%)
    pallas_call x2, Pallas kernels, reduce(): pl.pallas_call(functools.partial(reduce_kernel, layer, tp_size, last), ou...  55.2 us
    pallas_call x2, Pallas kernels, attn(): pl.pallas_call(functools.partial(attn_kernel, layer, n_local * tp_size, f...  22.1 us

profile of v4, /device:TPU:113, one launch (start us, length us, event | category | flops | bytes accessed | tf_op | source)
XLA Modules:
  0.0 78.9 jit_solution(11603013294754069021)
XLA Ops:
  0.6 0.0 copy-start
  0.6 0.0 copy-start.1
  0.7 0.0 copy-start.2
  0.7 0.0 copy-start.3
  0.7 0.0 copy-start.4
  0.7 0.0 copy-start.5
  0.7 0.0 copy-start.6
  0.7 11.1 %attn_0.1 = (f32[64,2048]{1,0:T(8,128)S(1)}, bf16[2,64,512,128]{3,2,1,0:T(8,128)(2,1)S(1)}, bf16[2,64,512,128]{3,2,1,0:T(8,128)(2,1)S(1)}) custom-call(bf16[64,2048]{1,0:T(8,128)(2,1)} %bitcast.6, bf16[2,2,2048]{2,1,0:T(2,128)(2,1)} %refs_2_.7, bf16[2,2,2048]{2,1,0:T(2,128)(2,1)} %refs_3_.7, bf16[2,768]{1,0:T(2,128)(2,1)} %refs_12_.1, ...), custom_call_target="tpu_custom_call" | custom-call | tf_op jit(solution)/shard_map/attn_0/pallas_call | solution.py:362
  11.8 0.0 copy-done
  11.9 0.0 copy-done.1
  11.9 0.0 copy-done.2
  11.9 0.0 copy-done.3
  11.9 0.0 copy-done.4
  11.9 0.0 copy-done.5
  11.9 0.0 copy-done.6
  11.9 29.5 %reduce_0.1 = (f32[64,768]{1,0:T(8,128)S(1)}, bf16[8,2048]{1,0:T(8,128)(2,1)S(1)}, bf16[2,64,512,128]{3,2,1,0:T(8,128)(2,1)S(1)}, bf16[2,64,512,128]{3,2,1,0:T(8,128)(2,1)S(1)}) custom-call(f32[64,2048]{1,0:T(8,128)S(1)} %get-tuple-element.13.refs_0_, bf16[64,2048]{1,0:T(8,128)(2,1)S(1)} %bitcast.7, ...), custom_call_target="tpu_custom_call", output_to_operand_aliasing={{2}: (13, {}), {3}: (14, {})} | custom-call | tf_op jit(solution)/shard_map/reduce_0/pallas_call | solution.py:384
  41.4 11.0 %attn_1.1 = (f32[64,2048]{1,0:T(8,128)S(1)}, bf16[2,64,512,128]{3,2,1,0:T(8,128)(2,1)}, bf16[2,64,512,128]{3,2,1,0:T(8,128)(2,1)}, bf16[2,64,512,128]{3,2,1,0:T(8,128)(2,1)S(1)}, bf16[2,64,512,128]{3,2,1,0:T(8,128)(2,1)S(1)}) custom-call(f32[64,768]{1,0:T(8,128)S(1)} %get-tuple-element.16.refs_0_, ...), custom_call_target="tpu_custom_call", output_to_operand_aliasing={{3}: (5, {}), {4}: (6, {})} | custom-call | tf_op jit(solution)/shard_map/attn_1/pallas_call | solution.py:362
  52.5 25.7 %reduce_1.1 = bf16[64,2048]{1,0:T(8,128)(2,1)S(1)} custom-call(f32[64,2048]{1,0:T(8,128)S(1)} %get-tuple-element.19.refs_0_, bf16[8,2048]{1,0:T(8,128)(2,1)S(1)} %get-tuple-element.20.refs_1_, bf16[2,2,2048]{2,1,0:T(2,128)(2,1)S(1)} %copy-done.1, bf16[2,2,2048]{2,1,0:T(2,128)(2,1)S(1)} %copy-done.2, bf16[2,2048]{1,0:T(2,128)(2,1)S(1)} %copy-done.3, ...), custom_call_target="tpu_custom_call" | custom-call | tf_op jit(solution)/shard_map/reduce_1/pallas_call | solution.py:384
  78.1 0.7 copy.28
Async XLA Ops:
  0.6 11.2 %copy-start = (bf16[64,1,2048]{2,0,1:T(8,128)(2,1)S(1)}, bf16[64,1,2048]{2,0,1:T(8,128)(2,1)}, u32[]{:S(2)}) copy-start(bf16[64,1,2048]{2,0,1:T(8,128)(2,1)} %param.16) | copy-start | bytes 786436
  0.6 11.2 %copy-start.1 = (bf16[2,2,2048]{2,1,0:T(2,128)(2,1)S(1)}, bf16[2,2,2048]{2,1,0:T(2,128)(2,1)}, u32[]{:S(2)}) copy-start(bf16[2,2,2048]{2,1,0:T(2,128)(2,1)} %refs_2_.7) | copy-start | bytes 49156
  0.7 11.2 %copy-start.2 = (bf16[2,2,2048]{2,1,0:T(2,128)(2,1)S(1)}, bf16[2,2,2048]{2,1,0:T(2,128)(2,1)}, u32[]{:S(2)}) copy-start(bf16[2,2,2048]{2,1,0:T(2,128)(2,1)} %refs_3_.7) | copy-start | bytes 49156
  0.7 11.2 %copy-start.3 = (bf16[2,2048]{1,0:T(2,128)(2,1)S(1)}, bf16[2,2048]{1,0:T(2,128)(2,1)}, u32[]{:S(2)}) copy-start(bf16[2,2048]{1,0:T(2,128)(2,1)} %refs_4_.7) | copy-start | bytes 24580
  0.7 11.2 %copy-start.4 = (bf16[2,2048]{1,0:T(2,128)(2,1)S(1)}, bf16[2,2048]{1,0:T(2,128)(2,1)}, u32[]{:S(2)}) copy-start(bf16[2,2048]{1,0:T(2,128)(2,1)} %refs_8_.5) | copy-start | bytes 24580
  0.7 11.2 %copy-start.5 = (bf16[2,1024]{1,0:T(2,128)(2,1)S(1)}, bf16[2,1024]{1,0:T(2,128)(2,1)}, u32[]{:S(2)}) copy-start(bf16[2,1024]{1,0:T(2,128)(2,1)} %refs_6_.5) | copy-start | bytes 12292
  0.7 11.2 %copy-start.6 = (bf16[2,768]{1,0:T(2,128)(2,1)S(1)}, bf16[2,768]{1,0:T(2,128)(2,1)}, u32[]{:S(2)}) copy-start(bf16[2,768]{1,0:T(2,128)(2,1)} %refs_12_.1) | copy-start | bytes 9220

commit v5 on v4

--- a/solution.py
+++ b/solution.py
@@ -14,6 +14,8 @@
 BF16 = jnp.bfloat16
 GROUP = 8
 AHEAD = 6
+SUB = 2
+EARLY = 2
 MIB = 2 ** 20
 
 
@@ -28,11 +30,12 @@
 def attn_kernel(layer, n_heads, first, *refs):
     if first:
         (x_in_ref, gain_in, shift_in, bq_in, wq_hbm, wo_hbm, slot_hbm, pos_in, valid_in, k_hbm, v_hbm,
-         part_ref, kall, vall,
-         pos_ref, valid_ref, slot_smem, wo, bias, attn, sem_w, sem_s,
+         part_ref, k_out, v_out, kall, vall,
+         pos_ref, valid_ref, slot_smem, wo, bias, attn, sem_w, sem_s, sem_out,
          x_ref, gain_ref, shift_ref, bq_ref, wq, qkv, sem_in) = refs
+        old = []
     else:
-        (qkv, wo_hbm, slot_hbm, pos_in, valid_in, k_raw, v_raw,
+        (qkv, wo_hbm, slot_hbm, pos_in, valid_in, k_part, v_part, k_raw, v_raw,
          part_ref, k_out, v_out, kall, vall,
          pos_ref, valid_ref, slot_smem, wo, bias, attn, sem_w, sem_s, sem_out) = refs
     kbuf, vbuf = kall.at[layer], vall.at[layer]
@@ -73,7 +76,7 @@
         wo_copy.start()
         old = [
             pltpu.make_async_copy(src.at[layer - 1, pl.ds(g * GROUP, GROUP)], dst.at[layer - 1, pl.ds(g * GROUP, GROUP)], sem_out.at[2 + i])
-            for g in range(n_groups) for i, (src, dst) in enumerate(((kall, k_out), (vall, v_out)))
+            for g in range(EARLY, n_groups) for i, (src, dst) in enumerate(((kall, k_out), (vall, v_out)))
         ]
         for c in old:
             c.start()
@@ -103,19 +106,7 @@
     rows = n_local * GROUP
     head0 = lax.axis_index('tp') * n_local
 
-    def group(g, carry):
-        if first:
-            in_copy(0, g).wait()
-            in_copy(1, g).wait()
-
-            @pl.when(g + AHEAD < n_groups)
-            def _():
-                in_copy(0, g + AHEAD).start()
-                in_copy(1, g + AHEAD).start()
-
-            @pl.when(g + AHEAD == n_groups)
-            def _():
-                wo_copy.start()
+    def update(g):
         base = pl.multiple_of(g * GROUP, GROUP)
         row16 = lax.broadcasted_iota(jnp.int32, (16, head_dim), 0)
         fresh = qkv[pl.ds(base, GROUP), :]
@@ -144,16 +135,23 @@
         queries = jnp.concatenate([fresh[:, 3 * h * head_dim:(3 * h + 1) * head_dim] for h in range(n_local)], axis=0)
         odd = lax.broadcasted_iota(jnp.int32, (rows, head_dim), 0) % 2 == 1
         q_pair = jnp.concatenate([jnp.where(odd, 0.0, queries), jnp.where(odd, queries, 0.0)], axis=1).astype(BF16)
+        return base, q_pair, jnp.concatenate(parts, axis=0)
+
+    def scores(base, q_pair, add):
         row_s = lax.broadcasted_iota(jnp.int32, (rows, n_cols), 0) % GROUP // 2
         s = None
         for b in range(0, GROUP, 2):
             keys = jnp.concatenate([kbuf[base + b], kbuf[base + b + 1]], axis=1)
             sb = lax.dot_general(q_pair, keys, (((1,), (1,)), ((), ())), preferred_element_type=F32)
             s = sb if s is None else jnp.where(row_s == b // 2, sb, s)
-        s = s * scale + jnp.concatenate(parts, axis=0)
+        return s * scale + add
+
+    def softmax(s):
         top = jnp.max(s, axis=-1, keepdims=True)
         e = jnp.exp(s - top)
-        p = (e * (1.0 / jnp.sum(e, axis=-1, keepdims=True))).astype(BF16)
+        return (e * (1.0 / jnp.sum(e, axis=-1, keepdims=True))).astype(BF16)
+
+    def mix(base, p):
         row_o = lax.broadcasted_iota(jnp.int32, (rows, head_dim), 0) % GROUP
         o = None
         for b in range(0, GROUP, 2):
@@ -164,20 +162,47 @@
                 o = oi if o is None else jnp.where(row_o == b + i, oi, o)
         for h in range(n_local):
             attn[pl.ds(base, GROUP), h * head_dim:(h + 1) * head_dim] = o[h * GROUP:(h + 1) * GROUP]
+
+    def groups(i, carry):
+        todo = [i * SUB + j for j in range(SUB)]
+        if first:
+            for g in todo:
+                in_copy(0, g).wait()
+                in_copy(1, g).wait()
+
+            @pl.when(todo[-1] + AHEAD < n_groups)
+            def _():
+                for g in todo:
+                    in_copy(0, g + AHEAD).start()
+                    in_copy(1, g + AHEAD).start()
+
+            @pl.when(i == n_groups // SUB - 2)
+            def _():
+                wo_copy.start()
+
+            @pl.when(i == n_groups // SUB - 1)
+            def _():
+                for g in range(EARLY):
+                    out_copy(0, g).start()
+                    out_copy(1, g).start()
+        state = [update(g) for g in todo]
+        probs = [scores(*st) for st in state]
+        for (base, _, _), s in zip(state, probs):
+            mix(base, softmax(s))
         if not first:
-            out_copy(0, g).start()
-            out_copy(1, g).start()
+            for g in todo:
+                out_copy(0, g).start()
+                out_copy(1, g).start()
         return carry
 
-    lax.fori_loop(0, n_groups, group, 0)
+    lax.fori_loop(0, n_groups // SUB, groups, 0)
     wo_copy.wait()
     part_ref[...] = jnp.dot(attn[...].astype(BF16), wo[...], preferred_element_type=F32)
-    if not first:
-        for c in old:
-            c.wait()
-        for g in range(n_groups):
-            out_copy(0, g).wait()
-            out_copy(1, g).wait()
+    for c in old:
+        c.wait()
+    for g in range(EARLY if first else n_groups):
+        out_copy(0, g).wait()
+        out_copy(1, g).wait()
 
 
 def reduce_kernel(layer, n_tp, last, *refs):
@@ -337,13 +362,14 @@
                 pltpu.VMEM((n_batch, n_local * head_dim), F32),
                 pltpu.SemaphoreType.DMA((5,)),
                 pltpu.SemaphoreType.DMA((7,)),
+                pltpu.SemaphoreType.DMA((4,)),
             ]
             alias = {}
             part = jax.ShapeDtypeStruct((n_batch, width), F32)
+            outs, out_specs = (part, shape, shape, held, held), (vm, hbm, hbm, vm, vm)
             if first:
                 ins = [in_hbm(a) for a in (x_in, ln_gain, ln_shift, b_qkv)] + [w_qkv, w_out] + shared + [k_in, v_in]
                 specs = [hbm] * len(ins)
-                outs, out_specs = (part, held, held), (vm, vm, vm)
                 scratch += [
                     pltpu.VMEM(x_in.shape, BF16),
                     pltpu.VMEM(ln_gain.shape, BF16),
@@ -355,10 +381,8 @@
                 ]
             else:
                 ins = [x_in, w_out] + shared + list(caches)
-                specs = [vm, hbm] + [hbm] * len(shared) + [vm] * 2
-                outs, out_specs = (part, shape, shape, held, held), (vm, hbm, hbm, vm, vm)
-                alias = {len(ins) - 2: 3, len(ins) - 1: 4}
-                scratch += [pltpu.SemaphoreType.DMA((4,))]
+                specs = [vm, hbm] + [hbm] * len(shared) + [hbm] * 2 + [vm] * 2
+                alias = {len(ins) - 4 + i: 1 + i for i in range(4)}
             return pl.pallas_call(
                 functools.partial(attn_kernel, layer, n_local * tp_size, first),
                 out_shape=outs,
@@ -402,9 +426,9 @@
                 name=f'reduce_{layer}',
             )(*ins)
 
-        part, k_held, v_held = attn(0, x0, None)
+        part, k_new, v_new, k_held, v_held = attn(0, x0, None)
         qkv, x1, k_held, v_held = reduce(0, part, x0, (k_held, v_held))
-        part, k_new, v_new = attn(1, qkv, (k_held, v_held))[:3]
+        part, k_new, v_new, _, _ = attn(1, qkv, (k_new, v_new, k_held, v_held))
         (x_last,) = reduce(1, part, x1)
         return x_last[:, None, :], k_new.reshape(k_cache.shape), v_new.reshape(v_cache.shape)
 

time: 79 us -> 76.6 us (0.970)
  Pallas kernels: 77.3 us -> 75 us
    pallas_call x2, Pallas kernels: 22.1 us -> 19.8 us  [attn(): pl.pallas_call(functools.partial(attn_kernel, layer, n_local * tp_size, f...]
where the time goes in v5:
time: 76.6 us; the launch traced here: 76.5 us
  Pallas kernels  75 us (98%)
  between operations  0.77 us (1%)
    pallas_call x2, Pallas kernels, reduce(): pl.pallas_call(functools.partial(reduce_kernel, layer, tp_size, last), ou...  55.2 us
    pallas_call x2, Pallas kernels, attn(): pl.pallas_call(functools.partial(attn_kernel, layer, n_local * tp_size, f...  19.8 us

profile of v5, /device:TPU:113, one launch (start us, length us, event | category | flops | bytes accessed | tf_op | source)
XLA Modules:
  0.0 76.5 jit_solution(3817241784347862122)
XLA Ops:
  0.6 0.0 copy-start
  0.6 0.0 copy-start.1
  0.7 0.0 copy-start.2
  0.7 0.0 copy-start.3
  0.7 0.0 copy-start.4
  0.7 0.0 copy-start.5
  0.7 0.0 copy-start.6
  0.7 10.1 %attn_0.1 = (f32[64,2048]{1,0:T(8,128)S(1)}, bf16[2,64,512,128]{3,2,1,0:T(8,128)(2,1)}, bf16[2,64,512,128]{3,2,1,0:T(8,128)(2,1)}, bf16[2,64,512,128]{3,2,1,0:T(8,128)(2,1)S(1)}, bf16[2,64,512,128]{3,2,1,0:T(8,128)(2,1)S(1)}) custom-call(bf16[64,2048]{1,0:T(8,128)(2,1)} %bitcast.6, bf16[2,2,2048]{2,1,0:T(2,128)(2,1)} %refs_2_.7, ...), custom_call_target="tpu_custom_call" | custom-call | tf_op jit(solution)/shard_map/attn_0/pallas_call | solution.py:386
  10.8 0.0 copy-done
  10.8 0.0 copy-done.1
  10.8 0.0 copy-done.2
  10.8 0.0 copy-done.3
  10.8 0.0 copy-done.4
  10.8 0.0 copy-done.5
  10.8 0.0 copy-done.6
  10.9 29.5 %reduce_0.1 = (f32[64,768]{1,0:T(8,128)S(1)}, bf16[8,2048]{1,0:T(8,128)(2,1)S(1)}, bf16[2,64,512,128]{3,2,1,0:T(8,128)(2,1)S(1)}, bf16[2,64,512,128]{3,2,1,0:T(8,128)(2,1)S(1)}) custom-call(f32[64,2048]{1,0:T(8,128)S(1)} %get-tuple-element.15.refs_0_, bf16[64,2048]{1,0:T(8,128)(2,1)S(1)} %bitcast.7, ...), custom_call_target="tpu_custom_call", output_to_operand_aliasing={{2}: (13, {}), {3}: (14, {})} | custom-call | tf_op jit(solution)/shard_map/reduce_0/pallas_call | solution.py:408
  40.4 9.7 %attn_1.1 = (f32[64,2048]{1,0:T(8,128)S(1)}, bf16[2,64,512,128]{3,2,1,0:T(8,128)(2,1)}, bf16[2,64,512,128]{3,2,1,0:T(8,128)(2,1)}, bf16[2,64,512,128]{3,2,1,0:T(8,128)(2,1)S(1)}, bf16[2,64,512,128]{3,2,1,0:T(8,128)(2,1)S(1)}) custom-call(f32[64,768]{1,0:T(8,128)S(1)} %get-tuple-element.18.refs, ...), custom_call_target="tpu_custom_call", output_to_operand_aliasing={{1}: (5, {}), {2}: (6, {}), {3}: (7, {}), {4}: (8, {})} | custom-call | tf_op jit(solution)/shard_map/attn_1/pallas_call | solution.py:386
  50.1 25.7 %reduce_1.1 = bf16[64,2048]{1,0:T(8,128)(2,1)S(1)} custom-call(f32[64,2048]{1,0:T(8,128)S(1)} %get-tuple-element.23.refs_0_, bf16[8,2048]{1,0:T(8,128)(2,1)S(1)} %get-tuple-element.24.refs_1_, bf16[2,2,2048]{2,1,0:T(2,128)(2,1)S(1)} %copy-done.1, bf16[2,2,2048]{2,1,0:T(2,128)(2,1)S(1)} %copy-done.2, bf16[2,2048]{1,0:T(2,128)(2,1)S(1)} %copy-done.3, ...), custom_call_target="tpu_custom_call" | custom-call | tf_op jit(solution)/shard_map/reduce_1/pallas_call | solution.py:408
  75.8 0.7 copy.32
Async XLA Ops:
  0.6 10.2 %copy-start = (bf16[64,1,2048]{2,0,1:T(8,128)(2,1)S(1)}, bf16[64,1,2048]{2,0,1:T(8,128)(2,1)}, u32[]{:S(2)}) copy-start(bf16[64,1,2048]{2,0,1:T(8,128)(2,1)} %param.16) | copy-start | bytes 786436
  0.6 10.2 %copy-start.1 = (bf16[2,2,2048]{2,1,0:T(2,128)(2,1)S(1)}, bf16[2,2,2048]{2,1,0:T(2,128)(2,1)}, u32[]{:S(2)}) copy-start(bf16[2,2,2048]{2,1,0:T(2,128)(2,1)} %refs_2_.7) | copy-start | bytes 49156
  0.7 10.2 %copy-start.2 = (bf16[2,2,2048]{2,1,0:T(2,128)(2,1)S(1)}, bf16[2,2,2048]{2,1,0:T(2,128)(2,1)}, u32[]{:S(2)}) copy-start(bf16[2,2,2048]{2,1,0:T(2,128)(2,1)} %refs_3_.7) | copy-start | bytes 49156
  0.7 10.2 %copy-start.3 = (bf16[2,2048]{1,0:T(2,128)(2,1)S(1)}, bf16[2,2048]{1,0:T(2,128)(2,1)}, u32[]{:S(2)}) copy-start(bf16[2,2048]{1,0:T(2,128)(2,1)} %refs_4_.7) | copy-start | bytes 24580
  0.7 10.2 %copy-start.4 = (bf16[2,2048]{1,0:T(2,128)(2,1)S(1)}, bf16[2,2048]{1,0:T(2,128)(2,1)}, u32[]{:S(2)}) copy-start(bf16[2,2048]{1,0:T(2,128)(2,1)} %refs_8_.5) | copy-start | bytes 24580
  0.7 10.2 %copy-start.5 = (bf16[2,1024]{1,0:T(2,128)(2,1)S(1)}, bf16[2,1024]{1,0:T(2,128)(2,1)}, u32[]{:S(2)}) copy-start(bf16[2,1024]{1,0:T(2,128)(2,1)} %refs_6_.5) | copy-start | bytes 12292
  0.7 10.2 %copy-start.6 = (bf16[2,768]{1,0:T(2,128)(2,1)S(1)}, bf16[2,768]{1,0:T(2,128)(2,1)}, u32[]{:S(2)}) copy-start(bf16[2,768]{1,0:T(2,128)(2,1)} %refs_12_.1) | copy-start | bytes 9220

commit v6 on v5

--- a/solution.py
+++ b/solution.py
@@ -16,6 +16,8 @@
 AHEAD = 6
 SUB = 2
 EARLY = 2
+RS_DIRECT = 512
+AG_PASSED = 1408
 MIB = 2 ** 20
 
 
@@ -212,8 +214,8 @@
     else:
         (k_hbm, v_hbm, wq_hbm, bq_ref, k_raw, v_raw, out_ref, own_ref, kall, vall) = refs[9:19]
         rest = refs[19:]
-    (wu, wd, part2, d2d, mid, got, gath, gath2, sem_w,
-     pair_s, pair_r, chip_s, chip_r, ag_s, ag_r, agp_s, agp_r) = rest
+    (wu, wd, part2, d2d, mid, got, near, gath, gath2, sem_w,
+     pair_s, pair_r, chip_s, chip_r, ag_s, ag_r, agp_s, agp_r, dir_s, dir_r, agd_s, agd_r) = rest
     n_batch, width = part_ref.shape
     n_chip = n_tp // 2
     blk = n_batch // n_tp
@@ -233,70 +235,102 @@
         wq = wu.at[:, pl.ds(0, n_qkv)]
         wq_copy = pltpu.make_async_copy(wq_hbm.at[layer + 1], wq, sem_w.at[4])
     barrier = pltpu.get_barrier_semaphore()
-    peers = [partner] + [chip(d) * 2 + 1 - c for d in range(1, n_chip)]
-    for peer in peers:
-        pl.semaphore_signal(barrier, inc=1, device_id={'tp': peer}, device_id_type=MESH)
+    for d in range(1, n_tp):
+        pl.semaphore_signal(barrier, inc=1, device_id={'tp': lax.rem(me + d, n_tp)}, device_id_type=MESH)
     for w in w_copies:
         w.start()
-    pl.semaphore_wait(barrier, len(peers))
+    pl.semaphore_wait(barrier, n_tp - 1)
 
     order = [2, 1, 3, 0] if n_chip == 4 else list(range(1, n_chip)) + [0]
 
     def rows_of(core, d):
         return pl.ds(pl.multiple_of((core * n_chip + chip(d)) * blk, blk), blk)
 
-    def reduce_scatter(phase, src):
-        pair = {
-            d: pltpu.make_async_remote_copy(
-                src_ref=src.at[rows_of(1 - c, d)], dst_ref=d2d.at[phase, d], send_sem=pair_s.at[phase, d],
-                recv_sem=pair_r.at[phase, d], device_id={'tp': partner}, device_id_type=MESH)
-            for d in order
-        }
+    direct, passed_cols = pl.ds(0, RS_DIRECT), pl.ds(0, AG_PASSED)
+    tail, spread = pl.ds(RS_DIRECT, width - RS_DIRECT), pl.ds(AG_PASSED, width - AG_PASSED)
+    far = order[:-1]
+    by_distance = sorted(order, key=lambda d: min(d, n_chip - d))
+
+    def remote(src, dst, send_sem, recv_sem, to):
+        return pltpu.make_async_remote_copy(src_ref=src, dst_ref=dst, send_sem=send_sem, recv_sem=recv_sem, device_id={'tp': to}, device_id_type=MESH)
+
+    def reduce_scatter(phase, src, fill_tail=None):
+        def straight(d, half, sender):
+            return remote(src.at[rows_of(half, d), direct], near.at[phase, sender, d], dir_s.at[phase, half, d], dir_r.at[phase, sender, d], chip(d) * 2 + 1 - half)
+
+        def paired(d):
+            cols = tail if d else pl.ds(0, width)
+            return remote(src.at[rows_of(1 - c, d), cols], d2d.at[phase, d, :, cols], pair_s.at[phase, d], pair_r.at[phase, d], partner)
+
+        def onward(d):
+            cols = tail if d else pl.ds(0, width)
+            return remote(mid.at[phase, d, :, cols], got.at[phase, d, :, cols], chip_s.at[phase, d], chip_r.at[phase, d], chip(d) * 2 + 1 - c)
+
+        for d in far:
+            for half in range(2):
+                straight(d, half, c).start()
+        if fill_tail is not None:
+            fill_tail()
         for d in order:
-            pair[d].start()
-        hops = {}
+            paired(d).start()
         for d in order:
-            pair[d].wait_recv()
-            mid[phase, d] = src[rows_of(c, d), :] + d2d[phase, d]
-            hops[d] = pltpu.make_async_remote_copy(
-                src_ref=mid.at[phase, d], dst_ref=got.at[phase, d], send_sem=chip_s.at[phase, d],
-                recv_sem=chip_r.at[phase, d], device_id={'tp': chip(d) * 2 + 1 - c}, device_id_type=MESH)
-            hops[d].start()
+            paired(d).wait_recv()
+            cols = tail if d else pl.ds(0, width)
+            mid[phase, d, :, cols] = src[rows_of(c, d), cols] + d2d[phase, d, :, cols]
+            onward(d).start()
+        head = None
+        for d in far:
+            for sender in range(2):
+                straight(d, 0, sender).wait_recv()
+                head = near[phase, sender, d] if head is None else head + near[phase, sender, d]
         acc = None
-        for d in sorted(hops, key=lambda d: min(d, n_chip - d)):
-            hops[d].wait_recv()
-            acc = got[phase, d] if acc is None else acc + got[phase, d]
+        for d in by_distance:
+            onward(d).wait_recv()
+            if d == 0:
+                head = head + got[phase, d, :, direct]
+            acc = got[phase, d, :, tail] if acc is None else acc + got[phase, d, :, tail]
         for d in order:
-            pair[d].wait_send()
-            hops[d].wait_send()
-        return acc
+            paired(d).wait_send()
+            onward(d).wait_send()
+        for d in far:
+            for half in range(2):
+                straight(d, half, c).wait_send()
+        return jnp.concatenate([head, acc], axis=1)
 
     def all_gather(phase, buf, value):
         buf[1 - c, x] = value
-        hops = {}
-        for d in order[:-1]:
-            hops[d] = pltpu.make_async_remote_copy(
-                src_ref=buf.at[1 - c, x], dst_ref=buf.at[1 - c, x], send_sem=ag_s.at[phase, d], recv_sem=ag_r.at[phase, d],
-                device_id={'tp': chip(d) * 2 + 1 - c}, device_id_type=MESH)
-            hops[d].start()
+
+        def onward(d):
+            return remote(buf.at[1 - c, x, :, passed_cols], buf.at[1 - c, x, :, passed_cols], ag_s.at[phase, d], ag_r.at[phase, d], chip(d) * 2 + 1 - c)
+
+        def straight(d, core, half, slot):
+            part = buf.at[half, slot, :, spread]
+            return remote(part, part, agd_s.at[phase, core, d], agd_r.at[phase, half, d], chip(d) * 2 + core)
 
         def pass_on(d):
             slot = lax.rem(x + n_chip - d, n_chip)
-            half = 1 - c if d == 0 else c
-            cp = pltpu.make_async_remote_copy(
-                src_ref=buf.at[half, slot], dst_ref=buf.at[half, slot], send_sem=agp_s.at[phase, d], recv_sem=agp_r.at[phase, d],
-                device_id={'tp': partner}, device_id_type=MESH)
-            cp.start()
-            return cp
-
-        passed = [pass_on(0)]
-        for d in sorted(hops, key=lambda d: min(d, n_chip - d)):
-            hops[d].wait_recv()
-            passed.append(pass_on(d))
-        for cp in passed:
-            cp.wait()
-        for d in hops:
-            hops[d].wait_send()
+            half = c if d else 1 - c
+            part = buf.at[half, slot, :, passed_cols] if d else buf.at[half, slot]
+            return remote(part, part, agp_s.at[phase, d], agp_r.at[phase, d], partner)
+
+        for d in far:
+            onward(d).start()
+        pass_on(0).start()
+        for d in far:
+            for core in range(2):
+                straight(d, core, 1 - c, x).start()
+        for d in by_distance[1:]:
+            onward(d).wait_recv()
+            pass_on(d).start()
+        for d in far:
+            for half in range(2):
+                straight(d, 0, half, lax.rem(x + n_chip - d, n_chip)).wait_recv()
+        for d in order:
+            pass_on(d).wait()
+        for d in far:
+            onward(d).wait_send()
+            for core in range(2):
+                straight(d, core, 1 - c, x).wait_send()
         return buf[...].astype(F32).reshape(n_batch, width)
 
     if last:
@@ -312,8 +346,12 @@
     if not last:
         wq_copy.start()
     w_copies[1].wait()
-    part2[...] = jnp.dot(act, wd[...], preferred_element_type=F32)
-    total = reduce_scatter(1, part2)
+    part2[:, :RS_DIRECT] = jnp.dot(act, wd[:, :RS_DIRECT], preferred_element_type=F32)
+
+    def fill_tail():
+        part2[:, RS_DIRECT:] = jnp.dot(act, wd[:, RS_DIRECT:], preferred_element_type=F32)
+
+    total = reduce_scatter(1, part2, fill_tail)
     x_next = (x_mid + total + bd_ref[layer:layer + 1].astype(F32)).astype(BF16)
     if last:
         out_ref[...] = all_gather(1, gath2, x_next).astype(BF16)
@@ -405,6 +443,7 @@
                 outs = [jax.ShapeDtypeStruct((n_batch, b_qkv.shape[1]), F32)]
                 outs += [jax.ShapeDtypeStruct((blk, width), BF16), held, held]
             dma = pltpu.SemaphoreType.DMA((2, n_chip))
+            dma2 = pltpu.SemaphoreType.DMA((2, 2, n_chip))
             return pl.pallas_call(
                 functools.partial(reduce_kernel, layer, tp_size, last),
                 out_shape=tuple(outs),
@@ -417,10 +456,11 @@
                     pltpu.VMEM((2, n_chip, blk, width), F32),
                     pltpu.VMEM((2, n_chip, blk, width), F32),
                     pltpu.VMEM((2, n_chip, blk, width), F32),
+                    pltpu.VMEM((2, 2, n_chip, blk, RS_DIRECT), F32),
                     pltpu.VMEM((2, n_chip, blk, width), BF16),
                     pltpu.VMEM((2, n_chip, blk, width), BF16),
                     pltpu.SemaphoreType.DMA((6,)),
-                ] + [dma] * 8,
+                ] + [dma] * 8 + [dma2] * 4,
                 input_output_aliases={} if last else {len(ins) - 2: 2, len(ins) - 1: 3},
                 compiler_params=pltpu.CompilerParams(vmem_limit_bytes=13 * MIB, collective_id=layer, has_side_effects=True),
                 name=f'reduce_{layer}',

time: 76.6 us -> 77.8 us (1.016)
  Pallas kernels: 75 us -> 76.2 us
    pallas_call x2, Pallas kernels: 55.2 us -> 56.4 us  [reduce(): pl.pallas_call(functools.partial(reduce_kernel, layer, tp_size, last), ou...]
where the time goes in v6:
time: 77.8 us; the launch traced here: 77.7 us
  Pallas kernels  76.2 us (98%)
    pallas_call x2, Pallas kernels, reduce(): pl.pallas_call(functools.partial(reduce_kernel, layer, tp_size, last), ou...  56.4 us
    pallas_call x2, Pallas kernels, attn(): pl.pallas_call(functools.partial(attn_kernel, layer, n_local * tp_size, f...  19.8 us

profile of v6, /device:TPU:113, one launch (start us, length us, event | category | flops | bytes accessed | tf_op | source)
XLA Modules:
  0.0 77.7 jit_solution(5556067695113536048)
XLA Ops:
  0.6 0.0 copy-start
  0.6 0.0 copy-start.1
  0.7 0.0 copy-start.2
  0.7 0.0 copy-start.3
  0.7 0.0 copy-start.4
  0.7 0.0 copy-start.5
  0.7 0.0 copy-start.6
  0.7 10.1 %attn_0.1 = (f32[64,2048]{1,0:T(8,128)S(1)}, bf16[2,64,512,128]{3,2,1,0:T(8,128)(2,1)}, bf16[2,64,512,128]{3,2,1,0:T(8,128)(2,1)}, bf16[2,64,512,128]{3,2,1,0:T(8,128)(2,1)S(1)}, bf16[2,64,512,128]{3,2,1,0:T(8,128)(2,1)S(1)}) custom-call(bf16[64,2048]{1,0:T(8,128)(2,1)} %bitcast.6, bf16[2,2,2048]{2,1,0:T(2,128)(2,1)} %refs_2_.7, ...), custom_call_target="tpu_custom_call" | custom-call | tf_op jit(solution)/shard_map/attn_0/pallas_call | solution.py:424
  10.8 0.0 copy-done
  10.8 0.0 copy-done.1
  10.8 0.0 copy-done.2
  10.8 0.0 copy-done.3
  10.8 0.0 copy-done.4
  10.8 0.0 copy-done.5
  10.8 0.0 copy-done.6
  10.9 29.9 %reduce_0.1 = (f32[64,768]{1,0:T(8,128)S(1)}, bf16[8,2048]{1,0:T(8,128)(2,1)S(1)}, bf16[2,64,512,128]{3,2,1,0:T(8,128)(2,1)S(1)}, bf16[2,64,512,128]{3,2,1,0:T(8,128)(2,1)S(1)}) custom-call(f32[64,2048]{1,0:T(8,128)S(1)} %get-tuple-element.15.refs_0_, bf16[64,2048]{1,0:T(8,128)(2,1)S(1)} %bitcast.7, ...), custom_call_target="tpu_custom_call", output_to_operand_aliasing={{2}: (13, {}), {3}: (14, {})} | custom-call | tf_op jit(solution)/shard_map/reduce_0/pallas_call | solution.py:447
  40.8 9.7 %attn_1.1 = (f32[64,2048]{1,0:T(8,128)S(1)}, bf16[2,64,512,128]{3,2,1,0:T(8,128)(2,1)}, bf16[2,64,512,128]{3,2,1,0:T(8,128)(2,1)}, bf16[2,64,512,128]{3,2,1,0:T(8,128)(2,1)S(1)}, bf16[2,64,512,128]{3,2,1,0:T(8,128)(2,1)S(1)}) custom-call(f32[64,768]{1,0:T(8,128)S(1)} %get-tuple-element.18.refs, ...), custom_call_target="tpu_custom_call", output_to_operand_aliasing={{1}: (5, {}), {2}: (6, {}), {3}: (7, {}), {4}: (8, {})} | custom-call | tf_op jit(solution)/shard_map/attn_1/pallas_call | solution.py:424
  50.5 26.4 %reduce_1.1 = bf16[64,2048]{1,0:T(8,128)(2,1)S(1)} custom-call(f32[64,2048]{1,0:T(8,128)S(1)} %get-tuple-element.23.refs_0_, bf16[8,2048]{1,0:T(8,128)(2,1)S(1)} %get-tuple-element.24.refs_1_, bf16[2,2,2048]{2,1,0:T(2,128)(2,1)S(1)} %copy-done.1, bf16[2,2,2048]{2,1,0:T(2,128)(2,1)S(1)} %copy-done.2, bf16[2,2048]{1,0:T(2,128)(2,1)S(1)} %copy-done.3, ...), custom_call_target="tpu_custom_call" | custom-call | tf_op jit(solution)/shard_map/reduce_1/pallas_call | solution.py:447
  77.0 0.7 copy.32
Async XLA Ops:
  0.6 10.2 %copy-start = (bf16[64,1,2048]{2,0,1:T(8,128)(2,1)S(1)}, bf16[64,1,2048]{2,0,1:T(8,128)(2,1)}, u32[]{:S(2)}) copy-start(bf16[64,1,2048]{2,0,1:T(8,128)(2,1)} %param.16) | copy-start | bytes 786436
  0.6 10.2 %copy-start.1 = (bf16[2,2,2048]{2,1,0:T(2,128)(2,1)S(1)}, bf16[2,2,2048]{2,1,0:T(2,128)(2,1)}, u32[]{:S(2)}) copy-start(bf16[2,2,2048]{2,1,0:T(2,128)(2,1)} %refs_2_.7) | copy-start | bytes 49156
  0.7 10.2 %copy-start.2 = (bf16[2,2,2048]{2,1,0:T(2,128)(2,1)S(1)}, bf16[2,2,2048]{2,1,0:T(2,128)(2,1)}, u32[]{:S(2)}) copy-start(bf16[2,2,2048]{2,1,0:T(2,128)(2,1)} %refs_3_.7) | copy-start | bytes 49156
  0.7 10.2 %copy-start.3 = (bf16[2,2048]{1,0:T(2,128)(2,1)S(1)}, bf16[2,2048]{1,0:T(2,128)(2,1)}, u32[]{:S(2)}) copy-start(bf16[2,2048]{1,0:T(2,128)(2,1)} %refs_4_.7) | copy-start | bytes 24580
  0.7 10.2 %copy-start.4 = (bf16[2,2048]{1,0:T(2,128)(2,1)S(1)}, bf16[2,2048]{1,0:T(2,128)(2,1)}, u32[]{:S(2)}) copy-start(bf16[2,2048]{1,0:T(2,128)(2,1)} %refs_8_.5) | copy-start | bytes 24580
  0.7 10.2 %copy-start.5 = (bf16[2,1024]{1,0:T(2,128)(2,1)S(1)}, bf16[2,1024]{1,0:T(2,128)(2,1)}, u32[]{:S(2)}) copy-start(bf16[2,1024]{1,0:T(2,128)(2,1)} %refs_6_.5) | copy-start | bytes 12292
  0.7 10.2 %copy-start.6 = (bf16[2,768]{1,0:T(2,128)(2,1)S(1)}, bf16[2,768]{1,0:T(2,128)(2,1)}, u32[]{:S(2)}) copy-start(bf16[2,768]{1,0:T(2,128)(2,1)} %refs_12_.1) | copy-start | bytes 9220

commit v7 on v5

--- a/solution.py
+++ b/solution.py
@@ -29,15 +29,15 @@
 
 def attn_kernel(layer, n_heads, first, *refs):
     if first:
-        (x_in_ref, gain_in, shift_in, bq_in, wq_hbm, wo_hbm, slot_hbm, pos_in, valid_in, k_hbm, v_hbm,
-         part_ref, k_out, v_out, kall, vall,
-         pos_ref, valid_ref, slot_smem, wo, bias, attn, sem_w, sem_s, sem_out,
+        (x_in_ref, gain_in, shift_in, bq_in, wq_hbm, slot_hbm, pos_in, valid_in, k_hbm, v_hbm,
+         attn_ref, k_out, v_out, kall, vall,
+         pos_ref, valid_ref, slot_smem, bias, attn, sem_w, sem_s, sem_out,
          x_ref, gain_ref, shift_ref, bq_ref, wq, qkv, sem_in) = refs
         old = []
     else:
-        (qkv, wo_hbm, slot_hbm, pos_in, valid_in, k_part, v_part, k_raw, v_raw,
-         part_ref, k_out, v_out, kall, vall,
-         pos_ref, valid_ref, slot_smem, wo, bias, attn, sem_w, sem_s, sem_out) = refs
+        (qkv, slot_hbm, pos_in, valid_in, k_part, v_part, k_raw, v_raw,
+         attn_ref, k_out, v_out, kall, vall,
+         pos_ref, valid_ref, slot_smem, bias, attn, sem_w, sem_s, sem_out) = refs
     kbuf, vbuf = kall.at[layer], vall.at[layer]
     n_batch, n_cols, head_dim = kbuf.shape
     n_groups = n_batch // GROUP
@@ -50,7 +50,6 @@
     small = [pltpu.make_async_copy(src, dst, sem_s.at[i]) for i, (src, dst) in enumerate(pairs)]
     for c in small:
         c.start()
-    wo_copy = pltpu.make_async_copy(wo_hbm.at[layer], wo, sem_w.at[n_chunk])
     if first:
         step = x_ref.shape[1] // n_chunk
         w_copies = [
@@ -73,7 +72,6 @@
             in_copy(0, g).start()
             in_copy(1, g).start()
     else:
-        wo_copy.start()
         old = [
             pltpu.make_async_copy(src.at[layer - 1, pl.ds(g * GROUP, GROUP)], dst.at[layer - 1, pl.ds(g * GROUP, GROUP)], sem_out.at[2 + i])
             for g in range(EARLY, n_groups) for i, (src, dst) in enumerate(((kall, k_out), (vall, v_out)))
@@ -176,10 +174,6 @@
                     in_copy(0, g + AHEAD).start()
                     in_copy(1, g + AHEAD).start()
 
-            @pl.when(i == n_groups // SUB - 2)
-            def _():
-                wo_copy.start()
-
             @pl.when(i == n_groups // SUB - 1)
             def _():
                 for g in range(EARLY):
@@ -196,8 +190,7 @@
         return carry
 
     lax.fori_loop(0, n_groups // SUB, groups, 0)
-    wo_copy.wait()
-    part_ref[...] = jnp.dot(attn[...].astype(BF16), wo[...], preferred_element_type=F32)
+    attn_ref[...] = attn[...].astype(BF16)
     for c in old:
         c.wait()
     for g in range(EARLY if first else n_groups):
@@ -206,13 +199,13 @@
 
 
 def reduce_kernel(layer, n_tp, last, *refs):
-    (part_ref, res_ref, gain_ref, shift_ref, bo_ref, wu_hbm, bu_ref, wd_hbm, bd_ref) = refs[:9]
+    (attn_ref, wo_hbm, res_ref, gain_ref, shift_ref, bo_ref, wu_hbm, bu_ref, wd_hbm, bd_ref) = refs[:10]
     if last:
-        out_ref, rest = refs[9], refs[10:]
+        out_ref, rest = refs[10], refs[11:]
     else:
-        (k_hbm, v_hbm, wq_hbm, bq_ref, k_raw, v_raw, out_ref, own_ref, kall, vall) = refs[9:19]
-        rest = refs[19:]
-    (wu, wd, part2, d2d, mid, got, gath, gath2, sem_w,
+        (k_hbm, v_hbm, wq_hbm, bq_ref, k_raw, v_raw, out_ref, own_ref, kall, vall) = refs[10:20]
+        rest = refs[20:]
+    (wo, wu, wd, part_ref, part2, d2d, mid, got, gath, gath2, sem_w,
      pair_s, pair_r, chip_s, chip_r, ag_s, ag_r, agp_s, agp_r) = rest
     n_batch, width = part_ref.shape
     n_chip = n_tp // 2
@@ -225,6 +218,8 @@
     def chip(d):
         return lax.rem(x + d, n_chip)
 
+    wo_copy = pltpu.make_async_copy(wo_hbm.at[layer], wo, sem_w.at[5])
+    wo_copy.start()
     w_copies = [pltpu.make_async_copy(wu_hbm.at[layer], wu, sem_w.at[0]), pltpu.make_async_copy(wd_hbm.at[layer], wd, sem_w.at[1])]
     if not last:
         w_copies.append(pltpu.make_async_copy(k_hbm.at[layer + 1], kall.at[layer + 1], sem_w.at[2]))
@@ -236,10 +231,13 @@
     peers = [partner] + [chip(d) * 2 + 1 - c for d in range(1, n_chip)]
     for peer in peers:
         pl.semaphore_signal(barrier, inc=1, device_id={'tp': peer}, device_id_type=MESH)
+    wo_copy.wait()
     for w in w_copies:
         w.start()
+    part_ref[...] = jnp.dot(attn_ref[...], wo[...], preferred_element_type=F32)
     pl.semaphore_wait(barrier, len(peers))
 
+    sent = []
     order = [2, 1, 3, 0] if n_chip == 4 else list(range(1, n_chip)) + [0]
 
     def rows_of(core, d):
@@ -266,9 +264,7 @@
         for d in sorted(hops, key=lambda d: min(d, n_chip - d)):
             hops[d].wait_recv()
             acc = got[phase, d] if acc is None else acc + got[phase, d]
-        for d in order:
-            pair[d].wait_send()
-            hops[d].wait_send()
+        sent.extend([*pair.values(), *hops.values()])
         return acc
 
     def all_gather(phase, buf, value):
@@ -294,9 +290,8 @@
             hops[d].wait_recv()
             passed.append(pass_on(d))
         for cp in passed:
-            cp.wait()
-        for d in hops:
-            hops[d].wait_send()
+            cp.wait_recv()
+        sent.extend([*passed, *hops.values()])
         return buf[...].astype(F32).reshape(n_batch, width)
 
     if last:
@@ -326,6 +321,8 @@
         out_ref[...] = qkv.astype(BF16).astype(F32)
         for w in w_copies[2:]:
             w.wait()
+    for cp in sent:
+        cp.wait_send()
 
 
 def solution(mesh):
@@ -357,7 +354,6 @@
                 pltpu.VMEM(key_pos.shape, jnp.int32),
                 pltpu.VMEM(key_valid.shape, jnp.int32),
                 pltpu.SMEM(write_slot.shape, jnp.int32),
-                pltpu.VMEM(w_out.shape[1:], BF16),
                 pltpu.VMEM((2, n_batch, n_cols), F32),
                 pltpu.VMEM((n_batch, n_local * head_dim), F32),
                 pltpu.SemaphoreType.DMA((5,)),
@@ -365,10 +361,10 @@
                 pltpu.SemaphoreType.DMA((4,)),
             ]
             alias = {}
-            part = jax.ShapeDtypeStruct((n_batch, width), F32)
+            part = jax.ShapeDtypeStruct((n_batch, n_local * head_dim), BF16)
             outs, out_specs = (part, shape, shape, held, held), (vm, hbm, hbm, vm, vm)
             if first:
-                ins = [in_hbm(a) for a in (x_in, ln_gain, ln_shift, b_qkv)] + [w_qkv, w_out] + shared + [k_in, v_in]
+                ins = [in_hbm(a) for a in (x_in, ln_gain, ln_shift, b_qkv)] + [w_qkv] + shared + [k_in, v_in]
                 specs = [hbm] * len(ins)
                 scratch += [
                     pltpu.VMEM(x_in.shape, BF16),
@@ -380,8 +376,8 @@
                     pltpu.SemaphoreType.DMA((2, n_groups)),
                 ]
             else:
-                ins = [x_in, w_out] + shared + list(caches)
-                specs = [vm, hbm] + [hbm] * len(shared) + [hbm] * 2 + [vm] * 2
+                ins = [x_in] + shared + list(caches)
+                specs = [vm] + [hbm] * len(shared) + [hbm] * 2 + [vm] * 2
                 alias = {len(ins) - 4 + i: 1 + i for i in range(4)}
             return pl.pallas_call(
                 functools.partial(attn_kernel, layer, n_local * tp_size, first),
@@ -390,14 +386,14 @@
                 out_specs=out_specs,
                 scratch_shapes=scratch,
                 input_output_aliases=alias,
-                compiler_params=pltpu.CompilerParams(vmem_limit_bytes=13 * MIB),
+                compiler_params=pltpu.CompilerParams(vmem_limit_bytes=14 * MIB),
                 name=f'attn_{layer}',
             )(*ins)
 
         def reduce(layer, part, res, caches=()):
             last = layer == n_layers - 1
-            ins = [part, res, ln_gain, ln_shift, b_out, w_up, b_up, w_down, b_down]
-            specs = [vm, vm, vm, vm, vm, hbm, vm, hbm, vm]
+            ins = [part, w_out, res, ln_gain, ln_shift, b_out, w_up, b_up, w_down, b_down]
+            specs = [vm, hbm, vm, vm, vm, vm, hbm, vm, hbm, vm]
             outs = [jax.ShapeDtypeStruct((n_batch, width), BF16)]
             if not last:
                 ins += [k_in, v_in, w_qkv, b_qkv, *caches]
@@ -411,8 +407,10 @@
                 in_specs=specs,
                 out_specs=tuple([vm] * len(outs)),
                 scratch_shapes=[
+                    pltpu.VMEM(w_out.shape[1:], BF16),
                     pltpu.VMEM(w_up.shape[1:], BF16),
                     pltpu.VMEM(w_down.shape[1:], BF16),
+                    pltpu.VMEM((n_batch, width), F32),
                     pltpu.VMEM((n_batch, width), F32),
                     pltpu.VMEM((2, n_chip, blk, width), F32),
                     pltpu.VMEM((2, n_chip, blk, width), F32),
@@ -422,7 +420,7 @@
                     pltpu.SemaphoreType.DMA((6,)),
                 ] + [dma] * 8,
                 input_output_aliases={} if last else {len(ins) - 2: 2, len(ins) - 1: 3},
-                compiler_params=pltpu.CompilerParams(vmem_limit_bytes=13 * MIB, collective_id=layer, has_side_effects=True),
+                compiler_params=pltpu.CompilerParams(vmem_limit_bytes=14 * MIB, collective_id=layer, has_side_effects=True),
                 name=f'reduce_{layer}',
             )(*ins)
 

time: 76.6 us -> 77.4 us (1.010)
  no operation moved by 1% of the time
where the time goes in v7:
time: 77.4 us; the launch traced here: 77.2 us
  Pallas kernels  75.7 us (98%)
    pallas_call x2, Pallas kernels, reduce(): pl.pallas_call(functools.partial(reduce_kernel, layer, tp_size, last), ou...  55.9 us
    pallas_call x2, Pallas kernels, attn(): pl.pallas_call(functools.partial(attn_kernel, layer, n_local * tp_size, f...  19.8 us

profile of v7, /device:TPU:113, one launch (start us, length us, event | category | flops | bytes accessed | tf_op | source)
XLA Modules:
  0.0 77.2 jit_solution(14929127314610139565)
XLA Ops:
  0.6 0.0 copy-start
  0.6 0.0 copy-start.1
  0.7 0.0 copy-start.2
  0.7 0.0 copy-start.3
  0.7 0.0 copy-start.4
  0.7 0.0 copy-start.5
  0.7 0.0 copy-start.6
  0.7 10.1 %attn_0.1 = (bf16[64,256]{1,0:T(8,128)(2,1)S(1)}, bf16[2,64,512,128]{3,2,1,0:T(8,128)(2,1)}, bf16[2,64,512,128]{3,2,1,0:T(8,128)(2,1)}, bf16[2,64,512,128]{3,2,1...) custom-call(bf16[64,2048]{1,0:T(8,128)(2,1)} %bitcast.6, bf16[2,2,2048]{2,1,0:T(2,128)(2,1)} %refs_3_.7, ...), custom_call_target="tpu_custom_call" | custom-call | tf_op jit(solution)/shard_map/attn_0/pallas_call | solution.py:382
  10.8 0.0 copy-done
  10.8 0.0 copy-done.1
  10.8 0.0 copy-done.2
  10.8 0.0 copy-done.3
  10.8 0.0 copy-done.4
  10.8 0.0 copy-done.5
  10.8 0.0 copy-done.6
  10.8 29.7 %reduce_0.1 = (f32[64,768]{1,0:T(8,128)S(1)}, bf16[8,2048]{1,0:T(8,128)(2,1)S(1)}, bf16[2,64,512,128]{3,2,1,0:T(8,128)(2,1)S(1)}, bf16[2,64,512,128]{3,2,1,0:T(8,128)(2,1)S(1)}) custom-call(bf16[64,256]{1,0:T(8,128)(2,1)S(1)} %get-tuple-element.15.refs_0_, bf16[2,256,2048]{2,1,0:T(8,128)(2,1)} %refs_1_.7, ...), custom_call_target="tpu_custom_call", output_to_operand_aliasing={{2}: (14, {}), {3}: (15, {})} | custom-call | tf_op jit(solution)/shard_map/reduce_0/pallas_call | solution.py:404
  40.6 9.7 %attn_1.1 = (bf16[64,256]{1,0:T(8,128)(2,1)S(1)}, bf16[2,64,512,128]{3,2,1,0:T(8,128)(2,1)}, bf16[2,64,512,128]{3,2,1,0:T(8,128)(2,1)}, bf16[2,64,512,128]{3,2,1...) custom-call(f32[64,768]{1,0:T(8,128)S(1)} %get-tuple-element.18.refs, ...), custom_call_target="tpu_custom_call", output_to_operand_aliasing={{1}: (4, {}), {2}: (5, {}), {3}: (6, {}), {4}: (7, {})} | custom-call | tf_op jit(solution)/shard_map/attn_1/pallas_call | solution.py:382
  50.3 26.2 %reduce_1.1 = bf16[64,2048]{1,0:T(8,128)(2,1)S(1)} custom-call(bf16[64,256]{1,0:T(8,128)(2,1)S(1)} %get-tuple-element.23.refs_0_, bf16[2,256,2048]{2,1,0:T(8,128)(2,1)} %refs_1_.7, bf16[8,2048]{1,0:T(8,128)(2,1)S(1)} %get-tuple-element.24.refs_2_, bf16[2,2,2048]{2,1,0:T(2,128)(2,1)S(1)} %copy-done.1, bf16[2,2,2048]{2,1,0:T(2,128)(2,1)S(1)} %copy-done.2, ...), custom_call_target="tpu_custom_call" | custom-call | tf_op jit(solution)/shard_map/reduce_1/pallas_call | solution.py:404
  76.5 0.7 copy.32
Async XLA Ops:
  0.6 10.1 %copy-start = (bf16[64,1,2048]{2,0,1:T(8,128)(2,1)S(1)}, bf16[64,1,2048]{2,0,1:T(8,128)(2,1)}, u32[]{:S(2)}) copy-start(bf16[64,1,2048]{2,0,1:T(8,128)(2,1)} %param.16) | copy-start | bytes 786436
  0.6 10.1 %copy-start.1 = (bf16[2,2,2048]{2,1,0:T(2,128)(2,1)S(1)}, bf16[2,2,2048]{2,1,0:T(2,128)(2,1)}, u32[]{:S(2)}) copy-start(bf16[2,2,2048]{2,1,0:T(2,128)(2,1)} %refs_3_.7) | copy-start | bytes 49156
  0.7 10.1 %copy-start.2 = (bf16[2,2,2048]{2,1,0:T(2,128)(2,1)S(1)}, bf16[2,2,2048]{2,1,0:T(2,128)(2,1)}, u32[]{:S(2)}) copy-start(bf16[2,2,2048]{2,1,0:T(2,128)(2,1)} %refs_4_.5) | copy-start | bytes 49156
  0.7 10.1 %copy-start.3 = (bf16[2,2048]{1,0:T(2,128)(2,1)S(1)}, bf16[2,2048]{1,0:T(2,128)(2,1)}, u32[]{:S(2)}) copy-start(bf16[2,2048]{1,0:T(2,128)(2,1)} %refs_5_.5) | copy-start | bytes 24580
  0.7 10.1 %copy-start.4 = (bf16[2,2048]{1,0:T(2,128)(2,1)S(1)}, bf16[2,2048]{1,0:T(2,128)(2,1)}, u32[]{:S(2)}) copy-start(bf16[2,2048]{1,0:T(2,128)(2,1)} %refs_9_.3) | copy-start | bytes 24580
  0.7 10.1 %copy-start.5 = (bf16[2,1024]{1,0:T(2,128)(2,1)S(1)}, bf16[2,1024]{1,0:T(2,128)(2,1)}, u32[]{:S(2)}) copy-start(bf16[2,1024]{1,0:T(2,128)(2,1)} %refs_7_.5) | copy-start | bytes 12292
  0.7 10.1 %copy-start.6 = (bf16[2,768]{1,0:T(2,128)(2,1)S(1)}, bf16[2,768]{1,0:T(2,128)(2,1)}, u32[]{:S(2)}) copy-start(bf16[2,768]{1,0:T(2,128)(2,1)} %refs_13_.1) | copy-start | bytes 9220

commit v8 on v5

--- a/solution.py
+++ b/solution.py
@@ -240,6 +240,7 @@
         w.start()
     pl.semaphore_wait(barrier, len(peers))
 
+    sent = []
     order = [2, 1, 3, 0] if n_chip == 4 else list(range(1, n_chip)) + [0]
 
     def rows_of(core, d):
@@ -266,9 +267,7 @@
         for d in sorted(hops, key=lambda d: min(d, n_chip - d)):
             hops[d].wait_recv()
             acc = got[phase, d] if acc is None else acc + got[phase, d]
-        for d in order:
-            pair[d].wait_send()
-            hops[d].wait_send()
+        sent.extend([*pair.values(), *hops.values()])
         return acc
 
     def all_gather(phase, buf, value):
@@ -294,9 +293,8 @@
             hops[d].wait_recv()
             passed.append(pass_on(d))
         for cp in passed:
-            cp.wait()
-        for d in hops:
-            hops[d].wait_send()
+            cp.wait_recv()
+        sent.extend([*passed, *hops.values()])
         return buf[...].astype(F32).reshape(n_batch, width)
 
     if last:
@@ -326,6 +324,8 @@
         out_ref[...] = qkv.astype(BF16).astype(F32)
         for w in w_copies[2:]:
             w.wait()
+    for cp in sent:
+        cp.wait_send()
 
 
 def solution(mesh):

time: 76.6 us -> 76.6 us (level)
  no operation moved by 1% of the time
where the time goes in v8:
time: 76.6 us; the launch traced here: 76.5 us
  Pallas kernels  75 us (98%)
  between operations  0.77 us (1%)
    pallas_call x2, Pallas kernels, reduce(): pl.pallas_call(functools.partial(reduce_kernel, layer, tp_size, last), ou...  55.1 us
    pallas_call x2, Pallas kernels, attn(): pl.pallas_call(functools.partial(attn_kernel, layer, n_local * tp_size, f...  19.8 us

profile of v8, /device:TPU:113, one launch (start us, length us, event | category | flops | bytes accessed | tf_op | source)
XLA Modules:
  0.0 76.5 jit_solution(11819489379720987386)
XLA Ops:
  0.6 0.0 copy-start
  0.6 0.0 copy-start.1
  0.7 0.0 copy-start.2
  0.7 0.0 copy-start.3
  0.7 0.0 copy-start.4
  0.7 0.0 copy-start.5
  0.7 0.0 copy-start.6
  0.7 10.1 %attn_0.1 = (f32[64,2048]{1,0:T(8,128)S(1)}, bf16[2,64,512,128]{3,2,1,0:T(8,128)(2,1)}, bf16[2,64,512,128]{3,2,1,0:T(8,128)(2,1)}, bf16[2,64,512,128]{3,2,1,0:T(8,128)(2,1)S(1)}, bf16[2,64,512,128]{3,2,1,0:T(8,128)(2,1)S(1)}) custom-call(bf16[64,2048]{1,0:T(8,128)(2,1)} %bitcast.6, bf16[2,2,2048]{2,1,0:T(2,128)(2,1)} %refs_2_.7, ...), custom_call_target="tpu_custom_call" | custom-call | tf_op jit(solution)/shard_map/attn_0/pallas_call | solution.py:386
  10.8 0.0 copy-done
  10.8 0.0 copy-done.1
  10.8 0.0 copy-done.2
  10.8 0.0 copy-done.3
  10.8 0.0 copy-done.4
  10.8 0.0 copy-done.5
  10.8 0.0 copy-done.6
  10.9 29.5 %reduce_0.1 = (f32[64,768]{1,0:T(8,128)S(1)}, bf16[8,2048]{1,0:T(8,128)(2,1)S(1)}, bf16[2,64,512,128]{3,2,1,0:T(8,128)(2,1)S(1)}, bf16[2,64,512,128]{3,2,1,0:T(8,128)(2,1)S(1)}) custom-call(f32[64,2048]{1,0:T(8,128)S(1)} %get-tuple-element.15.refs_0_, bf16[64,2048]{1,0:T(8,128)(2,1)S(1)} %bitcast.7, ...), custom_call_target="tpu_custom_call", output_to_operand_aliasing={{2}: (13, {}), {3}: (14, {})} | custom-call | tf_op jit(solution)/shard_map/reduce_0/pallas_call | solution.py:408
  40.4 9.7 %attn_1.1 = (f32[64,2048]{1,0:T(8,128)S(1)}, bf16[2,64,512,128]{3,2,1,0:T(8,128)(2,1)}, bf16[2,64,512,128]{3,2,1,0:T(8,128)(2,1)}, bf16[2,64,512,128]{3,2,1,0:T(8,128)(2,1)S(1)}, bf16[2,64,512,128]{3,2,1,0:T(8,128)(2,1)S(1)}) custom-call(f32[64,768]{1,0:T(8,128)S(1)} %get-tuple-element.18.refs, ...), custom_call_target="tpu_custom_call", output_to_operand_aliasing={{1}: (5, {}), {2}: (6, {}), {3}: (7, {}), {4}: (8, {})} | custom-call | tf_op jit(solution)/shard_map/attn_1/pallas_call | solution.py:386
  50.1 25.6 %reduce_1.1 = bf16[64,2048]{1,0:T(8,128)(2,1)S(1)} custom-call(f32[64,2048]{1,0:T(8,128)S(1)} %get-tuple-element.23.refs_0_, bf16[8,2048]{1,0:T(8,128)(2,1)S(1)} %get-tuple-element.24.refs_1_, bf16[2,2,2048]{2,1,0:T(2,128)(2,1)S(1)} %copy-done.1, bf16[2,2,2048]{2,1,0:T(2,128)(2,1)S(1)} %copy-done.2, bf16[2,2048]{1,0:T(2,128)(2,1)S(1)} %copy-done.3, ...), custom_call_target="tpu_custom_call" | custom-call | tf_op jit(solution)/shard_map/reduce_1/pallas_call | solution.py:408
  75.8 0.7 copy.32
Async XLA Ops:
  0.6 10.2 %copy-start = (bf16[64,1,2048]{2,0,1:T(8,128)(2,1)S(1)}, bf16[64,1,2048]{2,0,1:T(8,128)(2,1)}, u32[]{:S(2)}) copy-start(bf16[64,1,2048]{2,0,1:T(8,128)(2,1)} %param.16) | copy-start | bytes 786436
  0.6 10.2 %copy-start.1 = (bf16[2,2,2048]{2,1,0:T(2,128)(2,1)S(1)}, bf16[2,2,2048]{2,1,0:T(2,128)(2,1)}, u32[]{:S(2)}) copy-start(bf16[2,2,2048]{2,1,0:T(2,128)(2,1)} %refs_2_.7) | copy-start | bytes 49156
  0.7 10.2 %copy-start.2 = (bf16[2,2,2048]{2,1,0:T(2,128)(2,1)S(1)}, bf16[2,2,2048]{2,1,0:T(2,128)(2,1)}, u32[]{:S(2)}) copy-start(bf16[2,2,2048]{2,1,0:T(2,128)(2,1)} %refs_3_.7) | copy-start | bytes 49156
  0.7 10.2 %copy-start.3 = (bf16[2,2048]{1,0:T(2,128)(2,1)S(1)}, bf16[2,2048]{1,0:T(2,128)(2,1)}, u32[]{:S(2)}) copy-start(bf16[2,2048]{1,0:T(2,128)(2,1)} %refs_4_.7) | copy-start | bytes 24580
  0.7 10.2 %copy-start.4 = (bf16[2,2048]{1,0:T(2,128)(2,1)S(1)}, bf16[2,2048]{1,0:T(2,128)(2,1)}, u32[]{:S(2)}) copy-start(bf16[2,2048]{1,0:T(2,128)(2,1)} %refs_8_.5) | copy-start | bytes 24580
  0.7 10.2 %copy-start.5 = (bf16[2,1024]{1,0:T(2,128)(2,1)S(1)}, bf16[2,1024]{1,0:T(2,128)(2,1)}, u32[]{:S(2)}) copy-start(bf16[2,1024]{1,0:T(2,128)(2,1)} %refs_6_.5) | copy-start | bytes 12292
  0.7 10.2 %copy-start.6 = (bf16[2,768]{1,0:T(2,128)(2,1)S(1)}, bf16[2,768]{1,0:T(2,128)(2,1)}, u32[]{:S(2)}) copy-start(bf16[2,768]{1,0:T(2,128)(2,1)} %refs_12_.1) | copy-start | bytes 9220

commit v9 on v8

--- a/solution.py
+++ b/solution.py
@@ -15,7 +15,7 @@
 GROUP = 8
 AHEAD = 6
 SUB = 2
-EARLY = 2
+EARLY = 4
 MIB = 2 ** 20
 
 
@@ -180,9 +180,10 @@
             def _():
                 wo_copy.start()
 
-            @pl.when(i == n_groups // SUB - 1)
+            @pl.when(i >= (n_groups - EARLY) // SUB)
             def _():
-                for g in range(EARLY):
+                for j in range(SUB):
+                    g = i * SUB + j - (n_groups - EARLY)
                     out_copy(0, g).start()
                     out_copy(1, g).start()
         state = [update(g) for g in todo]

time: 76.6 us -> 75.6 us (0.987)
  Pallas kernels: 75 us -> 73.9 us
    pallas_call x2, Pallas kernels: 19.8 us -> 18.8 us  [attn(): pl.pallas_call(functools.partial(attn_kernel, layer, n_local * tp_size, f...]
where the time goes in v9:
time: 75.6 us; the launch traced here: 75.5 us
  Pallas kernels  73.9 us (98%)
  between operations  0.77 us (1%)
    pallas_call x2, Pallas kernels, reduce(): pl.pallas_call(functools.partial(reduce_kernel, layer, tp_size, last), ou...  55.1 us
    pallas_call x2, Pallas kernels, attn(): pl.pallas_call(functools.partial(attn_kernel, layer, n_local * tp_size, f...  18.8 us

profile of v9, /device:TPU:113, one launch (start us, length us, event | category | flops | bytes accessed | tf_op | source)
XLA Modules:
  0.0 75.5 jit_solution(5605039447831811417)
XLA Ops:
  0.6 0.0 copy-start
  0.6 0.0 copy-start.1
  0.7 0.0 copy-start.2
  0.7 0.0 copy-start.3
  0.7 0.0 copy-start.4
  0.7 0.0 copy-start.5
  0.7 0.0 copy-start.6
  0.7 10.3 %attn_0.1 = (f32[64,2048]{1,0:T(8,128)S(1)}, bf16[2,64,512,128]{3,2,1,0:T(8,128)(2,1)}, bf16[2,64,512,128]{3,2,1,0:T(8,128)(2,1)}, bf16[2,64,512,128]{3,2,1,0:T(8,128)(2,1)S(1)}, bf16[2,64,512,128]{3,2,1,0:T(8,128)(2,1)S(1)}) custom-call(bf16[64,2048]{1,0:T(8,128)(2,1)} %bitcast.6, bf16[2,2,2048]{2,1,0:T(2,128)(2,1)} %refs_2_.7, ...), custom_call_target="tpu_custom_call" | custom-call | tf_op jit(solution)/shard_map/attn_0/pallas_call | solution.py:387
  11.0 0.0 copy-done
  11.0 0.0 copy-done.1
  11.0 0.0 copy-done.2
  11.1 0.0 copy-done.3
  11.1 0.0 copy-done.4
  11.1 0.0 copy-done.5
  11.1 0.0 copy-done.6
  11.1 29.5 %reduce_0.1 = (f32[64,768]{1,0:T(8,128)S(1)}, bf16[8,2048]{1,0:T(8,128)(2,1)S(1)}, bf16[2,64,512,128]{3,2,1,0:T(8,128)(2,1)S(1)}, bf16[2,64,512,128]{3,2,1,0:T(8,128)(2,1)S(1)}) custom-call(f32[64,2048]{1,0:T(8,128)S(1)} %get-tuple-element.15.refs_0_, bf16[64,2048]{1,0:T(8,128)(2,1)S(1)} %bitcast.7, ...), custom_call_target="tpu_custom_call", output_to_operand_aliasing={{2}: (13, {}), {3}: (14, {})} | custom-call | tf_op jit(solution)/shard_map/reduce_0/pallas_call | solution.py:409
  40.6 8.5 %attn_1.1 = (f32[64,2048]{1,0:T(8,128)S(1)}, bf16[2,64,512,128]{3,2,1,0:T(8,128)(2,1)}, bf16[2,64,512,128]{3,2,1,0:T(8,128)(2,1)}, bf16[2,64,512,128]{3,2,1,0:T(8,128)(2,1)S(1)}, bf16[2,64,512,128]{3,2,1,0:T(8,128)(2,1)S(1)}) custom-call(f32[64,768]{1,0:T(8,128)S(1)} %get-tuple-element.18.refs, ...), custom_call_target="tpu_custom_call", output_to_operand_aliasing={{1}: (5, {}), {2}: (6, {}), {3}: (7, {}), {4}: (8, {})} | custom-call | tf_op jit(solution)/shard_map/attn_1/pallas_call | solution.py:387
  49.1 25.6 %reduce_1.1 = bf16[64,2048]{1,0:T(8,128)(2,1)S(1)} custom-call(f32[64,2048]{1,0:T(8,128)S(1)} %get-tuple-element.23.refs_0_, bf16[8,2048]{1,0:T(8,128)(2,1)S(1)} %get-tuple-element.24.refs_1_, bf16[2,2,2048]{2,1,0:T(2,128)(2,1)S(1)} %copy-done.1, bf16[2,2,2048]{2,1,0:T(2,128)(2,1)S(1)} %copy-done.2, bf16[2,2048]{1,0:T(2,128)(2,1)S(1)} %copy-done.3, ...), custom_call_target="tpu_custom_call" | custom-call | tf_op jit(solution)/shard_map/reduce_1/pallas_call | solution.py:409
  74.7 0.7 copy.32
Async XLA Ops:
  0.6 10.4 %copy-start = (bf16[64,1,2048]{2,0,1:T(8,128)(2,1)S(1)}, bf16[64,1,2048]{2,0,1:T(8,128)(2,1)}, u32[]{:S(2)}) copy-start(bf16[64,1,2048]{2,0,1:T(8,128)(2,1)} %param.16) | copy-start | bytes 786436
  0.6 10.4 %copy-start.1 = (bf16[2,2,2048]{2,1,0:T(2,128)(2,1)S(1)}, bf16[2,2,2048]{2,1,0:T(2,128)(2,1)}, u32[]{:S(2)}) copy-start(bf16[2,2,2048]{2,1,0:T(2,128)(2,1)} %refs_2_.7) | copy-start | bytes 49156
  0.7 10.4 %copy-start.2 = (bf16[2,2,2048]{2,1,0:T(2,128)(2,1)S(1)}, bf16[2,2,2048]{2,1,0:T(2,128)(2,1)}, u32[]{:S(2)}) copy-start(bf16[2,2,2048]{2,1,0:T(2,128)(2,1)} %refs_3_.7) | copy-start | bytes 49156
  0.7 10.4 %copy-start.3 = (bf16[2,2048]{1,0:T(2,128)(2,1)S(1)}, bf16[2,2048]{1,0:T(2,128)(2,1)}, u32[]{:S(2)}) copy-start(bf16[2,2048]{1,0:T(2,128)(2,1)} %refs_4_.7) | copy-start | bytes 24580
  0.7 10.4 %copy-start.4 = (bf16[2,2048]{1,0:T(2,128)(2,1)S(1)}, bf16[2,2048]{1,0:T(2,128)(2,1)}, u32[]{:S(2)}) copy-start(bf16[2,2048]{1,0:T(2,128)(2,1)} %refs_8_.5) | copy-start | bytes 24580
  0.7 10.4 %copy-start.5 = (bf16[2,1024]{1,0:T(2,128)(2,1)S(1)}, bf16[2,1024]{1,0:T(2,128)(2,1)}, u32[]{:S(2)}) copy-start(bf16[2,1024]{1,0:T(2,128)(2,1)} %refs_6_.5) | copy-start | bytes 12292
  0.7 10.4 %copy-start.6 = (bf16[2,768]{1,0:T(2,128)(2,1)S(1)}, bf16[2,768]{1,0:T(2,128)(2,1)}, u32[]{:S(2)}) copy-start(bf16[2,768]{1,0:T(2,128)(2,1)} %refs_12_.1) | copy-start | bytes 9220

commit v10 on v9

--- a/solution.py
+++ b/solution.py
@@ -237,7 +237,7 @@
     peers = [partner] + [chip(d) * 2 + 1 - c for d in range(1, n_chip)]
     for peer in peers:
         pl.semaphore_signal(barrier, inc=1, device_id={'tp': peer}, device_id_type=MESH)
-    for w in w_copies:
+    for w in w_copies[:2]:
         w.start()
     pl.semaphore_wait(barrier, len(peers))
 
@@ -247,81 +247,107 @@
     def rows_of(core, d):
         return pl.ds(pl.multiple_of((core * n_chip + chip(d)) * blk, blk), blk)
 
-    def reduce_scatter(phase, src):
-        pair = {
-            d: pltpu.make_async_remote_copy(
-                src_ref=src.at[rows_of(1 - c, d)], dst_ref=d2d.at[phase, d], send_sem=pair_s.at[phase, d],
-                recv_sem=pair_r.at[phase, d], device_id={'tp': partner}, device_id_type=MESH)
-            for d in order
-        }
-        for d in order:
-            pair[d].start()
-        hops = {}
-        for d in order:
-            pair[d].wait_recv()
-            mid[phase, d] = src[rows_of(c, d), :] + d2d[phase, d]
-            hops[d] = pltpu.make_async_remote_copy(
-                src_ref=mid.at[phase, d], dst_ref=got.at[phase, d], send_sem=chip_s.at[phase, d],
-                recv_sem=chip_r.at[phase, d], device_id={'tp': chip(d) * 2 + 1 - c}, device_id_type=MESH)
-            hops[d].start()
-        acc = None
-        for d in sorted(hops, key=lambda d: min(d, n_chip - d)):
-            hops[d].wait_recv()
-            acc = got[phase, d] if acc is None else acc + got[phase, d]
-        sent.extend([*pair.values(), *hops.values()])
-        return acc
-
-    def all_gather(phase, buf, value):
+    far = order[:-1]
+    by_distance = sorted(order, key=lambda d: min(d, n_chip - d))
+
+    def remote(src, dst, send_sem, recv_sem, to):
+        return pltpu.make_async_remote_copy(src_ref=src, dst_ref=dst, send_sem=send_sem, recv_sem=recv_sem, device_id={'tp': to}, device_id_type=MESH)
+
+    def reduce_scatter(phase, src, fills):
+        part = width // len(fills)
+        pair, hops = [], []
+        for k, fill in enumerate(fills):
+            sem, cols = phase + k, pl.ds(k * part, part)
+            if fill is not None:
+                fill(k * part, part)
+            pair.append({
+                d: remote(src.at[rows_of(1 - c, d), cols], d2d.at[phase, d, :, cols], pair_s.at[sem, d], pair_r.at[sem, d], partner)
+                for d in order
+            })
+            for d in order:
+                pair[k][d].start()
+        for k in range(len(fills)):
+            sem, cols = phase + k, pl.ds(k * part, part)
+            hops.append({})
+            for d in order:
+                pair[k][d].wait_recv()
+                mid[phase, d, :, cols] = src[rows_of(c, d), cols] + d2d[phase, d, :, cols]
+                hops[k][d] = remote(mid.at[phase, d, :, cols], got.at[phase, d, :, cols], chip_s.at[sem, d], chip_r.at[sem, d], chip(d) * 2 + 1 - c)
+                hops[k][d].start()
+        sums = []
+        for k in range(len(fills)):
+            acc = None
+            for d in by_distance:
+                hops[k][d].wait_recv()
+                term = got[phase, d, :, pl.ds(k * part, part)]
+                acc = term if acc is None else acc + term
+            sums.append(acc)
+            sent.extend([*pair[k].values(), *hops[k].values()])
+        return sums[0] if len(sums) == 1 else jnp.concatenate(sums, axis=1)
+
+    def all_gather(phase, buf, value, parts, consume):
         buf[1 - c, x] = value
-        hops = {}
-        for d in order[:-1]:
-            hops[d] = pltpu.make_async_remote_copy(
-                src_ref=buf.at[1 - c, x], dst_ref=buf.at[1 - c, x], send_sem=ag_s.at[phase, d], recv_sem=ag_r.at[phase, d],
-                device_id={'tp': chip(d) * 2 + 1 - c}, device_id_type=MESH)
-            hops[d].start()
-
-        def pass_on(d):
+        part = width // parts
+
+        def pass_on(k, d):
             slot = lax.rem(x + n_chip - d, n_chip)
-            half = 1 - c if d == 0 else c
-            cp = pltpu.make_async_remote_copy(
-                src_ref=buf.at[half, slot], dst_ref=buf.at[half, slot], send_sem=agp_s.at[phase, d], recv_sem=agp_r.at[phase, d],
-                device_id={'tp': partner}, device_id_type=MESH)
-            cp.start()
-            return cp
-
-        passed = [pass_on(0)]
-        for d in sorted(hops, key=lambda d: min(d, n_chip - d)):
-            hops[d].wait_recv()
-            passed.append(pass_on(d))
-        for cp in passed:
-            cp.wait_recv()
-        sent.extend([*passed, *hops.values()])
-        return buf[...].astype(F32).reshape(n_batch, width)
+            ref = buf.at[c if d else 1 - c, slot, :, pl.ds(k * part, part)]
+            return remote(ref, ref, agp_s.at[phase + k, d], agp_r.at[phase + k, d], partner)
+
+        hops, passed = [], []
+        for k in range(parts):
+            ref = buf.at[1 - c, x, :, pl.ds(k * part, part)]
+            hops.append({d: remote(ref, ref, ag_s.at[phase + k, d], ag_r.at[phase + k, d], chip(d) * 2 + 1 - c) for d in far})
+            for d in far:
+                hops[k][d].start()
+            passed.append([pass_on(k, 0)])
+            passed[k][0].start()
+        for k in range(parts):
+            for d in by_distance[1:]:
+                hops[k][d].wait_recv()
+                passed[k].append(pass_on(k, d))
+                passed[k][-1].start()
+        out = None
+        for k in range(parts):
+            for cp in passed[k]:
+                cp.wait_recv()
+            rows = buf[:, :, :, k * part:(k + 1) * part].astype(F32).reshape(n_batch, part).astype(BF16)
+            term = consume(k * part, part, rows)
+            out = term if out is None else out + term
+            sent.extend([*passed[k], *hops[k].values()])
+        return out
+
+    def product(ref, n_cols):
+        return lambda lo, size, rows: jnp.dot(rows, ref[lo:lo + size, :n_cols], preferred_element_type=F32)
 
     if last:
         res = res_ref[...].astype(F32)
     else:
         res = res_ref[rows_of(1 - c, 0), :].astype(F32)
-    total = reduce_scatter(0, part_ref)
+    total = reduce_scatter(0, part_ref, [None])
+    for w in w_copies[2:]:
+        w.start()
     x_mid = (res + total + bo_ref[layer:layer + 1].astype(F32)).astype(BF16).astype(F32)
-    normed = all_gather(0, gath, layer_norm_f32(x_mid, gain_ref[layer, 1:2], shift_ref[layer, 1:2])).astype(BF16)
     w_copies[0].wait()
-    up = jnp.dot(normed, wu[...], preferred_element_type=F32) + bu_ref[layer:layer + 1].astype(F32)
+    normed = layer_norm_f32(x_mid, gain_ref[layer, 1:2], shift_ref[layer, 1:2])
+    up = all_gather(0, gath, normed, 2, product(wu, wu.shape[1])) + bu_ref[layer:layer + 1].astype(F32)
     act = jax.nn.gelu(up, approximate=True).astype(BF16)
     if not last:
         wq_copy.start()
     w_copies[1].wait()
-    part2[...] = jnp.dot(act, wd[...], preferred_element_type=F32)
-    total = reduce_scatter(1, part2)
+
+    def down(lo, size):
+        part2[:, lo:lo + size] = jnp.dot(act, wd[:, lo:lo + size], preferred_element_type=F32)
+
+    total = reduce_scatter(1, part2, [down, down])
     x_next = (x_mid + total + bd_ref[layer:layer + 1].astype(F32)).astype(BF16)
     if last:
-        out_ref[...] = all_gather(1, gath2, x_next).astype(BF16)
+        out_ref[...] = all_gather(2, gath2, x_next, 1, lambda lo, size, rows: rows)
     else:
         own_ref[...] = x_next
         nxt = layer_norm_f32(x_next.astype(F32), gain_ref[layer + 1, 0:1], shift_ref[layer + 1, 0:1])
-        normed = all_gather(1, gath2, nxt).astype(BF16)
         wq_copy.wait()
-        qkv = jnp.dot(normed, wu[:, :n_qkv], preferred_element_type=F32) + bq_ref[layer + 1:layer + 2].astype(F32)
+        qkv = all_gather(2, gath2, nxt, 2, product(wu, n_qkv)) + bq_ref[layer + 1:layer + 2].astype(F32)
         out_ref[...] = qkv.astype(BF16).astype(F32)
         for w in w_copies[2:]:
             w.wait()
@@ -405,7 +431,7 @@
                 specs += [hbm, hbm, hbm, vm, vm, vm]
                 outs = [jax.ShapeDtypeStruct((n_batch, b_qkv.shape[1]), F32)]
                 outs += [jax.ShapeDtypeStruct((blk, width), BF16), held, held]
-            dma = pltpu.SemaphoreType.DMA((2, n_chip))
+            dma = pltpu.SemaphoreType.DMA((4, n_chip))
             return pl.pallas_call(
                 functools.partial(reduce_kernel, layer, tp_size, last),
                 out_shape=tuple(outs),

time: 75.6 us -> 76.5 us (1.012)
  Pallas kernels: 73.9 us -> 74.8 us
    pallas_call x2, Pallas kernels: 55.1 us -> 56 us  [reduce(): pl.pallas_call(functools.partial(reduce_kernel, layer, tp_size, last), ou...]
where the time goes in v10:
time: 76.5 us; the launch traced here: 76.3 us
  Pallas kernels  74.8 us (98%)
  between operations  0.77 us (1%)
    pallas_call x2, Pallas kernels, reduce(): pl.pallas_call(functools.partial(reduce_kernel, layer, tp_size, last), ou...  56 us
    pallas_call x2, Pallas kernels, attn(): pl.pallas_call(functools.partial(attn_kernel, layer, n_local * tp_size, f...  18.8 us

profile of v10, /device:TPU:113, one launch (start us, length us, event | category | flops | bytes accessed | tf_op | source)
XLA Modules:
  0.0 76.3 jit_solution(4311041477626000951)
XLA Ops:
  0.6 0.0 copy-start
  0.6 0.0 copy-start.1
  0.7 0.0 copy-start.2
  0.7 0.0 copy-start.3
  0.7 0.0 copy-start.4
  0.7 0.0 copy-start.5
  0.7 0.0 copy-start.6
  0.7 10.3 %attn_0.1 = (f32[64,2048]{1,0:T(8,128)S(1)}, bf16[2,64,512,128]{3,2,1,0:T(8,128)(2,1)}, bf16[2,64,512,128]{3,2,1,0:T(8,128)(2,1)}, bf16[2,64,512,128]{3,2,1,0:T(8,128)(2,1)S(1)}, bf16[2,64,512,128]{3,2,1,0:T(8,128)(2,1)S(1)}) custom-call(bf16[64,2048]{1,0:T(8,128)(2,1)} %bitcast.6, bf16[2,2,2048]{2,1,0:T(2,128)(2,1)} %refs_2_.7, ...), custom_call_target="tpu_custom_call" | custom-call | tf_op jit(solution)/shard_map/attn_0/pallas_call | solution.py:413
  11.0 0.0 copy-done
  11.0 0.0 copy-done.1
  11.0 0.0 copy-done.2
  11.1 0.0 copy-done.3
  11.1 0.0 copy-done.4
  11.1 0.0 copy-done.5
  11.1 0.0 copy-done.6
  11.1 29.6 %reduce_0.1 = (f32[64,768]{1,0:T(8,128)S(1)}, bf16[8,2048]{1,0:T(8,128)(2,1)S(1)}, bf16[2,64,512,128]{3,2,1,0:T(8,128)(2,1)S(1)}, bf16[2,64,512,128]{3,2,1,0:T(8,128)(2,1)S(1)}) custom-call(f32[64,2048]{1,0:T(8,128)S(1)} %get-tuple-element.15.refs_0_, bf16[64,2048]{1,0:T(8,128)(2,1)S(1)} %bitcast.7, ...), custom_call_target="tpu_custom_call", output_to_operand_aliasing={{2}: (13, {}), {3}: (14, {})} | custom-call | tf_op jit(solution)/shard_map/reduce_0/pallas_call | solution.py:435
  40.7 8.5 %attn_1.1 = (f32[64,2048]{1,0:T(8,128)S(1)}, bf16[2,64,512,128]{3,2,1,0:T(8,128)(2,1)}, bf16[2,64,512,128]{3,2,1,0:T(8,128)(2,1)}, bf16[2,64,512,128]{3,2,1,0:T(8,128)(2,1)S(1)}, bf16[2,64,512,128]{3,2,1,0:T(8,128)(2,1)S(1)}) custom-call(f32[64,768]{1,0:T(8,128)S(1)} %get-tuple-element.18.refs, ...), custom_call_target="tpu_custom_call", output_to_operand_aliasing={{1}: (5, {}), {2}: (6, {}), {3}: (7, {}), {4}: (8, {})} | custom-call | tf_op jit(solution)/shard_map/attn_1/pallas_call | solution.py:413
  49.2 26.5 %reduce_1.1 = bf16[64,2048]{1,0:T(8,128)(2,1)S(1)} custom-call(f32[64,2048]{1,0:T(8,128)S(1)} %get-tuple-element.23.refs_0_, bf16[8,2048]{1,0:T(8,128)(2,1)S(1)} %get-tuple-element.24.refs_1_, bf16[2,2,2048]{2,1,0:T(2,128)(2,1)S(1)} %copy-done.1, bf16[2,2,2048]{2,1,0:T(2,128)(2,1)S(1)} %copy-done.2, bf16[2,2048]{1,0:T(2,128)(2,1)S(1)} %copy-done.3, ...), custom_call_target="tpu_custom_call" | custom-call | tf_op jit(solution)/shard_map/reduce_1/pallas_call | solution.py:435
  75.6 0.7 copy.32
Async XLA Ops:
  0.6 10.4 %copy-start = (bf16[64,1,2048]{2,0,1:T(8,128)(2,1)S(1)}, bf16[64,1,2048]{2,0,1:T(8,128)(2,1)}, u32[]{:S(2)}) copy-start(bf16[64,1,2048]{2,0,1:T(8,128)(2,1)} %param.16) | copy-start | bytes 786436
  0.6 10.4 %copy-start.1 = (bf16[2,2,2048]{2,1,0:T(2,128)(2,1)S(1)}, bf16[2,2,2048]{2,1,0:T(2,128)(2,1)}, u32[]{:S(2)}) copy-start(bf16[2,2,2048]{2,1,0:T(2,128)(2,1)} %refs_2_.7) | copy-start | bytes 49156
  0.7 10.4 %copy-start.2 = (bf16[2,2,2048]{2,1,0:T(2,128)(2,1)S(1)}, bf16[2,2,2048]{2,1,0:T(2,128)(2,1)}, u32[]{:S(2)}) copy-start(bf16[2,2,2048]{2,1,0:T(2,128)(2,1)} %refs_3_.7) | copy-start | bytes 49156
  0.7 10.4 %copy-start.3 = (bf16[2,2048]{1,0:T(2,128)(2,1)S(1)}, bf16[2,2048]{1,0:T(2,128)(2,1)}, u32[]{:S(2)}) copy-start(bf16[2,2048]{1,0:T(2,128)(2,1)} %refs_4_.7) | copy-start | bytes 24580
  0.7 10.4 %copy-start.4 = (bf16[2,2048]{1,0:T(2,128)(2,1)S(1)}, bf16[2,2048]{1,0:T(2,128)(2,1)}, u32[]{:S(2)}) copy-start(bf16[2,2048]{1,0:T(2,128)(2,1)} %refs_8_.5) | copy-start | bytes 24580
  0.7 10.4 %copy-start.5 = (bf16[2,1024]{1,0:T(2,128)(2,1)S(1)}, bf16[2,1024]{1,0:T(2,128)(2,1)}, u32[]{:S(2)}) copy-start(bf16[2,1024]{1,0:T(2,128)(2,1)} %refs_6_.5) | copy-start | bytes 12292
  0.7 10.4 %copy-start.6 = (bf16[2,768]{1,0:T(2,128)(2,1)S(1)}, bf16[2,768]{1,0:T(2,128)(2,1)}, u32[]{:S(2)}) copy-start(bf16[2,768]{1,0:T(2,128)(2,1)} %refs_12_.1) | copy-start | bytes 9220

commit v11 on v10

--- a/solution.py
+++ b/solution.py
@@ -330,7 +330,7 @@
     x_mid = (res + total + bo_ref[layer:layer + 1].astype(F32)).astype(BF16).astype(F32)
     w_copies[0].wait()
     normed = layer_norm_f32(x_mid, gain_ref[layer, 1:2], shift_ref[layer, 1:2])
-    up = all_gather(0, gath, normed, 2, product(wu, wu.shape[1])) + bu_ref[layer:layer + 1].astype(F32)
+    up = all_gather(0, gath, normed, 1, product(wu, wu.shape[1])) + bu_ref[layer:layer + 1].astype(F32)
     act = jax.nn.gelu(up, approximate=True).astype(BF16)
     if not last:
         wq_copy.start()
@@ -347,7 +347,7 @@
         own_ref[...] = x_next
         nxt = layer_norm_f32(x_next.astype(F32), gain_ref[layer + 1, 0:1], shift_ref[layer + 1, 0:1])
         wq_copy.wait()
-        qkv = all_gather(2, gath2, nxt, 2, product(wu, n_qkv)) + bq_ref[layer + 1:layer + 2].astype(F32)
+        qkv = all_gather(2, gath2, nxt, 1, product(wu, n_qkv)) + bq_ref[layer + 1:layer + 2].astype(F32)
         out_ref[...] = qkv.astype(BF16).astype(F32)
         for w in w_copies[2:]:
             w.wait()

time: 76.5 us -> 76.7 us (level)
  no operation moved by 1% of the time
where the time goes in v11:
time: 76.7 us; the launch traced here: 76.5 us
  Pallas kernels  75 us (98%)
  between operations  0.77 us (1%)
    pallas_call x2, Pallas kernels, reduce(): pl.pallas_call(functools.partial(reduce_kernel, layer, tp_size, last), ou...  56.2 us
    pallas_call x2, Pallas kernels, attn(): pl.pallas_call(functools.partial(attn_kernel, layer, n_local * tp_size, f...  18.8 us

profile of v11, /device:TPU:113, one launch (start us, length us, event | category | flops | bytes accessed | tf_op | source)
XLA Modules:
  0.0 76.5 jit_solution(12887712645668056696)
XLA Ops:
  0.6 0.0 copy-start
  0.6 0.0 copy-start.1
  0.7 0.0 copy-start.2
  0.7 0.0 copy-start.3
  0.7 0.0 copy-start.4
  0.7 0.0 copy-start.5
  0.7 0.0 copy-start.6
  0.7 10.3 %attn_0.1 = (f32[64,2048]{1,0:T(8,128)S(1)}, bf16[2,64,512,128]{3,2,1,0:T(8,128)(2,1)}, bf16[2,64,512,128]{3,2,1,0:T(8,128)(2,1)}, bf16[2,64,512,128]{3,2,1,0:T(8,128)(2,1)S(1)}, bf16[2,64,512,128]{3,2,1,0:T(8,128)(2,1)S(1)}) custom-call(bf16[64,2048]{1,0:T(8,128)(2,1)} %bitcast.6, bf16[2,2,2048]{2,1,0:T(2,128)(2,1)} %refs_2_.7, ...), custom_call_target="tpu_custom_call" | custom-call | tf_op jit(solution)/shard_map/attn_0/pallas_call | solution.py:413
  11.0 0.0 copy-done
  11.0 0.0 copy-done.1
  11.0 0.0 copy-done.2
  11.1 0.0 copy-done.3
  11.1 0.0 copy-done.4
  11.1 0.0 copy-done.5
  11.1 0.0 copy-done.6
  11.1 29.9 %reduce_0.1 = (f32[64,768]{1,0:T(8,128)S(1)}, bf16[8,2048]{1,0:T(8,128)(2,1)S(1)}, bf16[2,64,512,128]{3,2,1,0:T(8,128)(2,1)S(1)}, bf16[2,64,512,128]{3,2,1,0:T(8,128)(2,1)S(1)}) custom-call(f32[64,2048]{1,0:T(8,128)S(1)} %get-tuple-element.15.refs_0_, bf16[64,2048]{1,0:T(8,128)(2,1)S(1)} %bitcast.7, ...), custom_call_target="tpu_custom_call", output_to_operand_aliasing={{2}: (13, {}), {3}: (14, {})} | custom-call | tf_op jit(solution)/shard_map/reduce_0/pallas_call | solution.py:435
  41.0 8.5 %attn_1.1 = (f32[64,2048]{1,0:T(8,128)S(1)}, bf16[2,64,512,128]{3,2,1,0:T(8,128)(2,1)}, bf16[2,64,512,128]{3,2,1,0:T(8,128)(2,1)}, bf16[2,64,512,128]{3,2,1,0:T(8,128)(2,1)S(1)}, bf16[2,64,512,128]{3,2,1,0:T(8,128)(2,1)S(1)}) custom-call(f32[64,768]{1,0:T(8,128)S(1)} %get-tuple-element.18.refs, ...), custom_call_target="tpu_custom_call", output_to_operand_aliasing={{1}: (5, {}), {2}: (6, {}), {3}: (7, {}), {4}: (8, {})} | custom-call | tf_op jit(solution)/shard_map/attn_1/pallas_call | solution.py:413
  49.5 26.3 %reduce_1.1 = bf16[64,2048]{1,0:T(8,128)(2,1)S(1)} custom-call(f32[64,2048]{1,0:T(8,128)S(1)} %get-tuple-element.23.refs_0_, bf16[8,2048]{1,0:T(8,128)(2,1)S(1)} %get-tuple-element.24.refs_1_, bf16[2,2,2048]{2,1,0:T(2,128)(2,1)S(1)} %copy-done.1, bf16[2,2,2048]{2,1,0:T(2,128)(2,1)S(1)} %copy-done.2, bf16[2,2048]{1,0:T(2,128)(2,1)S(1)} %copy-done.3, ...), custom_call_target="tpu_custom_call" | custom-call | tf_op jit(solution)/shard_map/reduce_1/pallas_call | solution.py:435
  75.8 0.7 copy.32
Async XLA Ops:
  0.6 10.4 %copy-start = (bf16[64,1,2048]{2,0,1:T(8,128)(2,1)S(1)}, bf16[64,1,2048]{2,0,1:T(8,128)(2,1)}, u32[]{:S(2)}) copy-start(bf16[64,1,2048]{2,0,1:T(8,128)(2,1)} %param.16) | copy-start | bytes 786436
  0.6 10.4 %copy-start.1 = (bf16[2,2,2048]{2,1,0:T(2,128)(2,1)S(1)}, bf16[2,2,2048]{2,1,0:T(2,128)(2,1)}, u32[]{:S(2)}) copy-start(bf16[2,2,2048]{2,1,0:T(2,128)(2,1)} %refs_2_.7) | copy-start | bytes 49156
  0.7 10.4 %copy-start.2 = (bf16[2,2,2048]{2,1,0:T(2,128)(2,1)S(1)}, bf16[2,2,2048]{2,1,0:T(2,128)(2,1)}, u32[]{:S(2)}) copy-start(bf16[2,2,2048]{2,1,0:T(2,128)(2,1)} %refs_3_.7) | copy-start | bytes 49156
  0.7 10.4 %copy-start.3 = (bf16[2,2048]{1,0:T(2,128)(2,1)S(1)}, bf16[2,2048]{1,0:T(2,128)(2,1)}, u32[]{:S(2)}) copy-start(bf16[2,2048]{1,0:T(2,128)(2,1)} %refs_4_.7) | copy-start | bytes 24580
  0.7 10.4 %copy-start.4 = (bf16[2,2048]{1,0:T(2,128)(2,1)S(1)}, bf16[2,2048]{1,0:T(2,128)(2,1)}, u32[]{:S(2)}) copy-start(bf16[2,2048]{1,0:T(2,128)(2,1)} %refs_8_.5) | copy-start | bytes 24580
  0.7 10.4 %copy-start.5 = (bf16[2,1024]{1,0:T(2,128)(2,1)S(1)}, bf16[2,1024]{1,0:T(2,128)(2,1)}, u32[]{:S(2)}) copy-start(bf16[2,1024]{1,0:T(2,128)(2,1)} %refs_6_.5) | copy-start | bytes 12292
  0.7 10.4 %copy-start.6 = (bf16[2,768]{1,0:T(2,128)(2,1)S(1)}, bf16[2,768]{1,0:T(2,128)(2,1)}, u32[]{:S(2)}) copy-start(bf16[2,768]{1,0:T(2,128)(2,1)} %refs_12_.1) | copy-start | bytes 9220

commit v12 on v10

--- a/solution.py
+++ b/solution.py
@@ -298,9 +298,11 @@
         for k in range(parts):
             ref = buf.at[1 - c, x, :, pl.ds(k * part, part)]
             hops.append({d: remote(ref, ref, ag_s.at[phase + k, d], ag_r.at[phase + k, d], chip(d) * 2 + 1 - c) for d in far})
-            for d in far:
+            hops[k][far[0]].start()
+            passed.append([pass_on(k, 0)])
+        for k in range(parts):
+            for d in far[1:]:
                 hops[k][d].start()
-            passed.append([pass_on(k, 0)])
             passed[k][0].start()
         for k in range(parts):
             for d in by_distance[1:]:
@@ -339,7 +341,7 @@
     def down(lo, size):
         part2[:, lo:lo + size] = jnp.dot(act, wd[:, lo:lo + size], preferred_element_type=F32)
 
-    total = reduce_scatter(1, part2, [down, down])
+    total = reduce_scatter(1, part2, [down])
     x_next = (x_mid + total + bd_ref[layer:layer + 1].astype(F32)).astype(BF16)
     if last:
         out_ref[...] = all_gather(2, gath2, x_next, 1, lambda lo, size, rows: rows)

time: 76.5 us -> 77.2 us (level)
  no operation moved by 1% of the time
where the time goes in v12:
time: 77.2 us; the launch traced here: 77 us
  Pallas kernels  75.5 us (98%)
    pallas_call x2, Pallas kernels, reduce(): pl.pallas_call(functools.partial(reduce_kernel, layer, tp_size, last), ou...  56.7 us
    pallas_call x2, Pallas kernels, attn(): pl.pallas_call(functools.partial(attn_kernel, layer, n_local * tp_size, f...  18.8 us

profile of v12, /device:TPU:113, one launch (start us, length us, event | category | flops | bytes accessed | tf_op | source)
XLA Modules:
  0.0 77.0 jit_solution(7154807513984481181)
XLA Ops:
  0.6 0.0 copy-start
  0.6 0.0 copy-start.1
  0.7 0.0 copy-start.2
  0.7 0.0 copy-start.3
  0.7 0.0 copy-start.4
  0.7 0.0 copy-start.5
  0.7 0.0 copy-start.6
  0.7 10.3 %attn_0.1 = (f32[64,2048]{1,0:T(8,128)S(1)}, bf16[2,64,512,128]{3,2,1,0:T(8,128)(2,1)}, bf16[2,64,512,128]{3,2,1,0:T(8,128)(2,1)}, bf16[2,64,512,128]{3,2,1,0:T(8,128)(2,1)S(1)}, bf16[2,64,512,128]{3,2,1,0:T(8,128)(2,1)S(1)}) custom-call(bf16[64,2048]{1,0:T(8,128)(2,1)} %bitcast.6, bf16[2,2,2048]{2,1,0:T(2,128)(2,1)} %refs_2_.7, ...), custom_call_target="tpu_custom_call" | custom-call | tf_op jit(solution)/shard_map/attn_0/pallas_call | solution.py:415
  11.0 0.0 copy-done
  11.0 0.0 copy-done.1
  11.0 0.0 copy-done.2
  11.1 0.0 copy-done.3
  11.1 0.0 copy-done.4
  11.1 0.0 copy-done.5
  11.1 0.0 copy-done.6
  11.1 30.1 %reduce_0.1 = (f32[64,768]{1,0:T(8,128)S(1)}, bf16[8,2048]{1,0:T(8,128)(2,1)S(1)}, bf16[2,64,512,128]{3,2,1,0:T(8,128)(2,1)S(1)}, bf16[2,64,512,128]{3,2,1,0:T(8,128)(2,1)S(1)}) custom-call(f32[64,2048]{1,0:T(8,128)S(1)} %get-tuple-element.15.refs_0_, bf16[64,2048]{1,0:T(8,128)(2,1)S(1)} %bitcast.7, ...), custom_call_target="tpu_custom_call", output_to_operand_aliasing={{2}: (13, {}), {3}: (14, {})} | custom-call | tf_op jit(solution)/shard_map/reduce_0/pallas_call | solution.py:437
  41.2 8.5 %attn_1.1 = (f32[64,2048]{1,0:T(8,128)S(1)}, bf16[2,64,512,128]{3,2,1,0:T(8,128)(2,1)}, bf16[2,64,512,128]{3,2,1,0:T(8,128)(2,1)}, bf16[2,64,512,128]{3,2,1,0:T(8,128)(2,1)S(1)}, bf16[2,64,512,128]{3,2,1,0:T(8,128)(2,1)S(1)}) custom-call(f32[64,768]{1,0:T(8,128)S(1)} %get-tuple-element.18.refs, ...), custom_call_target="tpu_custom_call", output_to_operand_aliasing={{1}: (5, {}), {2}: (6, {}), {3}: (7, {}), {4}: (8, {})} | custom-call | tf_op jit(solution)/shard_map/attn_1/pallas_call | solution.py:415
  49.7 26.6 %reduce_1.1 = bf16[64,2048]{1,0:T(8,128)(2,1)S(1)} custom-call(f32[64,2048]{1,0:T(8,128)S(1)} %get-tuple-element.23.refs_0_, bf16[8,2048]{1,0:T(8,128)(2,1)S(1)} %get-tuple-element.24.refs_1_, bf16[2,2,2048]{2,1,0:T(2,128)(2,1)S(1)} %copy-done.1, bf16[2,2,2048]{2,1,0:T(2,128)(2,1)S(1)} %copy-done.2, bf16[2,2048]{1,0:T(2,128)(2,1)S(1)} %copy-done.3, ...), custom_call_target="tpu_custom_call" | custom-call | tf_op jit(solution)/shard_map/reduce_1/pallas_call | solution.py:437
  76.3 0.7 copy.32
Async XLA Ops:
  0.6 10.4 %copy-start = (bf16[64,1,2048]{2,0,1:T(8,128)(2,1)S(1)}, bf16[64,1,2048]{2,0,1:T(8,128)(2,1)}, u32[]{:S(2)}) copy-start(bf16[64,1,2048]{2,0,1:T(8,128)(2,1)} %param.16) | copy-start | bytes 786436
  0.6 10.4 %copy-start.1 = (bf16[2,2,2048]{2,1,0:T(2,128)(2,1)S(1)}, bf16[2,2,2048]{2,1,0:T(2,128)(2,1)}, u32[]{:S(2)}) copy-start(bf16[2,2,2048]{2,1,0:T(2,128)(2,1)} %refs_2_.7) | copy-start | bytes 49156
  0.7 10.4 %copy-start.2 = (bf16[2,2,2048]{2,1,0:T(2,128)(2,1)S(1)}, bf16[2,2,2048]{2,1,0:T(2,128)(2,1)}, u32[]{:S(2)}) copy-start(bf16[2,2,2048]{2,1,0:T(2,128)(2,1)} %refs_3_.7) | copy-start | bytes 49156
  0.7 10.4 %copy-start.3 = (bf16[2,2048]{1,0:T(2,128)(2,1)S(1)}, bf16[2,2048]{1,0:T(2,128)(2,1)}, u32[]{:S(2)}) copy-start(bf16[2,2048]{1,0:T(2,128)(2,1)} %refs_4_.7) | copy-start | bytes 24580
  0.7 10.4 %copy-start.4 = (bf16[2,2048]{1,0:T(2,128)(2,1)S(1)}, bf16[2,2048]{1,0:T(2,128)(2,1)}, u32[]{:S(2)}) copy-start(bf16[2,2048]{1,0:T(2,128)(2,1)} %refs_8_.5) | copy-start | bytes 24580
  0.7 10.4 %copy-start.5 = (bf16[2,1024]{1,0:T(2,128)(2,1)S(1)}, bf16[2,1024]{1,0:T(2,128)(2,1)}, u32[]{:S(2)}) copy-start(bf16[2,1024]{1,0:T(2,128)(2,1)} %refs_6_.5) | copy-start | bytes 12292
  0.7 10.4 %copy-start.6 = (bf16[2,768]{1,0:T(2,128)(2,1)S(1)}, bf16[2,768]{1,0:T(2,128)(2,1)}, u32[]{:S(2)}) copy-start(bf16[2,768]{1,0:T(2,128)(2,1)} %refs_12_.1) | copy-start | bytes 9220

commit v13 on v9

--- a/solution.py
+++ b/solution.py
@@ -242,7 +242,7 @@
     pl.semaphore_wait(barrier, len(peers))
 
     sent = []
-    order = [2, 1, 3, 0] if n_chip == 4 else list(range(1, n_chip)) + [0]
+    order = [1, 3, 2, 0] if n_chip == 4 else list(range(1, n_chip)) + [0]
 
     def rows_of(core, d):
         return pl.ds(pl.multiple_of((core * n_chip + chip(d)) * blk, blk), blk)

time: 75.6 us -> 77.7 us (1.028)
  Pallas kernels: 73.9 us -> 76 us
    pallas_call x2, Pallas kernels: 55.1 us -> 57.2 us  [reduce(): pl.pallas_call(functools.partial(reduce_kernel, layer, tp_size, last), ou...]
where the time goes in v13:
time: 77.7 us; the launch traced here: 77.6 us
  Pallas kernels  76 us (98%)
    pallas_call x2, Pallas kernels, reduce(): pl.pallas_call(functools.partial(reduce_kernel, layer, tp_size, last), ou...  57.2 us
    pallas_call x2, Pallas kernels, attn(): pl.pallas_call(functools.partial(attn_kernel, layer, n_local * tp_size, f...  18.8 us

profile of v13, /device:TPU:113, one launch (start us, length us, event | category | flops | bytes accessed | tf_op | source)
XLA Modules:
  0.0 77.6 jit_solution(13051183291845797363)
XLA Ops:
  0.6 0.0 copy-start
  0.6 0.0 copy-start.1
  0.7 0.0 copy-start.2
  0.7 0.0 copy-start.3
  0.7 0.0 copy-start.4
  0.7 0.0 copy-start.5
  0.7 0.0 copy-start.6
  0.7 10.3 %attn_0.1 = (f32[64,2048]{1,0:T(8,128)S(1)}, bf16[2,64,512,128]{3,2,1,0:T(8,128)(2,1)}, bf16[2,64,512,128]{3,2,1,0:T(8,128)(2,1)}, bf16[2,64,512,128]{3,2,1,0:T(8,128)(2,1)S(1)}, bf16[2,64,512,128]{3,2,1,0:T(8,128)(2,1)S(1)}) custom-call(bf16[64,2048]{1,0:T(8,128)(2,1)} %bitcast.6, bf16[2,2,2048]{2,1,0:T(2,128)(2,1)} %refs_2_.7, ...), custom_call_target="tpu_custom_call" | custom-call | tf_op jit(solution)/shard_map/attn_0/pallas_call | solution.py:387
  11.0 0.0 copy-done
  11.0 0.0 copy-done.1
  11.0 0.0 copy-done.2
  11.1 0.0 copy-done.3
  11.1 0.0 copy-done.4
  11.1 0.0 copy-done.5
  11.1 0.0 copy-done.6
  11.1 30.5 %reduce_0.1 = (f32[64,768]{1,0:T(8,128)S(1)}, bf16[8,2048]{1,0:T(8,128)(2,1)S(1)}, bf16[2,64,512,128]{3,2,1,0:T(8,128)(2,1)S(1)}, bf16[2,64,512,128]{3,2,1,0:T(8,128)(2,1)S(1)}) custom-call(f32[64,2048]{1,0:T(8,128)S(1)} %get-tuple-element.15.refs_0_, bf16[64,2048]{1,0:T(8,128)(2,1)S(1)} %bitcast.7, ...), custom_call_target="tpu_custom_call", output_to_operand_aliasing={{2}: (13, {}), {3}: (14, {})} | custom-call | tf_op jit(solution)/shard_map/reduce_0/pallas_call | solution.py:409
  41.6 8.5 %attn_1.1 = (f32[64,2048]{1,0:T(8,128)S(1)}, bf16[2,64,512,128]{3,2,1,0:T(8,128)(2,1)}, bf16[2,64,512,128]{3,2,1,0:T(8,128)(2,1)}, bf16[2,64,512,128]{3,2,1,0:T(8,128)(2,1)S(1)}, bf16[2,64,512,128]{3,2,1,0:T(8,128)(2,1)S(1)}) custom-call(f32[64,768]{1,0:T(8,128)S(1)} %get-tuple-element.18.refs, ...), custom_call_target="tpu_custom_call", output_to_operand_aliasing={{1}: (5, {}), {2}: (6, {}), {3}: (7, {}), {4}: (8, {})} | custom-call | tf_op jit(solution)/shard_map/attn_1/pallas_call | solution.py:387
  50.1 26.7 %reduce_1.1 = bf16[64,2048]{1,0:T(8,128)(2,1)S(1)} custom-call(f32[64,2048]{1,0:T(8,128)S(1)} %get-tuple-element.23.refs_0_, bf16[8,2048]{1,0:T(8,128)(2,1)S(1)} %get-tuple-element.24.refs_1_, bf16[2,2,2048]{2,1,0:T(2,128)(2,1)S(1)} %copy-done.1, bf16[2,2,2048]{2,1,0:T(2,128)(2,1)S(1)} %copy-done.2, bf16[2,2048]{1,0:T(2,128)(2,1)S(1)} %copy-done.3, ...), custom_call_target="tpu_custom_call" | custom-call | tf_op jit(solution)/shard_map/reduce_1/pallas_call | solution.py:409
  76.8 0.7 copy.32
Async XLA Ops:
  0.6 10.4 %copy-start = (bf16[64,1,2048]{2,0,1:T(8,128)(2,1)S(1)}, bf16[64,1,2048]{2,0,1:T(8,128)(2,1)}, u32[]{:S(2)}) copy-start(bf16[64,1,2048]{2,0,1:T(8,128)(2,1)} %param.16) | copy-start | bytes 786436
  0.6 10.4 %copy-start.1 = (bf16[2,2,2048]{2,1,0:T(2,128)(2,1)S(1)}, bf16[2,2,2048]{2,1,0:T(2,128)(2,1)}, u32[]{:S(2)}) copy-start(bf16[2,2,2048]{2,1,0:T(2,128)(2,1)} %refs_2_.7) | copy-start | bytes 49156
  0.7 10.4 %copy-start.2 = (bf16[2,2,2048]{2,1,0:T(2,128)(2,1)S(1)}, bf16[2,2,2048]{2,1,0:T(2,128)(2,1)}, u32[]{:S(2)}) copy-start(bf16[2,2,2048]{2,1,0:T(2,128)(2,1)} %refs_3_.7) | copy-start | bytes 49156
  0.7 10.4 %copy-start.3 = (bf16[2,2048]{1,0:T(2,128)(2,1)S(1)}, bf16[2,2048]{1,0:T(2,128)(2,1)}, u32[]{:S(2)}) copy-start(bf16[2,2048]{1,0:T(2,128)(2,1)} %refs_4_.7) | copy-start | bytes 24580
  0.7 10.4 %copy-start.4 = (bf16[2,2048]{1,0:T(2,128)(2,1)S(1)}, bf16[2,2048]{1,0:T(2,128)(2,1)}, u32[]{:S(2)}) copy-start(bf16[2,2048]{1,0:T(2,128)(2,1)} %refs_8_.5) | copy-start | bytes 24580
  0.7 10.4 %copy-start.5 = (bf16[2,1024]{1,0:T(2,128)(2,1)S(1)}, bf16[2,1024]{1,0:T(2,128)(2,1)}, u32[]{:S(2)}) copy-start(bf16[2,1024]{1,0:T(2,128)(2,1)} %refs_6_.5) | copy-start | bytes 12292
  0.7 10.4 %copy-start.6 = (bf16[2,768]{1,0:T(2,128)(2,1)S(1)}, bf16[2,768]{1,0:T(2,128)(2,1)}, u32[]{:S(2)}) copy-start(bf16[2,768]{1,0:T(2,128)(2,1)} %refs_12_.1) | copy-start | bytes 9220
